TPU v7x, 32 devices: a whole 2x2x4 slice. The times are simulated.
32 devices in a mesh: dp: 32 (over z, y, x, core).
Axes of the slice: x: 2, y: 2, z: 4, core: 2. Of those that a mesh axis runs over, the one named last changes fastest.
Arguments:
- token_ids: int32 [32768], P('dp'), may hold values from 0 to 31999, as said below
- tokens: bfloat16 [32768, 4096], P('dp'), may hold values from -64 to 64
- frozen_weight: bfloat16 [4096, 1024], replicated, may hold values from -0.09375 to 0.09375
- adapter_down: bfloat16 [4096, 128], replicated, may hold values from -0.09375 to 0.09375
- adapter_up: bfloat16 [128, 1024], replicated, may hold values from -1.5 to 1.5
- gate_weight: bfloat16 [4096, 8], replicated, may hold values from -1 to 1
- upstream: bfloat16 [32768, 1024], P('dp'), may hold values from -6 to 6
Outputs:
- projected: bfloat16 [32768, 1024], P('dp')
- input_grad: bfloat16 [32768, 4096], P('dp')
- clipped_down: float32 [4096, 128], replicated
- clipped_up: float32 [128, 1024], replicated
- clipped_gate: float32 [4096, 8], replicated
- load: float32 [8], replicated
- entropy: float32 [], replicated
Inputs may be any that keep to these rules, and one draw needn't show every extreme that they name: `token_ids`: within each device's block of 1024 tokens the live tokens (id not 0) come first, 256 or more of them, and padding (id 0) fills the rest; the last block is wholly live.
All inputs are finite; a program needn't handle non-finite values.
Results may differ from a plain program's by a relative error of at most 0.0095.
Values sent between devices are 32-bit elements; how exact they have to be, the bound alone decides.
No kernel may reach another device: no remote copies, remote signals or barrier semaphores. Data moves between devices by JAX's collectives and lax.ppermute only.
A program may use at most 192 MiB of HBM per device.

v0:
```python
import math

import jax
import jax.numpy as jnp
from jax import lax
from jax.sharding import PartitionSpec as P


def left_dot(first, second):
    return lax.dot_general(
        first, second, (((0,), (0,)), ((), ())), preferred_element_type=jnp.float32
    )


def right_dot(first, second):
    return lax.dot_general(
        first, second, (((1,), (1,)), ((), ())), preferred_element_type=jnp.float32
    )


def exact_left(tokens, matrix):
    upper = matrix.astype(jnp.bfloat16)
    lower = (matrix - upper.astype(jnp.float32)).astype(jnp.bfloat16)
    return left_dot(tokens, upper) + left_dot(tokens, lower)


def share_stats(local):
    return lax.psum((local[0], local[1], local[2]), "dp")


def reduce_clip(terms, finish, limit):
    summed = lax.psum((terms[0], terms[1], terms[2]), "dp")
    grads = finish(summed)
    total = (
        jnp.sum(grads[0] * grads[0]) + jnp.sum(grads[1] * grads[1]) + jnp.sum(grads[2] * grads[2])
    )
    factor = jnp.minimum(1.0, limit / jnp.sqrt(total))
    return (grads[0] * factor, grads[1] * factor, grads[2] * factor)


def on_device(token_ids, tokens, frozen_weight, adapter_down, adapter_up, gate_weight, upstream):
    width = tokens.shape[1]
    experts = gate_weight.shape[1]
    ranks = adapter_down.shape[1]
    rank = ranks // experts
    outputs = frozen_weight.shape[1]
    rows = tokens.shape[0]
    live = (token_ids != 0).astype(jnp.float32)
    base = jnp.dot(tokens, frozen_weight, preferred_element_type=jnp.float32)
    logits = jnp.dot(tokens, gate_weight, preferred_element_type=jnp.float32)
    prob = jax.nn.softmax(logits, axis=1)
    logp = jax.nn.log_softmax(logits, axis=1)
    low = jnp.dot(tokens, adapter_down, preferred_element_type=jnp.float32).astype(jnp.bfloat16)
    spread = jnp.repeat(prob, rank, axis=1)
    weighted = (low.astype(jnp.float32) * spread).astype(jnp.bfloat16)
    projected = (
        base + 2.0 * jnp.dot(weighted, adapter_up, preferred_element_type=jnp.float32)
    ).astype(jnp.bfloat16)
    masked = upstream * live.astype(jnp.bfloat16)[:, None]
    grad_up = 2.0 * left_dot(weighted, masked)
    back = right_dot(masked, adapter_up)
    gate_task = 2.0 * jnp.sum((low.astype(jnp.float32) * back).reshape(rows, experts, rank), axis=2)
    low_grad = (2.0 * spread * back).astype(jnp.bfloat16)
    grad_down = left_dot(tokens, low_grad)
    ent_tok = -jnp.sum(prob * logp, axis=1)
    local_stats = (jnp.sum(live[:, None] * prob, axis=0), jnp.sum(live * ent_tok), jnp.sum(live))

    def jac(vector):
        return prob * (vector - jnp.sum(prob * vector, axis=1, keepdims=True))

    plain_z = jac(gate_task) + 50.0 * live[:, None] * prob * (logp + ent_tok[:, None])
    frozen_back = right_dot(masked, frozen_weight) + right_dot(low_grad, adapter_down)
    count = width * ranks + ranks * outputs + width * experts
    limit = math.sqrt(count)
    load_all, ent_all, live_all = share_stats(local_stats)
    gate_z = plain_z + 2.0 * experts * 100.0 / live_all * live[:, None] * jac(load_all[None, :])
    terms = (grad_down, grad_up, exact_left(tokens, gate_z))

    def finish(summed):
        return summed

    clipped = reduce_clip(terms, finish, limit)
    input_grad = frozen_back + jnp.dot(
        gate_z, gate_weight.astype(jnp.float32).T, precision=lax.Precision.HIGHEST
    )
    return (
        projected,
        input_grad.astype(jnp.bfloat16),
        clipped[0],
        clipped[1],
        clipped[2],
        load_all / live_all,
        ent_all / live_all,
    )


def solution(mesh):
    placed = (P("dp"), P("dp", None), P(), P(), P(), P(), P("dp", None))
    return jax.shard_map(
        on_device,
        mesh=mesh,
        in_specs=placed,
        out_specs=(P("dp", None), P("dp", None), P(), P(), P(), P(), P()),
        check_vma=False,
    )
```

profile of v0, /device:TPU:0, one launch (start us, length us, event | category | flops | bytes accessed | tf_op | source)
XLA Modules:
  0.0 237.1 jit_solution(10412498830634973112)
XLA Ops:
  7.2 0.0 copy-start
  7.2 0.0 all-reduce.4.cloned.1.call-start
  7.2 5.8 %fusion.21 = (f32[1024]{0:T(1024)S(1)}, f32[1024,8]{0,1:T(8,128)S(1)}) fusion(bf16[1024,4096]{1,0:T(8,128)(2,1)} %param.8, bf16[4096,8]{0,1:T(8,128)(2,1)} %param.12), kind=kOutput, calls=%fused_computation.48 | convolution fusion | flops 67116032 | bytes 8491008 | tf_op jit(solution)/shard_map/dot_general | solution.py:50
  13.2 0.1 copy-done.1
  13.3 2.9 %fusion.10 = f32[1024,128]{0,1:T(8,128)S(1)} fusion(bf16[1024,4096]{1,0:T(8,128)(2,1)S(1)} %copy-done.1, bf16[4096,128]{1,0:T(8,128)(2,1)S(1)} %copy-done), kind=kOutput, calls=%fused_computation.14 | convolution fusion | flops 1074003968 | bytes 9961472 | tf_op jit(solution)/shard_map/dot_general | solution.py:53
  16.3 1.5 fusion.16
  17.8 0.1 bitcast_reduce_fusion
  17.9 0.1 multiply_reduce_fusion.6
  18.0 0.6 select_reduce_fusion
  18.6 42.4 %all-reduce = (f32[8]{0:T(128)S(1)}, f32[]{:T(128)}, f32[]{:T(128)}) all-reduce(f32[8]{0:T(128)S(1)} %get-tuple-element.16, f32[]{:T(128)} %get-tuple-element.18, f32[]{:T(128)} %get-tuple-element.17), channel_id=1, replica_groups=mesh['dp'=32] {'dp'}, use_global_device_ids=true, to_apply=%region_8.9 | all-reduce | flops 10 | bytes 80 | tf_op jit(solution)/shard_map/psum | solution.py:28
  61.0 0.1 multiply_reduce_fusion.3
  61.8 6.0 %convolution_bitcast_fusion = f32[4096,128]{0,1:T(8,128)} fusion(bf16[1024,128]{0,1:T(8,128)(2,1)S(1)} %get-tuple-element.27, bf16[1024,4096]{1,0:T(8,128)(2,1)} %param.8), kind=kOutput, calls=%fused_computation.1 | convolution fusion | flops 1073741824 | bytes 10747904 | tf_op jit(solution)/shard_map/dot_general | solution.py:10
  67.8 1.3 fusion.7
  69.2 0.1 multiply_add_fusion
  69.2 4.7 %fusion.18 = f32[8,4096]{1,0:T(8,128)S(1)} fusion(bf16[1024,4096]{1,0:T(8,128)(2,1)} %param.8, f32[1024,8]{0,1:T(8,128)S(1)} %multiply_add_fusion), kind=kOutput, calls=%fused_computation.38 | convolution fusion | flops 67117056 | bytes 8552448 | tf_op jit(solution)/shard_map/dot_general | solution.py:10
  74.0 0.1 slice-done.1
  74.1 1.9 fusion
  76.0 0.0 all-reduce.4.cloned.1.call-update
  76.0 10.2 %fusion.23 = f32[1024,4096]{1,0:T(8,128)} fusion(f32[1024,8]{0,1:T(8,128)S(1)} %multiply_add_fusion, bf16[4096,8]{0,1:T(8,128)(2,1)S(1)} %copy-done.7), kind=kOutput, calls=%fused_computation.50 | convolution fusion | flops 402653184 | bytes 16875520 | tf_op jit(solution)/shard_map/dot_general | solution.py:83
  86.2 12.7 %fusion.22 = f32[1024,1024]{1,0:T(8,128)S(1)} fusion(bf16[1024,4096]{1,0:T(8,128)(2,1)} %param.8, bf16[4096,1024]{1,0:T(8,128)(2,1)} %param.9), kind=kOutput, calls=%fused_computation.49 | convolution fusion | flops 8589934592 | bytes 20971520 | tf_op jit(solution)/shard_map/dot_general | solution.py:49
  98.9 14.8 %fusion.5 = f32[1024,4096]{1,0:T(8,128)} fusion(bf16[4096,1024]{1,0:T(8,128)(2,1)} %param.9, bf16[1024,1024]{1,0:T(8,128)(2,1)S(1)} %copy-done.2, bf16[1024]{0:T(1024)(128)(2,1)S(1)} %get-tuple-element.32), kind=kOutput, calls=%fused_computation.10 | convolution fusion | flops 8590983168 | bytes 27265024 | tf_op jit(solution)/shard_map/dot_general | solution.py:16
  113.7 1.2 broadcast_divide_fusion
  114.8 2.1 add_convert_fusion.1
  118.2 15.5 %add_convert_fusion = bf16[1024,4096]{1,0:T(8,128)(2,1)} fusion(f32[1024,4096]{1,0:T(8,128)} %fusion.23, f32[1024,4096]{1,0:T(8,128)} %fusion.5, bf16[1024,128]{0,1:T(8,128)(2,1)S(1)} %get-tuple-element.27, bf16[4096,128]{1,0:T(8,128)(2,1)S(1)} %copy-done), kind=kOutput, calls=%fused_computation | convolution fusion | flops 1086324736 | bytes 43253760 | tf_op jit(solution)/shard_map/dot_general | solution.py:16
  133.7 80.3 %all-reduce.4.cloned.1.call-done = (f32[4096,128]{0,1:T(8,128)}, f32[128,1024]{1,0:T(8,128)}, f32[4096,8]{0,1:T(8,128)}) async-done(((f32[4096,128]{0,1:T(8,128)}, f32[128,1024]{1,0:T(8,128)}, f32[4096,8]{0,1:T(8,128)}), (f32[4096,128]{0,1:T(8,128)}, f32[128,1024]{1,0:T(8,128)}, f32[4096,8]{0,1:T(8,128)})) %all-reduce.4.cloned.1.call-update) | async-done | bytes 2752528 | tf_op jit(solution)/shard_map/psum | solution.py:32
  214.0 2.7 %multiply_reduce_fusion = f32[]{:T(128)} fusion(f32[4096,128]{0,1:T(8,128)} %get-tuple-element.22), kind=kLoop, calls=%fused_computation.5 | loop fusion | flops 1048575 | bytes 2097156 | tf_op jit(solution)/shard_map/reduce_sum | solution.py:35
  216.7 1.8 multiply_reduce_fusion.1
  218.5 1.5 multiply_reduce_fusion.2
  222.1 1.8 broadcast_multiply_fusion
  223.8 1.9 broadcast_multiply_fusion.1
  225.7 1.6 broadcast_multiply_fusion.2
  227.3 1.8 copy.14
  (26 shorter events, 0.1 us)
Async XLA Ops:
  7.2 6.0 %copy-start = (bf16[4096,128]{1,0:T(8,128)(2,1)S(1)}, bf16[4096,128]{1,0:T(8,128)(2,1)}, u32[]{:S(2)}) copy-start(bf16[4096,128]{1,0:T(8,128)(2,1)} %param.10) | copy-start | bytes 3145732
  7.2 206.8 %all-reduce.4.cloned.1.call-start = ((), (), s32[]{:S(2)}) async-start(), calls=%async_computation | async-start | bytes 5505024 | tf_op jit(solution)/shard_map/psum | solution.py:32
  7.2 6.1 %copy-start.1 = (bf16[1024,4096]{1,0:T(8,128)(2,1)S(1)}, bf16[1024,4096]{1,0:T(8,128)(2,1)}, u32[]{:S(2)}) copy-start(bf16[1024,4096]{1,0:T(8,128)(2,1)} %param.8) | copy-start | bytes 25165828
  13.1 3.2 %copy-start.8 = (s32[1024]{0:T(1024)S(1)}, s32[1024]{0:T(1024)}, u32[]{:S(2)}) copy-start(s32[1024]{0:T(1024)} %param.7) | copy-start | bytes 12292
  13.1 3.2 %copy-start.2 = (bf16[1024,1024]{1,0:T(8,128)(2,1)S(1)}, bf16[1024,1024]{1,0:T(8,128)(2,1)}, u32[]{:S(2)}) copy-start(bf16[1024,1024]{1,0:T(8,128)(2,1)} %param.13) | copy-start | bytes 6291460
  13.1 3.2 %copy-start.3 = (bf16[128,1024]{1,0:T(8,128)(2,1)S(1)}, bf16[128,1024]{1,0:T(8,128)(2,1)}, u32[]{:S(2)}) copy-start(bf16[128,1024]{1,0:T(8,128)(2,1)} %param.11) | copy-start | bytes 786436
  61.8 6.0 %copy-start.5 = (bf16[1024,128]{0,1:T(8,128)(2,1)S(1)}, bf16[1024,128]{0,1:T(8,128)(2,1)}, u32[]{:S(2)}) copy-start(bf16[1024,128]{0,1:T(8,128)(2,1)} %get-tuple-element.29) | copy-start | bytes 786436
  67.8 6.1 %slice-start = ((s8[8388608]{0:T(1024)(128)(4,1)}), s8[4194304]{0:T(1024)(128)(4,1)S(1)}, s32[]{:S(2)}) async-start(s8[8388608]{0:T(1024)(128)(4,1)} %bitcast.34), calls=%async_computation.1 | async-start | bytes 8388608
  69.2 4.9 %slice-start.1 = ((s8[8388608]{0:T(1024)(128)(4,1)}), s8[4194304]{0:T(1024)(128)(4,1)S(1)}, s32[]{:S(2)}) async-start(s8[8388608]{0:T(1024)(128)(4,1)} %bitcast.34), calls=%async_computation.2 | async-start | bytes 8388608
  74.1 1.9 copy-start.7
  98.9 15.9 %copy-start.4 = (bf16[128,1024]{1,0:T(8,128)(2,1)S(1)}, bf16[128,1024]{1,0:T(8,128)(2,1)}, u32[]{:S(2)}) copy-start(bf16[128,1024]{1,0:T(8,128)(2,1)} %param.11) | copy-start | bytes 786436
  98.9 15.9 %copy-start.6 = (bf16[1024,128]{0,1:T(8,128)(2,1)S(1)}, bf16[1024,128]{0,1:T(8,128)(2,1)}, u32[]{:S(2)}) copy-start(bf16[1024,128]{0,1:T(8,128)(2,1)} %get-tuple-element.29) | copy-start | bytes 786436
Sparse Core Ops, SparseCore 0:
  76.1 137.8 all-reduce.3
where the time goes:
time: 238 us; the launch traced here: 237 us
  waiting for transfers between devices  80.3 us (34%)
  matrix products  79.3 us (33%)
  blocking collectives  42.4 us (18%)
  between operations  19.4 us (8%)
  other arithmetic  13.5 us (6%)
    psum x1, waiting for transfers between devices, reduce_clip(): summed = lax.psum((terms[0], terms[1], terms[2]), 'dp')  80.3 us
    psum x1, blocking collectives, share_stats(): return lax.psum((local[0], local[1], local[2]), 'dp')  42.4 us
    dot_general x3, matrix products, right_dot(): lax.dot_general(first, second, (((1,), (1,)), ((), ())), preferred_elemen...  31.8 us
    dot_general x4, matrix products, left_dot(): lax.dot_general(first, second, (((0,), (0,)), ((), ())), preferred_elemen...  13.9 us
    dot_general x1, matrix products, on_device(): base = jnp.dot(tokens, frozen_weight, preferred_element_type=jnp.float32)  12.7 us
    dot_general x1, matrix products, on_device(): jnp.dot(gate_z, gate_weight.astype(jnp.float32).T, precision=lax.Precisio...  10.2 us
    dot_general x1, matrix products, on_device(): logits = jnp.dot(tokens, gate_weight, preferred_element_type=jnp.float32)  5.81 us
    mul x3, other arithmetic, reduce_clip(): return (grads[0] * factor, grads[1] * factor, grads[2] * factor)  5.23 us
  transfers between devices with their start and end apart: 1, of which 1 were waited for; matrix products, arithmetic and copies ran while one was open for 24% of the time, Pallas kernels for 0%

commit v1 on v0

v1 whole, which is shorter than its diff:
```python
import functools
import math

import jax
import jax.numpy as jnp
from jax import lax
from jax.experimental import pallas as pl
from jax.experimental.pallas import tpu as pltpu
from jax.sharding import PartitionSpec as P

F32 = jnp.float32
BF16 = jnp.bfloat16
LANES = 128
TILES = 4
VMEM = pltpu.VMEM
SMEM = pltpu.SMEM
HIGH = 60 * 1024 * 1024


def nn(a, b):
    return lax.dot_general(a, b, (((1,), (0,)), ((), ())), preferred_element_type=F32)


def nt(a, b):
    return lax.dot_general(a, b, (((1,), (1,)), ((), ())), preferred_element_type=F32)


def split(x):
    upper = x.astype(BF16).astype(F32)
    return upper, x - upper


def count_live(ids_ref):
    return jnp.sum((ids_ref[...] != 0).astype(jnp.int32))


def place(word, order, depth):
    spot = 0
    for step in range(depth):
        spot = spot + (((word >> order[step]) & 1) << (depth - 1 - step))
    return spot


def spots(mine, pair, side, orders, depth):
    word = (mine ^ pair) & ((1 << depth) - 1)
    first = place(word, orders[0], depth)
    second = place(word, orders[1], depth)
    kept = jnp.where(side == 0, first, second)
    sent = jnp.where(side == 0, second, first)
    return kept, sent


def local_kernel(
    orders_a, orders_b, experts, where_ref, ids_ref, gate_ref, down_ref, up_ref, tok_hbm, ups_hbm,
    keep_a, send_a, keep_b, send_b, weighted_ref, lowgrad_ref, plain_ref, share_ref, wide_ref,
    tok, ups, left, left_t, weighted_t, grad_up, stats, tok_sem, ups_sem,
):
    rows, width = tok.shape
    ranks = down_ref.shape[1]
    rank = ranks // experts
    tile = rows // TILES
    for t in range(TILES):
        part = pl.ds(t * tile, tile)
        pltpu.make_async_copy(tok_hbm.at[part], tok.at[part], tok_sem.at[t]).start()
        pltpu.make_async_copy(ups_hbm.at[part], ups.at[part], ups_sem.at[t]).start()
    mine, side = where_ref[0], where_ref[1]
    count = count_live(ids_ref)
    row_i = lax.broadcasted_iota(jnp.int32, (experts, ranks), 0)
    col_i = lax.broadcasted_iota(jnp.int32, (experts, ranks), 1)
    repeat = (col_i // rank == row_i).astype(BF16)
    gate_t = gate_ref[...].astype(F32).T.astype(BF16)
    wide_ref[:, :ranks] = down_ref[...]
    wide_ref[:, ranks:] = nn(gate_t, repeat).astype(BF16)
    up = up_ref[...]
    r2 = lax.broadcasted_iota(jnp.int32, (2 * ranks, ranks), 0)
    c2 = lax.broadcasted_iota(jnp.int32, (2 * ranks, ranks), 1)
    group = ((r2 % ranks) // rank == c2 // rank).astype(BF16)
    r1 = lax.broadcasted_iota(jnp.int32, (ranks, ranks), 0)
    c1 = lax.broadcasted_iota(jnp.int32, (ranks, ranks), 1)
    regroup = ((r1 % rank) * experts + r1 // rank == c1).astype(BF16)
    slot = lax.broadcasted_iota(jnp.int32, (tile, ranks), 1) % rank
    load = jnp.zeros((1, ranks), F32)
    entropy = jnp.zeros((1, 1), F32)
    for t in range(TILES):
        part = pl.ds(t * tile, tile)
        pltpu.make_async_copy(tok_hbm.at[part], tok.at[part], tok_sem.at[t]).wait()
        pltpu.make_async_copy(ups_hbm.at[part], ups.at[part], ups_sem.at[t]).wait()
        live = lax.broadcasted_iota(jnp.int32, (tile, 1), 0) + t * tile < count
        alive = live.astype(F32)
        both = nn(tok[part, :], wide_ref[...])
        low = both[:, :ranks].astype(BF16).astype(F32)
        logits = both[:, ranks:]
        shifted = logits - jnp.max(logits, axis=1, keepdims=True)
        powers = jnp.exp(shifted)
        total = jnp.sum(powers, axis=1, keepdims=True) * (1.0 / rank)
        prob = powers / total
        logp = shifted - jnp.log(total)
        weighted = (low * prob).astype(BF16)
        weighted_ref[part, :] = weighted
        weighted_t[:, part] = weighted.astype(F32).T.astype(BF16)
        ent = -jnp.sum(prob * logp, axis=1, keepdims=True) * (1.0 / rank)
        masked = jnp.where(live, ups[part, :].astype(F32), 0.0).astype(BF16)
        ups[part, :] = masked
        back = nt(masked, up)
        low_grad = (2.0 * prob * back).astype(BF16)
        lowgrad_ref[part, :] = low_grad
        big, small = split(low * back)
        task = 2.0 * nn(jnp.concatenate([big, small], axis=1).astype(BF16), group)
        inner = jnp.sum(prob * task, axis=1, keepdims=True) * (1.0 / rank)
        share = alive * prob
        plain = prob * (task - inner) + 50.0 * share * (logp + ent)
        plain_ref[part, :] = plain
        share_ref[part, :] = share
        load = load + jnp.sum(share, axis=0, keepdims=True)
        entropy = entropy + jnp.sum(alive * ent, axis=0, keepdims=True)
        chosen = jnp.zeros((tile, ranks), F32)
        for step in range(experts // 2 + 1):
            value = plain if step == 0 else share * pltpu.roll(prob, ranks - rank * step, 1)
            big, small = split(value)
            chosen = jnp.where(slot == 2 * step, big, chosen)
            chosen = jnp.where(slot == 2 * step + 1, small, chosen)
        picked = nn(chosen.astype(BF16), regroup)
        left_t[:ranks, part] = low_grad.astype(F32).T.astype(BF16)
        left_t[ranks:, part] = picked.T.astype(BF16)
    grad_up[...] = 2.0 * nn(weighted_t[...], ups[...])
    stat_row = lax.broadcasted_iota(jnp.int32, (8, ranks), 0)
    stats[...] = jnp.where(
        stat_row == 0,
        load,
        jnp.where(stat_row == 1, entropy, jnp.where(stat_row == 2, count.astype(F32), 0.0)),
    )
    kinds = experts // 2 + 1
    used = ranks + 2 * kinds * experts
    pairs = width // (2 * LANES)
    depth = pairs.bit_length() - 1
    gate_rows = kinds * experts
    up_rows = ranks * up_ref.shape[1] // (2 * pairs * LANES)
    per = ranks // up_rows
    for pair in range(pairs):
        kept_a, sent_a = spots(mine, pair, side, orders_a, depth)
        kept_b, sent_b = spots(mine, pair, side, orders_b, depth)
        piece = nn(left_t[:used, :], tok[:, pl.ds(pair * 2 * LANES, 2 * LANES)])
        one, two = piece[:, :LANES], piece[:, LANES:]
        keep = jnp.where(side == 0, one, two)
        send = jnp.where(side == 0, two, one)
        keep_a[kept_a] = keep[:ranks]
        send_a[sent_a] = send[:ranks]
        for kind in range(kinds):
            at = ranks + 2 * kind * experts
            to = pl.ds(kind * experts, experts)
            keep_b[kept_b, to] = keep[at : at + experts] + keep[at + experts : at + 2 * experts]
            send_b[sent_b, to] = send[at : at + experts] + send[at + experts : at + 2 * experts]
        keep_b[kept_b, pl.ds(gate_rows, 8)] = stats[...]
        send_b[sent_b, pl.ds(gate_rows, 8)] = stats[...]
        first, second = 2 * pair, 2 * pair + 1
        one = grad_up[pl.ds((first % per) * up_rows, up_rows), pl.ds(first // per * LANES, LANES)]
        two = grad_up[pl.ds((second % per) * up_rows, up_rows), pl.ds(second // per * LANES, LANES)]
        to = pl.ds(gate_rows + 8, up_rows)
        keep_b[kept_b, to] = jnp.where(side == 0, one, two)
        send_b[sent_b, to] = jnp.where(side == 0, two, one)


def local_grads(where, ids, gate_t, down, up, tokens, upstream, orders_a, orders_b):
    rows, width = tokens.shape
    outs = upstream.shape[1]
    experts, ranks = gate_t.shape[0], down.shape[1]
    pairs = width // (2 * LANES)
    kinds = experts // 2 + 1
    rows_b = kinds * experts + 8 + ranks * outs // (2 * pairs * LANES)
    any_spec = pl.BlockSpec(memory_space=pl.ANY)
    vmem = pl.BlockSpec(memory_space=VMEM)
    return pl.pallas_call(
        functools.partial(local_kernel, orders_a, orders_b, experts),
        out_shape=[
            jax.ShapeDtypeStruct((pairs, ranks, LANES), F32),
            jax.ShapeDtypeStruct((pairs, ranks, LANES), F32),
            jax.ShapeDtypeStruct((pairs, rows_b, LANES), F32),
            jax.ShapeDtypeStruct((pairs, rows_b, LANES), F32),
            jax.ShapeDtypeStruct((rows, ranks), BF16),
            jax.ShapeDtypeStruct((rows, ranks), BF16),
            jax.ShapeDtypeStruct((rows, ranks), F32),
            jax.ShapeDtypeStruct((rows, ranks), F32),
            jax.ShapeDtypeStruct((width, 2 * ranks), BF16),
        ],
        in_specs=[pl.BlockSpec(memory_space=SMEM), vmem, vmem, vmem, vmem, any_spec, any_spec],
        out_specs=[vmem] * 9,
        scratch_shapes=[
            VMEM((rows, width), BF16),
            VMEM((rows, outs), BF16),
            VMEM((8, LANES), F32),
            VMEM((2 * ranks, rows), BF16),
            VMEM((ranks, rows), BF16),
            VMEM((ranks, outs), F32),
            VMEM((8, ranks), F32),
            pltpu.SemaphoreType.DMA((TILES,)),
            pltpu.SemaphoreType.DMA((TILES,)),
        ],
        compiler_params=pltpu.CompilerParams(vmem_limit_bytes=HIGH),
        cost_estimate=pl.CostEstimate(
            flops=2 * rows * width * 512, bytes_accessed=2 * rows * (width + outs), transcendentals=0
        ),
        name="local_grads",
    )(where, ids, gate_t, down, up, tokens, upstream)


def project_kernel(tok_ref, weighted_ref, frozen_ref, up_ref, out_ref):
    base = nn(tok_ref[...], frozen_ref[...])
    out_ref[...] = (base + 2.0 * nn(weighted_ref[...], up_ref[...])).astype(BF16)


def project(tokens, weighted, frozen, up):
    rows, width = tokens.shape
    outs, ranks = frozen.shape[1], up.shape[0]
    tile = rows // TILES
    return pl.pallas_call(
        project_kernel,
        grid=(TILES,),
        out_shape=jax.ShapeDtypeStruct((rows, outs), BF16),
        in_specs=[
            pl.BlockSpec((tile, width), lambda i: (i, 0)),
            pl.BlockSpec((tile, ranks), lambda i: (i, 0)),
            pl.BlockSpec((width, outs), lambda i: (0, 0)),
            pl.BlockSpec((ranks, outs), lambda i: (0, 0)),
        ],
        out_specs=pl.BlockSpec((tile, outs), lambda i: (i, 0)),
        compiler_params=pltpu.CompilerParams(vmem_limit_bytes=HIGH),
        cost_estimate=pl.CostEstimate(
            flops=2 * rows * outs * (width + ranks),
            bytes_accessed=2 * (rows * width + width * outs + rows * outs),
            transcendentals=0,
        ),
        name="project",
    )(tokens, weighted, frozen, up)


def owner_kernel(experts, keep_ref, recv_ref, out_ref, stats_ref):
    block = keep_ref[0] + recv_ref[0]
    kinds = experts // 2 + 1
    at = kinds * experts
    stats = block[at : at + 8]
    stats_ref[...] = stats
    rank = LANES // experts
    row = lax.broadcasted_iota(jnp.int32, (experts, LANES), 0)
    lane = lax.broadcasted_iota(jnp.int32, (experts, LANES), 1)
    weight = jnp.broadcast_to(stats[0:1], (experts, LANES))

    def column(step):
        hit = lane == (row + step) % experts * rank
        return jnp.sum(jnp.where(hit, weight, 0.0), axis=1, keepdims=True)

    mine = column(0)
    total = jnp.zeros((experts, LANES), F32)
    for step in range(1, kinds):
        both = block[step * experts : (step + 1) * experts]
        total = total + both * (mine - column(step))
        if 2 * step != experts:
            total = total + pltpu.roll(both, step, 0) * (mine - column(experts - step))
    scale = 2.0 * experts * 100.0 / stats[2:3]
    out_ref[0, :experts] = block[:experts] + scale * total
    out_ref[0, experts:] = block[at + 8 :]


def owner_rows(keep, recv, experts):
    kinds = experts // 2 + 1
    rows = keep.shape[1] - kinds * experts - 8 + experts
    return pl.pallas_call(
        functools.partial(owner_kernel, experts),
        out_shape=[
            jax.ShapeDtypeStruct((1, rows, LANES), F32),
            jax.ShapeDtypeStruct((8, LANES), F32),
        ],
        name="owner_rows",
    )(keep, recv)


def input_kernel(experts, ids_ref, ups_ref, lowgrad_ref, plain_ref, share_ref, stats_ref, frozen_ref, wide_ref, out_ref, left):
    rows, outs = ups_ref.shape
    ranks = lowgrad_ref.shape[1]
    rank = ranks // experts

    @pl.when(pl.program_id(0) == 0)
    def _():
        count = count_live(ids_ref)
        tile = rows // TILES
        weight = stats_ref[0:1, :]
        scale = 2.0 * experts * 100.0 / stats_ref[2:3, :]
        slot = lax.broadcasted_iota(jnp.int32, (tile, ranks), 1) % rank
        for t in range(TILES):
            part = pl.ds(t * tile, tile)
            live = lax.broadcasted_iota(jnp.int32, (tile, 1), 0) + t * tile < count
            left[part, :outs] = jnp.where(live, ups_ref[part, :].astype(F32), 0.0).astype(BF16)
            left[part, outs : outs + ranks] = lowgrad_ref[part, :]
            share = share_ref[part, :]
            inner = jnp.sum(share * weight, axis=1, keepdims=True) * (1.0 / rank)
            value = plain_ref[part, :] + scale * share * (weight - inner)
            big, small = split(value)
            left[part, outs + ranks :] = jnp.where(
                slot == 0, big, jnp.where(slot == 1, small, 0.0)
            ).astype(BF16)

    out_ref[...] = (
        nt(left[:, :outs], frozen_ref[...]) + nt(left[:, outs:], wide_ref[...])
    ).astype(BF16)


def input_grads(ids, upstream, low_grad, plain, share, stats, frozen, wide, experts):
    rows, outs = upstream.shape
    width, ranks = frozen.shape[0], low_grad.shape[1]
    steps = 8
    tile = width // steps
    whole = lambda i: (0, 0)
    return pl.pallas_call(
        functools.partial(input_kernel, experts),
        grid=(steps,),
        out_shape=jax.ShapeDtypeStruct((rows, width), BF16),
        in_specs=[
            pl.BlockSpec(ids.shape, whole),
            pl.BlockSpec((rows, outs), whole),
            pl.BlockSpec((rows, ranks), whole),
            pl.BlockSpec((rows, ranks), whole),
            pl.BlockSpec((rows, ranks), whole),
            pl.BlockSpec(stats.shape, whole),
            pl.BlockSpec((tile, outs), lambda i: (i, 0)),
            pl.BlockSpec((tile, 2 * ranks), lambda i: (i, 0)),
        ],
        out_specs=pl.BlockSpec((rows, tile), lambda i: (0, i)),
        scratch_shapes=[VMEM((rows, outs + 2 * ranks), BF16)],
        compiler_params=pltpu.CompilerParams(vmem_limit_bytes=HIGH),
        cost_estimate=pl.CostEstimate(
            flops=2 * rows * width * (outs + 2 * ranks),
            bytes_accessed=2 * (rows * width + width * outs + rows * outs),
            transcendentals=0,
        ),
        name="input_grads",
    )(ids, upstream, low_grad, plain, share, stats, frozen, wide)


def clip_kernel(orders_a, orders_b, experts, limit, where_ref, own_a, other_a, own_b, other_b, stat_own, stat_other, down_ref, up_ref, gate_ref, load_ref):
    mine, side = where_ref[0], where_ref[1]
    pairs, ranks = own_a.shape[0], own_a.shape[1]
    depth = pairs.bit_length() - 1
    up_rows = own_b.shape[1] - experts
    per = ranks // up_rows

    def fold(block):
        square = block * block
        return jnp.sum(square.reshape(block.shape[0] // 8, 8, LANES), axis=0)

    def measure(pair, sums):
        kept_a, sent_a = spots(mine, pair, side, orders_a, depth)
        kept_b, sent_b = spots(mine, pair, side, orders_b, depth)
        first = sums[0] + fold(own_a[kept_a]) + fold(own_b[kept_b])
        second = sums[1] + fold(other_a[sent_a]) + fold(other_b[sent_b])
        return first, second

    zero = jnp.zeros((8, LANES), F32)
    sums = lax.fori_loop(0, pairs, measure, (zero, zero))
    total = jnp.sum(sums[0] + sums[1], axis=(0, 1), keepdims=True)
    factor = jnp.minimum(1.0, limit / jnp.sqrt(total))

    def emit(block_a, block_b, at):
        down_ref[pl.ds(pl.multiple_of(at * LANES, LANES), LANES), :] = (block_a * factor).T
        lanes = pl.ds(pl.multiple_of(at * LANES, LANES), LANES)
        gate_ref[:, lanes] = block_b[:experts] * factor
        rows = pl.ds(pl.multiple_of(at % per * up_rows, up_rows), up_rows)
        lanes = pl.ds(pl.multiple_of(at // per * LANES, LANES), LANES)
        up_ref[rows, lanes] = block_b[experts:] * factor

    def write(pair, carry):
        kept_a, sent_a = spots(mine, pair, side, orders_a, depth)
        kept_b, sent_b = spots(mine, pair, side, orders_b, depth)
        emit(own_a[kept_a], own_b[kept_b], 2 * pair + side)
        emit(other_a[sent_a], other_b[sent_b], 2 * pair + 1 - side)
        return carry

    lax.fori_loop(0, pairs, write, 0)
    stats = jnp.where(side == 0, stat_own[...], stat_other[...])
    load_ref[...] = stats / stats[2:3]


def clip_write(where, own_a, other_a, own_b, other_b, stat_own, stat_other, outs, experts, orders_a, orders_b):
    pairs, ranks = own_a.shape[0], own_a.shape[1]
    width = 2 * pairs * LANES
    limit = math.sqrt(width * ranks + ranks * outs + width * experts)
    vmem = pl.BlockSpec(memory_space=VMEM)
    return pl.pallas_call(
        functools.partial(clip_kernel, orders_a, orders_b, experts, limit),
        out_shape=[
            jax.ShapeDtypeStruct((width, ranks), F32),
            jax.ShapeDtypeStruct((ranks, outs), F32),
            jax.ShapeDtypeStruct((experts, width), F32),
            jax.ShapeDtypeStruct((8, LANES), F32),
        ],
        in_specs=[pl.BlockSpec(memory_space=SMEM)] + [vmem] * 6,
        out_specs=[vmem] * 4,
        compiler_params=pltpu.CompilerParams(vmem_limit_bytes=HIGH),
        name="clip_write",
    )(where, own_a, other_a, own_b, other_b, stat_own, stat_other)


def swap(array, masks):
    size = lax.axis_size("dp")
    return lax.ppermute(array, "dp", [(i, i ^ masks[i & 1]) for i in range(size)])


def halve(keep, recv):
    half = keep.shape[0] // 2
    send = keep[half:] + recv[half:]
    return keep[:half] + recv[:half], send


def on_device(token_ids, tokens, frozen, down, up, gate, upstream):
    experts = gate.shape[1]
    rank = down.shape[1] // experts
    outs = frozen.shape[1]
    rows = tokens.shape[0]
    size = lax.axis_size("dp")
    bits = size.bit_length() - 2
    depth = (tokens.shape[1] // (2 * LANES)).bit_length() - 1
    rest = tuple(range(2, bits))
    orders_a = ((0, 1) + rest, (1, 0) + rest)
    orders_b = ((0, 1) + rest, (1, 0) + rest)
    me = lax.axis_index("dp")
    where = jnp.stack([me >> 1, me & 1]).astype(jnp.int32)
    ids = token_ids.reshape(rows // LANES, LANES)
    masks_a = [(2 << orders_a[0][s], 2 << orders_a[1][s]) for s in range(bits)]
    masks_b = [(2 << orders_b[0][s], 2 << orders_b[1][s]) for s in range(bits)]

    keep_a, send_a, keep_b, send_b, weighted, low_grad, plain, share, wide = local_grads(
        where, ids, gate.T, down, up, tokens, upstream, orders_a, orders_b
    )
    recv_b = swap(send_b, (1, 1))
    recv_a = swap(send_a, (1, 1))
    projected = project(tokens, weighted, frozen, up)
    for step in range(bits):
        if step < depth:
            keep_b, send_b = halve(keep_b, recv_b)
            keep_a, send_a = halve(keep_a, recv_a)
        else:
            keep_b = send_b = keep_b + recv_b
            keep_a = send_a = keep_a + recv_a
        recv_b = swap(send_b, masks_b[step])
        recv_a = swap(send_a, masks_a[step])
    own_b, stats = owner_rows(keep_b, recv_b, experts)
    own_a = keep_a + recv_a
    input_grad = input_grads(ids, upstream, low_grad, plain, share, stats, frozen, wide, experts)
    stat_other = swap(stats, (1, 1))
    for step in reversed(range(depth)):
        own_b = jnp.concatenate([own_b, swap(own_b, masks_b[step])], axis=0)
        own_a = jnp.concatenate([own_a, swap(own_a, masks_a[step])], axis=0)
    other_b = swap(own_b, (1, 1))
    other_a = swap(own_a, (1, 1))
    clipped_down, clipped_up, clipped_gate, summary = clip_write(
        where, own_a, other_a, own_b, other_b, stats, stat_other, outs, experts, orders_a, orders_b
    )
    return (
        projected,
        input_grad,
        clipped_down,
        clipped_up,
        clipped_gate.T,
        summary[0, ::rank],
        summary[1, 0],
    )


def solution(mesh):
    placed = (P("dp"), P("dp", None), P(), P(), P(), P(), P("dp", None))
    return jax.shard_map(
        on_device,
        mesh=mesh,
        in_specs=placed,
        out_specs=(P("dp", None), P("dp", None), P(), P(), P(), P(), P()),
        check_vma=False,
    )
```

time: 238 us -> 126 us (0.53)
  matrix products: 79.3 us -> 0 us
  Pallas kernels: 0 us -> 56 us
  waiting for transfers between devices: 80.3 us -> 26.9 us
  blocking collectives: 42.4 us -> 0 us
  starting transfers between devices: 0.04 us -> 31.5 us
  between operations: 19.4 us -> 0.82 us
  other arithmetic: 13.5 us -> 4.38 us
  local copies, waits for them, and re-layouts: 2.14 us -> 5.64 us
    psum x1 -> x0, waiting for transfers between devices: 80.3 us -> none  [reduce_clip(): summed = lax.psum((terms[0], terms[1], terms[2]), 'dp')]
    dot_general x12 -> x0, matrix products: 79.3 us -> none  [the longest x3 31.8 us: right_dot(): lax.dot_general(first, second, (((1,), (1,)), ((), ())), preferred_elemen...]
    pallas_call x0 -> x5, Pallas kernels: none -> 56 us  [the longest x1 17.2 us: local_grads(): pl.pallas_call(functools.partial(local_kernel, orders_a, orders_b, expert...]
    psum x1 -> x0, blocking collectives: 42.4 us -> none  [share_stats(): return lax.psum((local[0], local[1], local[2]), 'dp')]
    ppermute x0 -> x21, starting transfers between devices: none -> 31.5 us  [swap(): lax.ppermute(array, 'dp', [(i, i ^ masks[i & 1]) for i in range(size)])]
    ppermute x0 -> x21, waiting for transfers between devices: none -> 26.9 us  [swap(): lax.ppermute(array, 'dp', [(i, i ^ masks[i & 1]) for i in range(size)])]
    reduce_sum x8 -> x0, other arithmetic: 6.98 us -> none  [the longest x1 2.73 us: reduce_clip(): jnp.sum(grads[0] * grads[0]) + jnp.sum(grads[1] * grads[1])]
    mul x5 -> x0, other arithmetic: 5.24 us -> none  [the longest x3 5.23 us: reduce_clip(): return (grads[0] * factor, grads[1] * factor, grads[2] * factor)]
  transfers between devices with their start and end apart: 1 -> 21, of which waited for: 1 -> 11; matrix products, arithmetic and copies ran while one was open for 24% -> 4% of each run, Pallas kernels for 0% -> 27%
where the time goes in v1:
time: 126 us; the launch traced here: 125 us
  Pallas kernels  56 us (44%)
  starting transfers between devices  31.5 us (25%)
  waiting for transfers between devices  26.9 us (21%)
  local copies, waits for them, and re-layouts  5.64 us (4%)
  other arithmetic  4.38 us (3%)
    ppermute x21, starting transfers between devices, swap(): lax.ppermute(array, 'dp', [(i, i ^ masks[i & 1]) for i in range(size)])  31.5 us
    ppermute x21, waiting for transfers between devices, swap(): lax.ppermute(array, 'dp', [(i, i ^ masks[i & 1]) for i in range(size)])  26.9 us
    pallas_call x1, Pallas kernels, local_grads(): pl.pallas_call(functools.partial(local_kernel, orders_a, orders_b, expert...  17.2 us
    pallas_call x1, Pallas kernels, input_grads(): pl.pallas_call(functools.partial(input_kernel, experts), grid=(steps,), o...  17.1 us
    pallas_call x1, Pallas kernels, project(): pl.pallas_call(project_kernel, grid=(TILES,), out_shape=jax.ShapeDtypeStr...  14.7 us
    pallas_call x1, Pallas kernels, clip_write(): pl.pallas_call(functools.partial(clip_kernel, orders_a, orders_b, experts...  5.5 us
    unnamed x23, local copies, waits for them, and re-layouts  3.13 us
  transfers between devices with their start and end apart: 21, of which 11 were waited for; matrix products, arithmetic and copies ran while one was open for 4% of the time, Pallas kernels for 27%

profile of v1, /device:TPU:0, one launch (start us, length us, event | category | flops | bytes accessed | tf_op | source)
XLA Modules:
  0.0 125.2 jit_solution(10137888148588813104)
XLA Ops:
  1.3 17.2 %local_grads.1 = (f32[16,128,128]{2,1,0:T(8,128)}, f32[16,128,128]{2,1,0:T(8,128)}, f32[16,80,128]{2,1,0:T(8,128)}, f32[16,80,128]{2,1,0:T(8,128)}, bf16[1024,12...) custom-call(s32[2]{0:T(128)} %pad_add_fusion.where_ref, ...), custom_call_target="tpu_custom_call" | custom-call | flops 4294967296 | bytes 10485760 | tf_op jit(solution)/shard_map/local_grads/pallas_call | solution.py:172
  19.1 2.4 %collective-permute-done.5 = f32[16,128,128]{2,1,0:T(8,128)S(1)} collective-permute-done((f32[16,128,128]{2,1,0:T(8,128)}, f32[16,128,128]{2,1,0:T(8,128)S(1)}, u32[]{:S(2)}, u32[]{:S(2)}) %collective-permute-start.5) | collective-permute-done | bytes 1048608 | tf_op jit(solution)/shard_map/ppermute | solution.py:403
  21.5 1.3 %slice_add_fusion.1 = (f32[8,128,128]{2,1,0:T(8,128)S(1)}, f32[8,128,128]{2,1,0:T(8,128)S(1)}) fusion(f32[16,128,128]{2,1,0:T(8,128)S(1)} %collective-permute-done.5, f32[16,128,128]{2,1,0:T(8,128)} %get-tuple-element.30), kind=kLoop, calls=%fused_computation.1 | loop fusion | flops 262144 | bytes 3145728 | tf_op jit(solution)/shard_map/add | solution.py:409
  22.8 2.9 %collective-permute-start.6 = (f32[8,128,128]{2,1,0:T(8,128)S(1)}, f32[8,128,128]{2,1,0:T(8,128)S(1)}, u32[]{:S(2)}, u32[]{:S(2)}) collective-permute-start(f32[8,128,128]{2,1,0:T(8,128)S(1)} %get-tuple-element.40), channel_id=1, source_target_pairs={{0,2},{1,5},{2,0},{3,7},{4,6},{5,1},{6,4},{7,3},{8,10},{9,13},{10,... | collective-permute-start | bytes 1572872 | tf_op jit(solution)/shard_map/ppermute | solution.py:403
  25.9 7.0 %collective-permute-done.6 = f32[8,128,128]{2,1,0:T(8,128)S(1)} collective-permute-done((f32[8,128,128]{2,1,0:T(8,128)S(1)}, f32[8,128,128]{2,1,0:T(8,128)S(1)}, u32[]{:S(2)}, u32[]{:S(2)}) %collective-permute-start.6) | collective-permute-done | bytes 524320 | tf_op jit(solution)/shard_map/ppermute | solution.py:403
  33.0 2.1 %collective-permute-start.7 = (f32[4,128,128]{2,1,0:T(8,128)S(1)}, f32[4,128,128]{2,1,0:T(8,128)S(1)}, u32[]{:S(2)}, u32[]{:S(2)}) collective-permute-start(f32[4,128,128]{2,1,0:T(8,128)S(1)} %get-tuple-element.44), channel_id=1, source_target_pairs={{0,4},{1,3},{2,6},{3,1},{4,0},{5,7},{6,2},{7,5},{8,12},{9,11},{10,... | collective-permute-start | bytes 786440 | tf_op jit(solution)/shard_map/ppermute | solution.py:403
  35.1 2.5 %collective-permute-done.1 = f32[8,80,128]{2,1,0:T(8,128)S(1)} collective-permute-done((f32[8,80,128]{2,1,0:T(8,128)S(1)}, f32[8,80,128]{2,1,0:T(8,128)S(1)}, u32[]{:S(2)}, u32[]{:S(2)}) %collective-permute-start.1) | collective-permute-done | bytes 327712 | tf_op jit(solution)/shard_map/ppermute | solution.py:403
  37.7 2.4 %collective-permute-start.2 = (f32[4,80,128]{2,1,0:T(8,128)S(1)}, f32[4,80,128]{2,1,0:T(8,128)S(1)}, u32[]{:S(2)}, u32[]{:S(2)}) collective-permute-start(f32[4,80,128]{2,1,0:T(8,128)S(1)} %get-tuple-element.46), channel_id=1, source_target_pairs={{0,4},{1,3},{2,6},{3,1},{4,0},{5,7},{6,2},{7,5},{8,12},{9,11},{10,... | collective-permute-start | bytes 491528 | tf_op jit(solution)/shard_map/ppermute | solution.py:403
  40.1 1.6 %collective-permute-start.8 = (f32[2,128,128]{2,1,0:T(8,128)S(1)}, f32[2,128,128]{2,1,0:T(8,128)S(1)}, u32[]{:S(2)}, u32[]{:S(2)}) collective-permute-start(f32[2,128,128]{2,1,0:T(8,128)S(1)} %get-tuple-element.48), channel_id=1, source_target_pairs={{0,8},{1,9},{2,10},{3,11},{4,12},{5,13},{6,14},{7,15},{8,0},{9,1},... | collective-permute-start | bytes 393224 | tf_op jit(solution)/shard_map/ppermute | solution.py:403
  41.8 1.6 %collective-permute-done.2 = f32[4,80,128]{2,1,0:T(8,128)S(1)} collective-permute-done((f32[4,80,128]{2,1,0:T(8,128)S(1)}, f32[4,80,128]{2,1,0:T(8,128)S(1)}, u32[]{:S(2)}, u32[]{:S(2)}) %collective-permute-start.2) | collective-permute-done | bytes 163872 | tf_op jit(solution)/shard_map/ppermute | solution.py:403
  43.4 2.1 %collective-permute-start.3 = (f32[2,80,128]{2,1,0:T(8,128)S(1)}, f32[2,80,128]{2,1,0:T(8,128)S(1)}, u32[]{:S(2)}, u32[]{:S(2)}) collective-permute-start(f32[2,80,128]{2,1,0:T(8,128)S(1)} %get-tuple-element.50), channel_id=1, source_target_pairs={{0,8},{1,9},{2,10},{3,11},{4,12},{5,13},{6,14},{7,15},{8,0},{9,1},... | collective-permute-start | bytes 245768 | tf_op jit(solution)/shard_map/ppermute | solution.py:403
  46.1 2.8 %collective-permute-start.9 = (f32[1,128,128]{2,1,0:T(8,128)S(1)}, f32[1,128,128]{2,1,0:T(8,128)S(1)}, u32[]{:S(2)}, u32[]{:S(2)}) collective-permute-start(f32[1,128,128]{2,1,0:T(8,128)S(1)} %slice_add_fusion.12), channel_id=1, source_target_pairs={{0,16},{1,17},{2,18},{3,19},{4,20},{5,21},{6,22},{7,23},{8,24},{9,... | collective-permute-start | bytes 196616 | tf_op jit(solution)/shard_map/ppermute | solution.py:403
  49.6 2.1 %collective-permute-start.4 = (f32[1,80,128]{2,1,0:T(8,128)S(1)}, f32[1,80,128]{2,1,0:T(8,128)S(1)}, u32[]{:S(2)}, u32[]{:S(2)}) collective-permute-start(f32[1,80,128]{2,1,0:T(8,128)S(1)} %get-tuple-element.51), channel_id=1, source_target_pairs={{0,16},{1,17},{2,18},{3,19},{4,20},{5,21},{6,22},{7,23},{8,24},{9,... | collective-permute-start | bytes 122888 | tf_op jit(solution)/shard_map/ppermute | solution.py:403
  51.8 2.4 %collective-permute-start.10 = (f32[1,128,128]{2,1,0:T(8,128)S(1)}, f32[1,128,128]{2,1,0:T(8,128)S(1)}, u32[]{:S(2)}, u32[]{:S(2)}) collective-permute-start(f32[1,128,128]{2,1,0:T(8,128)S(1)} %get-tuple-element.38), channel_id=1, source_target_pairs={{0,16},{1,17},{2,18},{3,19},{4,20},{5,21},{6,22},{7,23},{8,24},{9,... | collective-permute-start | bytes 196616 | tf_op jit(solution)/shard_map/ppermute | solution.py:403
  54.2 14.7 %project.1 = bf16[1024,1024]{1,0:T(8,128)(2,1)} custom-call(bf16[1024,4096]{1,0:T(8,128)(2,1)} %tok_ref.1, bf16[1024,128]{1,0:T(8,128)(2,1)} %get-tuple-element.22.weighted_ref, bf16[4096,1024]{1,0:T(8,128)(2,1)} %frozen_ref.3, bf16[128,1024]{1,0:T(8,128)(2,1)} %up_ref.3), custom_call_target="tpu_custom_call" | custom-call | flops 8858370048 | bytes 18874368 | tf_op jit(solution)/shard_map/project/pallas_call | solution.py:215
  69.5 1.5 %owner_rows.1 = (f32[1,40,128]{2,1,0:T(8,128)}, f32[8,128]{1,0:T(8,128)}) custom-call(f32[1,80,128]{2,1,0:T(8,128)} %get-tuple-element.52.keep_ref, f32[1,80,128]{2,1,0:T(8,128)} %copy-done.6), custom_call_target="tpu_custom_call" | custom-call | tf_op jit(solution)/shard_map/owner_rows/pallas_call | solution.py:266
  71.6 2.1 %collective-permute-start.11 = (f32[2,128,128]{2,1,0:T(8,128)S(1)}, f32[2,128,128]{2,1,0:T(8,128)S(1)}, u32[]{:S(2)}, u32[]{:S(2)}) collective-permute-start(f32[2,128,128]{2,1,0:T(8,128)S(1)} %pad_maximum_fusion.3), channel_id=1, source_target_pairs={{0,8},{1,9},{2,10},{3,11},{4,12},{5,13},{6,14},{7,15},{8,0},{9,1},... | collective-permute-start | bytes 393224 | tf_op jit(solution)/shard_map/ppermute | solution.py:403
  74.5 1.5 %collective-permute-done.15 = f32[1,40,128]{2,1,0:T(8,128)S(1)} collective-permute-done((f32[1,40,128]{2,1,0:T(8,128)}, f32[1,40,128]{2,1,0:T(8,128)S(1)}, u32[]{:S(2)}, u32[]{:S(2)}) %collective-permute-start.15) | collective-permute-done | bytes 20512 | tf_op jit(solution)/shard_map/ppermute | solution.py:403
  76.7 2.3 %collective-permute-start.16 = (f32[2,40,128]{2,1,0:T(8,128)S(1)}, f32[2,40,128]{2,1,0:T(8,128)S(1)}, u32[]{:S(2)}, u32[]{:S(2)}) collective-permute-start(f32[2,40,128]{2,1,0:T(8,128)S(1)} %pad_maximum_fusion.5), channel_id=1, source_target_pairs={{0,8},{1,9},{2,10},{3,11},{4,12},{5,13},{6,14},{7,15},{8,0},{9,1},... | collective-permute-start | bytes 122888 | tf_op jit(solution)/shard_map/ppermute | solution.py:403
  79.1 2.4 %collective-permute-start.12 = (f32[4,128,128]{2,1,0:T(8,128)S(1)}, f32[4,128,128]{2,1,0:T(8,128)S(1)}, u32[]{:S(2)}, u32[]{:S(2)}) collective-permute-start(f32[4,128,128]{2,1,0:T(8,128)S(1)} %pad_maximum_fusion.1), channel_id=1, source_target_pairs={{0,4},{1,3},{2,6},{3,1},{4,0},{5,7},{6,2},{7,5},{8,12},{9,11},{10,... | collective-permute-start | bytes 786440 | tf_op jit(solution)/shard_map/ppermute | solution.py:403
  81.5 0.7 pad_maximum_fusion.4
  82.3 1.9 %collective-permute-start.17 = (f32[4,40,128]{2,1,0:T(8,128)S(1)}, f32[4,40,128]{2,1,0:T(8,128)S(1)}, u32[]{:S(2)}, u32[]{:S(2)}) collective-permute-start(f32[4,40,128]{2,1,0:T(8,128)S(1)} %pad_maximum_fusion.4), channel_id=1, source_target_pairs={{0,4},{1,3},{2,6},{3,1},{4,0},{5,7},{6,2},{7,5},{8,12},{9,11},{10,... | collective-permute-start | bytes 245768 | tf_op jit(solution)/shard_map/ppermute | solution.py:403
  84.2 3.1 %collective-permute-done.12 = f32[4,128,128]{2,1,0:T(8,128)S(1)} collective-permute-done((f32[4,128,128]{2,1,0:T(8,128)S(1)}, f32[4,128,128]{2,1,0:T(8,128)S(1)}, u32[]{:S(2)}, u32[]{:S(2)}) %collective-permute-start.12) | collective-permute-done | bytes 262176 | tf_op jit(solution)/shard_map/ppermute | solution.py:403
  87.2 1.4 %collective-permute-start.13 = (f32[8,128,128]{2,1,0:T(8,128)S(1)}, f32[8,128,128]{2,1,0:T(8,128)S(1)}, u32[]{:S(2)}, u32[]{:S(2)}) collective-permute-start(f32[8,128,128]{2,1,0:T(8,128)S(1)} %pad_maximum_fusion), channel_id=1, source_target_pairs={{0,2},{1,5},{2,0},{3,7},{4,6},{5,1},{6,4},{7,3},{8,10},{9,13},{10,... | collective-permute-start | bytes 1572872 | tf_op jit(solution)/shard_map/ppermute | solution.py:403
  89.0 1.4 %collective-permute-start.18 = (f32[8,40,128]{2,1,0:T(8,128)S(1)}, f32[8,40,128]{2,1,0:T(8,128)S(1)}, u32[]{:S(2)}, u32[]{:S(2)}) collective-permute-start(f32[8,40,128]{2,1,0:T(8,128)S(1)} %pad_maximum_fusion.2), channel_id=1, source_target_pairs={{0,2},{1,5},{2,0},{3,7},{4,6},{5,1},{6,4},{7,3},{8,10},{9,13},{10,... | collective-permute-start | bytes 491528 | tf_op jit(solution)/shard_map/ppermute | solution.py:403
  90.4 6.1 %collective-permute-done.13 = f32[8,128,128]{2,1,0:T(8,128)S(1)} collective-permute-done((f32[8,128,128]{2,1,0:T(8,128)S(1)}, f32[8,128,128]{2,1,0:T(8,128)S(1)}, u32[]{:S(2)}, u32[]{:S(2)}) %collective-permute-start.13) | collective-permute-done | bytes 524320 | tf_op jit(solution)/shard_map/ppermute | solution.py:403
  96.6 1.6 %collective-permute-done.18 = f32[8,40,128]{2,1,0:T(8,128)S(1)} collective-permute-done((f32[8,40,128]{2,1,0:T(8,128)S(1)}, f32[8,40,128]{2,1,0:T(8,128)S(1)}, u32[]{:S(2)}, u32[]{:S(2)}) %collective-permute-start.18) | collective-permute-done | bytes 163872 | tf_op jit(solution)/shard_map/ppermute | solution.py:403
  98.4 17.1 %input_grads.1 = bf16[1024,4096]{1,0:T(8,128)(2,1)} custom-call(s32[8,128]{1,0:T(8,128)} %bitcast.10, bf16[1024,1024]{1,0:T(8,128)(2,1)} %ups_ref.1, bf16[1024,128]{1,0:T(8,128)(2,1)} %get-tuple-element.23.lowgrad_ref, f32[1024,128]{1,0:T(8,128)} %get-tuple-element.24.plain_ref, f32[1024,128]{1,0:T(8,128)} %get-tuple-element.25.share_ref, ...), custom_call_target="tpu_custom_call" | custom-call | flops 10737418240 | bytes 18874368 | tf_op jit(solution)/shard_map/input_grads/pallas_call | solution.py:312
  116.3 1.0 copy-done.1
  117.3 5.5 %clip_write.1 = (f32[4096,128]{1,0:T(8,128)}, f32[128,1024]{1,0:T(8,128)}, f32[8,4096]{1,0:T(8,128)}, f32[8,128]{1,0:T(8,128)}) custom-call(s32[2]{0:T(128)} %pad_add_fusion.where_ref, f32[16,128,128]{2,1,0:T(8,128)} %copy-done, f32[16,128,128]{2,1,0:T(8,128)} %copy-done.1, f32[16,40,128]{2,1,0:T(8,128)} %copy-done.3, f32[16,40,128]{2,1,0:T(8,128)} %copy-done.5, ...), custom_call_target="tpu_custom_call" | custom-call | tf_op jit(solution)/shard_map/clip_write/pallas_call | solution.py:386
  122.8 1.3 %slice.134 = f32[1,8]{1,0:T(1,128)} slice(f32[8,128]{1,0:T(8,128)} %get-tuple-element.36), slice={[0:1:1], [0:128:16]} | slice | bytes 64 | tf_op jit(solution)/shard_map/slice | solution.py:462
  124.0 1.2 slice.135
  (58 shorter events, 7.0 us)
Async XLA Ops:
  18.5 7.3 %copy-start.2 = (f32[16,80,128]{2,1,0:T(8,128)S(1)}, f32[16,80,128]{2,1,0:T(8,128)}, u32[]{:S(2)}) copy-start(f32[16,80,128]{2,1,0:T(8,128)} %get-tuple-element.26) | copy-start | bytes 1966084
  18.5 3.1 %collective-permute-start.5 = (f32[16,128,128]{2,1,0:T(8,128)}, f32[16,128,128]{2,1,0:T(8,128)S(1)}, u32[]{:S(2)}, u32[]{:S(2)}) collective-permute-start(f32[16,128,128]{2,1,0:T(8,128)} %get-tuple-element.31), channel_id=1, source_target_pairs={{0,1},{1,0},{2,3},{3,2},{4,5},{5,4},{6,7},{7,6},{8,9},{9,8},{10,11... | collective-permute-start | bytes 3145736 | tf_op jit(solution)/shard_map/ppermute | solution.py:403
  19.0 6.7 %collective-permute-start = (f32[16,80,128]{2,1,0:T(8,128)}, f32[16,80,128]{2,1,0:T(8,128)S(1)}, u32[]{:S(2)}, u32[]{:S(2)}) collective-permute-start(f32[16,80,128]{2,1,0:T(8,128)} %get-tuple-element.27), channel_id=1, source_target_pairs={{0,1},{1,0},{2,3},{3,2},{4,5},{5,4},{6,7},{7,6},{8,9},{9,8},{10,11... | collective-permute-start | bytes 1966088 | tf_op jit(solution)/shard_map/ppermute | solution.py:403
  22.8 10.1 %collective-permute-start.6 = (f32[8,128,128]{2,1,0:T(8,128)S(1)}, f32[8,128,128]{2,1,0:T(8,128)S(1)}, u32[]{:S(2)}, u32[]{:S(2)}) collective-permute-start(f32[8,128,128]{2,1,0:T(8,128)S(1)} %get-tuple-element.40), channel_id=1, source_target_pairs={{0,2},{1,5},{2,0},{3,7},{4,6},{5,1},{6,4},{7,3},{8,10},{9,13},{10,... | collective-permute-start | bytes 1572872 | tf_op jit(solution)/shard_map/ppermute | solution.py:403
  25.8 11.8 %collective-permute-start.1 = (f32[8,80,128]{2,1,0:T(8,128)S(1)}, f32[8,80,128]{2,1,0:T(8,128)S(1)}, u32[]{:S(2)}, u32[]{:S(2)}) collective-permute-start(f32[8,80,128]{2,1,0:T(8,128)S(1)} %get-tuple-element.42), channel_id=1, source_target_pairs={{0,2},{1,5},{2,0},{3,7},{4,6},{5,1},{6,4},{7,3},{8,10},{9,13},{10,... | collective-permute-start | bytes 983048 | tf_op jit(solution)/shard_map/ppermute | solution.py:403
  33.0 7.1 %collective-permute-start.7 = (f32[4,128,128]{2,1,0:T(8,128)S(1)}, f32[4,128,128]{2,1,0:T(8,128)S(1)}, u32[]{:S(2)}, u32[]{:S(2)}) collective-permute-start(f32[4,128,128]{2,1,0:T(8,128)S(1)} %get-tuple-element.44), channel_id=1, source_target_pairs={{0,4},{1,3},{2,6},{3,1},{4,0},{5,7},{6,2},{7,5},{8,12},{9,11},{10,... | collective-permute-start | bytes 786440 | tf_op jit(solution)/shard_map/ppermute | solution.py:403
  37.7 5.7 %collective-permute-start.2 = (f32[4,80,128]{2,1,0:T(8,128)S(1)}, f32[4,80,128]{2,1,0:T(8,128)S(1)}, u32[]{:S(2)}, u32[]{:S(2)}) collective-permute-start(f32[4,80,128]{2,1,0:T(8,128)S(1)} %get-tuple-element.46), channel_id=1, source_target_pairs={{0,4},{1,3},{2,6},{3,1},{4,0},{5,7},{6,2},{7,5},{8,12},{9,11},{10,... | collective-permute-start | bytes 491528 | tf_op jit(solution)/shard_map/ppermute | solution.py:403
  40.1 6.0 %collective-permute-start.8 = (f32[2,128,128]{2,1,0:T(8,128)S(1)}, f32[2,128,128]{2,1,0:T(8,128)S(1)}, u32[]{:S(2)}, u32[]{:S(2)}) collective-permute-start(f32[2,128,128]{2,1,0:T(8,128)S(1)} %get-tuple-element.48), channel_id=1, source_target_pairs={{0,8},{1,9},{2,10},{3,11},{4,12},{5,13},{6,14},{7,15},{8,0},{9,1},... | collective-permute-start | bytes 393224 | tf_op jit(solution)/shard_map/ppermute | solution.py:403
  43.4 5.5 %collective-permute-start.3 = (f32[2,80,128]{2,1,0:T(8,128)S(1)}, f32[2,80,128]{2,1,0:T(8,128)S(1)}, u32[]{:S(2)}, u32[]{:S(2)}) collective-permute-start(f32[2,80,128]{2,1,0:T(8,128)S(1)} %get-tuple-element.50), channel_id=1, source_target_pairs={{0,8},{1,9},{2,10},{3,11},{4,12},{5,13},{6,14},{7,15},{8,0},{9,1},... | collective-permute-start | bytes 245768 | tf_op jit(solution)/shard_map/ppermute | solution.py:403
  46.1 5.7 %collective-permute-start.9 = (f32[1,128,128]{2,1,0:T(8,128)S(1)}, f32[1,128,128]{2,1,0:T(8,128)S(1)}, u32[]{:S(2)}, u32[]{:S(2)}) collective-permute-start(f32[1,128,128]{2,1,0:T(8,128)S(1)} %slice_add_fusion.12), channel_id=1, source_target_pairs={{0,16},{1,17},{2,18},{3,19},{4,20},{5,21},{6,22},{7,23},{8,24},{9,... | collective-permute-start | bytes 196616 | tf_op jit(solution)/shard_map/ppermute | solution.py:403
  49.6 19.3 %collective-permute-start.4 = (f32[1,80,128]{2,1,0:T(8,128)S(1)}, f32[1,80,128]{2,1,0:T(8,128)S(1)}, u32[]{:S(2)}, u32[]{:S(2)}) collective-permute-start(f32[1,80,128]{2,1,0:T(8,128)S(1)} %get-tuple-element.51), channel_id=1, source_target_pairs={{0,16},{1,17},{2,18},{3,19},{4,20},{5,21},{6,22},{7,23},{8,24},{9,... | collective-permute-start | bytes 122888 | tf_op jit(solution)/shard_map/ppermute | solution.py:403
  51.8 19.8 %collective-permute-start.10 = (f32[1,128,128]{2,1,0:T(8,128)S(1)}, f32[1,128,128]{2,1,0:T(8,128)S(1)}, u32[]{:S(2)}, u32[]{:S(2)}) collective-permute-start(f32[1,128,128]{2,1,0:T(8,128)S(1)} %get-tuple-element.38), channel_id=1, source_target_pairs={{0,16},{1,17},{2,18},{3,19},{4,20},{5,21},{6,22},{7,23},{8,24},{9,... | collective-permute-start | bytes 196616 | tf_op jit(solution)/shard_map/ppermute | solution.py:403
  68.9 0.6 copy-start.6
  71.0 18.0 %copy-start.4 = (f32[1,40,128]{2,1,0:T(8,128)S(1)}, f32[1,40,128]{2,1,0:T(8,128)}, u32[]{:S(2)}) copy-start(f32[1,40,128]{2,1,0:T(8,128)} %get-tuple-element.32) | copy-start | bytes 61444
  71.0 5.0 %collective-permute-start.15 = (f32[1,40,128]{2,1,0:T(8,128)}, f32[1,40,128]{2,1,0:T(8,128)S(1)}, u32[]{:S(2)}, u32[]{:S(2)}) collective-permute-start(f32[1,40,128]{2,1,0:T(8,128)} %get-tuple-element.32), channel_id=1, source_target_pairs={{0,16},{1,17},{2,18},{3,19},{4,20},{5,21},{6,22},{7,23},{8,24},{9,... | collective-permute-start | bytes 61448 | tf_op jit(solution)/shard_map/ppermute | solution.py:403
  71.6 7.4 %collective-permute-start.11 = (f32[2,128,128]{2,1,0:T(8,128)S(1)}, f32[2,128,128]{2,1,0:T(8,128)S(1)}, u32[]{:S(2)}, u32[]{:S(2)}) collective-permute-start(f32[2,128,128]{2,1,0:T(8,128)S(1)} %pad_maximum_fusion.3), channel_id=1, source_target_pairs={{0,8},{1,9},{2,10},{3,11},{4,12},{5,13},{6,14},{7,15},{8,0},{9,1},... | collective-permute-start | bytes 393224 | tf_op jit(solution)/shard_map/ppermute | solution.py:403
  74.5 41.0 %collective-permute-start.20 = (f32[8,128]{1,0:T(8,128)}, f32[8,128]{1,0:T(8,128)S(1)}, u32[]{:S(2)}, u32[]{:S(2)}) collective-permute-start(f32[8,128]{1,0:T(8,128)} %get-tuple-element.28.stats_ref.stat_own), channel_id=1, source_target_pairs={{0,1},{1,0},{2,3},{3,2},{4,5},{5,4},{6,7},{7,6},{8,9},{9,8},{10,11... | collective-permute-start | bytes 12296 | tf_op jit(solution)/shard_map/ppermute | solution.py:403
  76.7 4.8 %collective-permute-start.16 = (f32[2,40,128]{2,1,0:T(8,128)S(1)}, f32[2,40,128]{2,1,0:T(8,128)S(1)}, u32[]{:S(2)}, u32[]{:S(2)}) collective-permute-start(f32[2,40,128]{2,1,0:T(8,128)S(1)} %pad_maximum_fusion.5), channel_id=1, source_target_pairs={{0,8},{1,9},{2,10},{3,11},{4,12},{5,13},{6,14},{7,15},{8,0},{9,1},... | collective-permute-start | bytes 122888 | tf_op jit(solution)/shard_map/ppermute | solution.py:403
  79.1 8.1 %collective-permute-start.12 = (f32[4,128,128]{2,1,0:T(8,128)S(1)}, f32[4,128,128]{2,1,0:T(8,128)S(1)}, u32[]{:S(2)}, u32[]{:S(2)}) collective-permute-start(f32[4,128,128]{2,1,0:T(8,128)S(1)} %pad_maximum_fusion.1), channel_id=1, source_target_pairs={{0,4},{1,3},{2,6},{3,1},{4,0},{5,7},{6,2},{7,5},{8,12},{9,11},{10,... | collective-permute-start | bytes 786440 | tf_op jit(solution)/shard_map/ppermute | solution.py:403
  82.3 6.7 %collective-permute-start.17 = (f32[4,40,128]{2,1,0:T(8,128)S(1)}, f32[4,40,128]{2,1,0:T(8,128)S(1)}, u32[]{:S(2)}, u32[]{:S(2)}) collective-permute-start(f32[4,40,128]{2,1,0:T(8,128)S(1)} %pad_maximum_fusion.4), channel_id=1, source_target_pairs={{0,4},{1,3},{2,6},{3,1},{4,0},{5,7},{6,2},{7,5},{8,12},{9,11},{10,... | collective-permute-start | bytes 245768 | tf_op jit(solution)/shard_map/ppermute | solution.py:403
  87.2 9.2 %collective-permute-start.13 = (f32[8,128,128]{2,1,0:T(8,128)S(1)}, f32[8,128,128]{2,1,0:T(8,128)S(1)}, u32[]{:S(2)}, u32[]{:S(2)}) collective-permute-start(f32[8,128,128]{2,1,0:T(8,128)S(1)} %pad_maximum_fusion), channel_id=1, source_target_pairs={{0,2},{1,5},{2,0},{3,7},{4,6},{5,1},{6,4},{7,3},{8,10},{9,13},{10,... | collective-permute-start | bytes 1572872 | tf_op jit(solution)/shard_map/ppermute | solution.py:403
  89.0 9.3 %collective-permute-start.18 = (f32[8,40,128]{2,1,0:T(8,128)S(1)}, f32[8,40,128]{2,1,0:T(8,128)S(1)}, u32[]{:S(2)}, u32[]{:S(2)}) collective-permute-start(f32[8,40,128]{2,1,0:T(8,128)S(1)} %pad_maximum_fusion.2), channel_id=1, source_target_pairs={{0,2},{1,5},{2,0},{3,7},{4,6},{5,1},{6,4},{7,3},{8,10},{9,13},{10,... | collective-permute-start | bytes 491528 | tf_op jit(solution)/shard_map/ppermute | solution.py:403
  96.5 19.0 %copy-start = (f32[16,128,128]{2,1,0:T(8,128)}, f32[16,128,128]{2,1,0:T(8,128)S(1)}, u32[]{:S(2)}) copy-start(f32[16,128,128]{2,1,0:T(8,128)S(1)} %constant_dynamic-update-slice_fusion.own_a) | copy-start | bytes 3145732
  96.5 19.0 %collective-permute-start.14 = (f32[16,128,128]{2,1,0:T(8,128)S(1)}, f32[16,128,128]{2,1,0:T(8,128)S(1)}, u32[]{:S(2)}, u32[]{:S(2)}) collective-permute-start(f32[16,128,128]{2,1,0:T(8,128)S(1)} %constant_dynamic-update-slice_fusion.own_a), channel_id=1, source_target_pairs={{0,1},{1,0},{2,3},{3,2},{4,5},{5,4},{6,7},{7,6},{8,9},{9,8},{10,11... | collective-permute-start | bytes 3145736 | tf_op jit(solution)/shard_map/ppermute | solution.py:403
  98.3 17.2 %copy-start.3 = (f32[16,40,128]{2,1,0:T(8,128)}, f32[16,40,128]{2,1,0:T(8,128)S(1)}, u32[]{:S(2)}) copy-start(f32[16,40,128]{2,1,0:T(8,128)S(1)} %constant_dynamic-update-slice_fusion.5.own_b) | copy-start | bytes 983044
  98.3 17.2 %collective-permute-start.19 = (f32[16,40,128]{2,1,0:T(8,128)S(1)}, f32[16,40,128]{2,1,0:T(8,128)S(1)}, u32[]{:S(2)}, u32[]{:S(2)}) collective-permute-start(f32[16,40,128]{2,1,0:T(8,128)S(1)} %constant_dynamic-update-slice_fusion.5.own_b), channel_id=1, source_target_pairs={{0,1},{1,0},{2,3},{3,2},{4,5},{5,4},{6,7},{7,6},{8,9},{9,8},{10,11... | collective-permute-start | bytes 983048 | tf_op jit(solution)/shard_map/ppermute | solution.py:403
  115.5 0.6 copy-start.7
  115.5 0.8 copy-start.5
  116.3 1.0 copy-start.1

commit v2 on v1

v2 whole, which is shorter than its diff:
```python
import functools
import math

import jax
import jax.numpy as jnp
from jax import lax
from jax.experimental import pallas as pl
from jax.experimental.pallas import tpu as pltpu
from jax.sharding import PartitionSpec as P

F32 = jnp.float32
BF16 = jnp.bfloat16
LANES = 128
TILES = 4
VMEM = pltpu.VMEM
SMEM = pltpu.SMEM
HBM = pltpu.HBM
MIB = 1024 * 1024


def nn(a, b):
    return lax.dot_general(a, b, (((1,), (0,)), ((), ())), preferred_element_type=F32)


def nt(a, b):
    return lax.dot_general(a, b, (((1,), (1,)), ((), ())), preferred_element_type=F32)


def split(x):
    upper = x.astype(BF16).astype(F32)
    return upper, x - upper


def place(word, order, depth):
    spot = 0
    for step in range(depth):
        spot = spot + (((word >> order[step]) & 1) << (depth - 1 - step))
    return spot


def spots(mine, pair, side, orders, depth):
    word = (mine ^ pair) & ((1 << depth) - 1)
    first = place(word, orders[0], depth)
    second = place(word, orders[1], depth)
    kept = jnp.where(side == 0, first, second)
    sent = jnp.where(side == 0, second, first)
    return kept, sent


def local_kernel(
    orders_a, orders_b, where_ref, ids_hbm, gate_hbm, down_hbm, up_hbm, tok_hbm, ups_hbm, frozen_hbm,
    keep_a, send_a, keep_b, send_b, weighted_ref, lowgrad_ref, plain_ref, share_ref, wide_ref, ups,
    tok, up, frozen, ids, gate, down, both, back, left_t, weighted_t, grad_up, stats, sem, tok_sem, ups_sem,
):
    rows, width = tok.shape
    experts, ranks = gate.shape[0], down.shape[1]
    rank = ranks // experts
    tile = rows // TILES

    def fetch(source, target, flag):
        return pltpu.make_async_copy(source, target, flag)

    def tok_copy(t):
        part = pl.ds(t * tile, tile)
        return fetch(tok_hbm.at[part], tok.at[part], tok_sem.at[t])

    def ups_copy(t):
        part = pl.ds(t * tile, tile)
        return fetch(ups_hbm.at[part], ups.at[part], ups_sem.at[t])

    gate_copy = fetch(gate_hbm, gate, sem.at[0])
    down_copy = fetch(down_hbm, down, sem.at[1])
    ids_copy = fetch(ids_hbm, ids, sem.at[2])
    up_copy = fetch(up_hbm, up, sem.at[3])
    gate_copy.start()
    down_copy.start()
    ids_copy.start()
    up_copy.start()
    for t in range(TILES):
        tok_copy(t).start()
        ups_copy(t).start()
    frozen_copy = fetch(frozen_hbm, frozen, sem.at[4])
    frozen_copy.start()
    mine, side = where_ref[0], where_ref[1]
    row_i = lax.broadcasted_iota(jnp.int32, (experts, ranks), 0)
    col_i = lax.broadcasted_iota(jnp.int32, (experts, ranks), 1)
    twice = ((col_i % experts == row_i) & (col_i < 2 * experts)).astype(BF16)
    gate_copy.wait()
    wide_ref[:, ranks:] = nn(gate[...].astype(F32).T.astype(BF16), twice).astype(BF16)
    down_copy.wait()
    wide_ref[:, :ranks] = down[...]
    ids_copy.wait()
    count = jnp.sum((ids[...] != 0).astype(jnp.int32))
    up_copy.wait()
    for t in range(TILES):
        part = pl.ds(t * tile, tile)
        tok_copy(t).wait()
        both[part, :] = nn(tok[part, :], wide_ref[...])
        ups_copy(t).wait()
        live = lax.broadcasted_iota(jnp.int32, (tile, 1), 0) + t * tile < count
        ups[part, :] = ups[part, :] * live.astype(F32).astype(BF16)
        back[part, :] = nt(ups[part, :], up[...])
    logits = both[:, ranks:].T[:experts, :]
    shifted = logits - jnp.max(logits, axis=0, keepdims=True)
    powers = jnp.exp(shifted)
    total = jnp.sum(powers, axis=0, keepdims=True)
    prob = powers / total
    logp = shifted - jnp.log(total)
    ent = -jnp.sum(prob * logp, axis=0, keepdims=True)
    alive = (lax.broadcasted_iota(jnp.int32, (1, rows), 1) < count).astype(F32)
    share = alive * prob
    share_ref[...] = share
    big, rest = split(prob)
    mid, small = split(rest)
    parts = jnp.concatenate([big, mid, small], axis=0).T.astype(BF16)
    row_p = lax.broadcasted_iota(jnp.int32, (3 * experts, ranks), 0)
    col_p = lax.broadcasted_iota(jnp.int32, (3 * experts, ranks), 1)
    spread_by = (row_p % experts == col_p // rank).astype(BF16)
    row_g = lax.broadcasted_iota(jnp.int32, (experts, 2 * ranks), 0)
    col_g = lax.broadcasted_iota(jnp.int32, (experts, 2 * ranks), 1)
    group = ((col_g % ranks) // rank == row_g).astype(BF16)
    tasks = []
    for t in range(TILES):
        part = pl.ds(t * tile, tile)
        spread = nn(parts[t * tile : (t + 1) * tile], spread_by)
        low = both[part, :ranks].astype(BF16).astype(F32)
        weighted = (low * spread).astype(BF16)
        weighted_ref[part, :] = weighted
        weighted_t[:, part] = weighted.astype(F32).T.astype(BF16)
        low_grad = (2.0 * spread * back[part, :]).astype(BF16)
        lowgrad_ref[part, :] = low_grad
        left_t[:ranks, part] = low_grad.astype(F32).T.astype(BF16)
        big, small = split(low * back[part, :])
        tasks.append(nt(group, jnp.concatenate([big, small], axis=1).astype(BF16)))
    grad_up[...] = 2.0 * nn(weighted_t[...], ups[...])
    task = 2.0 * jnp.concatenate(tasks, axis=1)
    inner = jnp.sum(prob * task, axis=0, keepdims=True)
    plain = prob * (task - inner) + 50.0 * share * (logp + ent)
    plain_ref[...] = plain
    kinds = experts // 2 + 1
    for kind in range(kinds):
        value = plain if kind == 0 else share * pltpu.roll(prob, experts - kind, 0)
        big, small = split(value)
        at = pl.ds(ranks + 2 * kind * experts, 2 * experts)
        left_t[at, :] = jnp.concatenate([big, small], axis=0).astype(BF16)
    load = jnp.sum(share, axis=1, keepdims=True)
    entropy = jnp.sum(alive * ent, axis=1, keepdims=True)
    lane = lax.broadcasted_iota(jnp.int32, (experts, LANES), 1)
    stats[...] = jnp.where(
        lane < LANES // 2, load, jnp.where(lane < LANES // 4 * 3, entropy, count.astype(F32))
    )
    used = ranks + 2 * kinds * experts
    pairs = width // (2 * LANES)
    depth = pairs.bit_length() - 1
    gate_rows = kinds * experts
    up_rows = ranks * up.shape[1] // (2 * pairs * LANES)
    per = ranks // up_rows
    for pair in range(pairs):
        kept_a, sent_a = spots(mine, pair, side, orders_a, depth)
        kept_b, sent_b = spots(mine, pair, side, orders_b, depth)
        piece = nn(left_t[:used, :], tok[:, pl.ds(pair * 2 * LANES, 2 * LANES)])
        one, two = piece[:, :LANES], piece[:, LANES:]
        gates = []
        for kind in range(kinds):
            at = ranks + 2 * kind * experts
            gates.append(piece[at : at + experts] + piece[at + experts : at + 2 * experts])
        gates = jnp.concatenate(gates, axis=0)
        keep_a[kept_a] = jnp.where(side == 0, one[:ranks], two[:ranks])
        send_a[sent_a] = jnp.where(side == 0, two[:ranks], one[:ranks])
        to = pl.ds(0, gate_rows)
        keep_b[kept_b, to] = jnp.where(side == 0, gates[:, :LANES], gates[:, LANES:])
        send_b[sent_b, to] = jnp.where(side == 0, gates[:, LANES:], gates[:, :LANES])
        keep_b[kept_b, pl.ds(gate_rows, experts)] = stats[...]
        send_b[sent_b, pl.ds(gate_rows, experts)] = stats[...]
        first, second = 2 * pair, 2 * pair + 1
        one = grad_up[pl.ds((first % per) * up_rows, up_rows), pl.ds(first // per * LANES, LANES)]
        two = grad_up[pl.ds((second % per) * up_rows, up_rows), pl.ds(second // per * LANES, LANES)]
        to = pl.ds(gate_rows + experts, up_rows)
        keep_b[kept_b, to] = jnp.where(side == 0, one, two)
        send_b[sent_b, to] = jnp.where(side == 0, two, one)
    frozen_copy.wait()


def in_vmem(*arrays):
    return [pltpu.with_memory_space_constraint(array, VMEM) for array in arrays]


def in_hbm(*arrays):
    return [pltpu.with_memory_space_constraint(array, HBM) for array in arrays]


def local_grads(where, ids, gate_t, down, up, tokens, upstream, frozen, orders_a, orders_b):
    rows, width = tokens.shape
    outs = upstream.shape[1]
    experts, ranks = gate_t.shape[0], down.shape[1]
    pairs = width // (2 * LANES)
    kinds = experts // 2 + 1
    rows_b = (kinds + 1) * experts + ranks * outs // (2 * pairs * LANES)
    return pl.pallas_call(
        functools.partial(local_kernel, orders_a, orders_b),
        out_shape=[
            VMEM((pairs, ranks, LANES), F32),
            VMEM((pairs, ranks, LANES), F32),
            VMEM((pairs, rows_b, LANES), F32),
            VMEM((pairs, rows_b, LANES), F32),
            VMEM((rows, ranks), BF16),
            VMEM((rows, ranks), BF16),
            VMEM((experts, rows), F32),
            VMEM((experts, rows), F32),
            VMEM((width, 2 * ranks), BF16),
            VMEM((rows, outs), BF16),
            VMEM((rows, width), BF16),
            VMEM((ranks, outs), BF16),
            VMEM((width, outs), BF16),
        ],
        in_specs=[pl.BlockSpec(memory_space=SMEM)] + [pl.BlockSpec(memory_space=HBM)] * 7,
        out_specs=[pl.BlockSpec(memory_space=VMEM)] * 13,
        scratch_shapes=[
            VMEM(ids.shape, jnp.int32),
            VMEM((experts, width), BF16),
            VMEM((width, ranks), BF16),
            VMEM((rows, 2 * ranks), F32),
            VMEM((rows, ranks), F32),
            VMEM((2 * ranks, rows), BF16),
            VMEM((ranks, rows), BF16),
            VMEM((ranks, outs), F32),
            VMEM((experts, LANES), F32),
            pltpu.SemaphoreType.DMA((5,)),
            pltpu.SemaphoreType.DMA((TILES,)),
            pltpu.SemaphoreType.DMA((TILES,)),
        ],
        compiler_params=pltpu.CompilerParams(vmem_limit_bytes=20 * MIB),
        cost_estimate=pl.CostEstimate(
            flops=2 * rows * width * 512, bytes_accessed=2 * rows * (width + outs), transcendentals=0
        ),
        name="local_grads",
    )(where, *in_hbm(ids, gate_t, down, up, tokens, upstream, frozen))


def project_kernel(begin, tok, weighted_ref, frozen, up_ref, *rest):
    out_ref, out, out_sem = rest[-3:]
    parts, _, cols = out.shape

    def out_copy(c):
        target = out_ref.at[:, pl.ds((begin + c) * cols, cols)]
        return pltpu.make_async_copy(out.at[c], target, out_sem.at[c])

    for c in range(parts):
        lanes = pl.ds((begin + c) * cols, cols)
        base = nn(tok[...], frozen[:, lanes])
        out[c] = (base + 2.0 * nn(weighted_ref[...], up_ref[:, lanes])).astype(BF16)
        out_copy(c).start()
    for c in range(parts):
        out_copy(c).wait()


def project(tokens, weighted, frozen, up, begin, parts, past):
    rows, width = tokens.shape
    outs, ranks = frozen.shape[1], up.shape[0]
    cols = outs // TILES
    hbm = pl.BlockSpec(memory_space=HBM)
    vmem = pl.BlockSpec(memory_space=VMEM)
    return pl.pallas_call(
        functools.partial(project_kernel, begin),
        out_shape=HBM((rows, outs), BF16),
        in_specs=[vmem] * 4 + [hbm] * len(past),
        out_specs=hbm,
        input_output_aliases={4: 0} if past else {},
        scratch_shapes=[
            VMEM((parts, rows, cols), BF16),
            pltpu.SemaphoreType.DMA((parts,)),
        ],
        compiler_params=pltpu.CompilerParams(vmem_limit_bytes=8 * MIB),
        cost_estimate=pl.CostEstimate(
            flops=2 * rows * cols * parts * (width + ranks),
            bytes_accessed=2 * (rows * width + width * cols * parts + rows * cols * parts),
            transcendentals=0,
        ),
        name="project",
    )(*in_vmem(tokens, weighted, frozen, up), *in_hbm(*past))


def owner_kernel(experts, keep_a, keep_b, recv, own_ref, stats_ref):
    ranks = keep_a.shape[1]
    own_ref[0, :ranks] = keep_a[0] + recv[0, :ranks]
    block = keep_b[0] + recv[0, ranks:]
    kinds = experts // 2 + 1
    at = kinds * experts
    stats = block[at : at + experts]
    stats_ref[...] = stats
    mine = jnp.broadcast_to(stats[:, :1], (experts, LANES))
    total = jnp.zeros((experts, LANES), F32)
    for step in range(1, kinds):
        both = block[step * experts : (step + 1) * experts]
        total = total + both * (mine - pltpu.roll(mine, experts - step, 0))
        if 2 * step != experts:
            total = total + pltpu.roll(both, step, 0) * (mine - pltpu.roll(mine, step, 0))
    scale = 2.0 * experts * 100.0 / stats[:, LANES - 1 :]
    own_ref[0, ranks : ranks + experts] = block[:experts] + scale * total
    own_ref[0, ranks + experts :] = block[at + experts :]


def owner_rows(keep_a, keep_b, recv, experts):
    kinds = experts // 2 + 1
    rows = recv.shape[1] - kinds * experts
    return pl.pallas_call(
        functools.partial(owner_kernel, experts),
        out_shape=[
            jax.ShapeDtypeStruct((1, rows, LANES), F32),
            jax.ShapeDtypeStruct((experts, LANES), F32),
        ],
        compiler_params=pltpu.CompilerParams(vmem_limit_bytes=2 * MIB),
        name="owner_rows",
    )(keep_a, keep_b, recv)


def input_kernel(experts, begin, first, *refs):
    if first:
        masked, lowgrad_ref, plain_ref, share_ref, stats_ref, frozen, wide_ref = refs[:7]
        out_ref, left = refs[7:9]
    else:
        masked, left, frozen, wide_ref = refs[:4]
        out_ref = refs[5]
    out, out_sem = refs[-2:]
    parts, _, cols = out.shape

    def out_copy(c):
        target = out_ref.at[:, pl.ds((begin + c) * cols, cols)]
        return pltpu.make_async_copy(out.at[c], target, out_sem.at[c])

    if first:
        rows, ranks = lowgrad_ref.shape
        weight = stats_ref[:, :1]
        scale = 2.0 * experts * 100.0 / stats_ref[:, LANES - 1 :]
        share = share_ref[...]
        inner = jnp.sum(share * weight, axis=0, keepdims=True)
        value = plain_ref[...] + scale * share * (weight - inner)
        big, small = split(value)
        filler = jnp.zeros((ranks - 2 * experts, rows), F32)
        left[:, :ranks] = lowgrad_ref[...]
        left[:, ranks:] = jnp.concatenate([big, small, filler], axis=0).T.astype(BF16)
    for c in range(parts):
        part = pl.ds((begin + c) * cols, cols)
        out[c] = (nt(masked[...], frozen[part, :]) + nt(left[...], wide_ref[part, :])).astype(BF16)
        out_copy(c).start()
    for c in range(parts):
        out_copy(c).wait()


def input_grads(masked, lefts, frozen, wide, experts, begin, parts, past):
    rows, outs = masked.shape
    width, ranks = frozen.shape[0], wide.shape[1] // 2
    cols = 4 * LANES
    first = not past
    hbm = pl.BlockSpec(memory_space=HBM)
    vmem = pl.BlockSpec(memory_space=VMEM)
    out = HBM((rows, width), BF16)
    return pl.pallas_call(
        functools.partial(input_kernel, experts, begin, first),
        out_shape=[out, VMEM((rows, 2 * ranks), BF16)] if first else out,
        in_specs=[vmem] * (3 + len(lefts)) + [hbm] * len(past),
        out_specs=[hbm, vmem] if first else hbm,
        input_output_aliases={} if first else {4: 0},
        scratch_shapes=[
            VMEM((parts, rows, cols), BF16),
            pltpu.SemaphoreType.DMA((parts,)),
        ],
        compiler_params=pltpu.CompilerParams(vmem_limit_bytes=14 * MIB),
        cost_estimate=pl.CostEstimate(
            flops=2 * rows * cols * parts * (outs + 2 * ranks),
            bytes_accessed=2 * (rows + outs) * cols * parts + 2 * rows * outs,
            transcendentals=0,
        ),
        name="input_grads",
    )(*in_vmem(masked, *lefts, frozen, wide), *in_hbm(*past))


def clip_kernel(orders_a, orders_b, experts, limit, where_ref, own_a, other_a, own_b, other_b, stat_own, stat_other, down_ref, up_ref, gate_ref, load_ref):
    mine, side = where_ref[0], where_ref[1]
    pairs, ranks = own_a.shape[0], own_a.shape[1]
    depth = pairs.bit_length() - 1
    up_rows = own_b.shape[1] - experts
    per = ranks // up_rows

    def fold(block):
        square = block * block
        return jnp.sum(square.reshape(block.shape[0] // 8, 8, LANES), axis=0)

    def measure(pair, sums):
        kept_a, sent_a = spots(mine, pair, side, orders_a, depth)
        kept_b, sent_b = spots(mine, pair, side, orders_b, depth)
        first = sums[0] + fold(own_a[kept_a]) + fold(own_b[kept_b])
        second = sums[1] + fold(other_a[sent_a]) + fold(other_b[sent_b])
        return first, second

    zero = jnp.zeros((8, LANES), F32)
    sums = lax.fori_loop(0, pairs, measure, (zero, zero), unroll=4)
    total = jnp.sum(sums[0] + sums[1], axis=(0, 1), keepdims=True)
    factor = jnp.minimum(1.0, limit / jnp.sqrt(total))

    def emit(block_a, block_b, at):
        down_ref[pl.ds(pl.multiple_of(at * LANES, LANES), LANES), :] = (block_a * factor).T
        lanes = pl.ds(pl.multiple_of(at * LANES, LANES), LANES)
        gate_ref[:, lanes] = block_b[:experts] * factor
        rows = pl.ds(pl.multiple_of(at % per * up_rows, up_rows), up_rows)
        lanes = pl.ds(pl.multiple_of(at // per * LANES, LANES), LANES)
        up_ref[rows, lanes] = block_b[experts:] * factor

    def write(pair, carry):
        kept_a, sent_a = spots(mine, pair, side, orders_a, depth)
        kept_b, sent_b = spots(mine, pair, side, orders_b, depth)
        emit(own_a[kept_a], own_b[kept_b], 2 * pair + side)
        emit(other_a[sent_a], other_b[sent_b], 2 * pair + 1 - side)
        return carry

    lax.fori_loop(0, pairs, write, 0, unroll=4)
    stats = jnp.where(side == 0, stat_own[...], stat_other[...])
    stats = stats / stats[:, LANES - 1 :]
    row = lax.broadcasted_iota(jnp.int32, stats.shape, 0)
    lane = lax.broadcasted_iota(jnp.int32, stats.shape, 1)
    load = jnp.sum(jnp.where(row == lane, stats, 0.0), axis=0, keepdims=True)
    load_ref[...] = jnp.where(lane < LANES // 2, load, stats)


def clip_write(where, own_a, other_a, own_b, other_b, stat_own, stat_other, outs, experts, orders_a, orders_b):
    pairs, ranks = own_a.shape[0], own_a.shape[1]
    width = 2 * pairs * LANES
    limit = math.sqrt(width * ranks + ranks * outs + width * experts)
    vmem = pl.BlockSpec(memory_space=VMEM)
    return pl.pallas_call(
        functools.partial(clip_kernel, orders_a, orders_b, experts, limit),
        out_shape=[
            jax.ShapeDtypeStruct((width, ranks), F32),
            jax.ShapeDtypeStruct((ranks, outs), F32),
            jax.ShapeDtypeStruct((experts, width), F32),
            jax.ShapeDtypeStruct((experts, LANES), F32),
        ],
        in_specs=[pl.BlockSpec(memory_space=SMEM)] + [vmem] * 6,
        out_specs=[vmem] * 4,
        compiler_params=pltpu.CompilerParams(vmem_limit_bytes=24 * MIB),
        name="clip_write",
    )(where, own_a, other_a, own_b, other_b, stat_own, stat_other)


def swap(array, masks):
    size = lax.axis_size("dp")
    return lax.ppermute(array, "dp", [(i, i ^ masks[i & 1]) for i in range(size)])


def halve(keep, recv):
    half = keep.shape[0] // 2
    send = keep[half:] + recv[half:]
    return keep[:half] + recv[:half], send


def on_device(token_ids, tokens, frozen, down, up, gate, upstream):
    experts = gate.shape[1]
    outs = frozen.shape[1]
    rows = tokens.shape[0]
    size = lax.axis_size("dp")
    bits = size.bit_length() - 2
    depth = (tokens.shape[1] // (2 * LANES)).bit_length() - 1
    rest = tuple(range(2, bits))
    orders_a = ((0, 1) + rest, (1, 0) + rest)
    orders_b = ((2, 0, 1) + rest[1:], (2, 1, 0) + rest[1:])
    me = lax.axis_index("dp")
    where = jnp.stack([me >> 1, me & 1]).astype(jnp.int32)
    ids = token_ids.reshape(rows // LANES, LANES)
    masks_a = [(2 << orders_a[0][s], 2 << orders_a[1][s]) for s in range(bits)]
    masks_b = [(2 << orders_b[0][s], 2 << orders_b[1][s]) for s in range(bits)]

    keep_a, send_a, keep_b, send_b, weighted, low_grad, plain, share, wide, masked, tok, up_v, near = (
        local_grads(where, ids, gate.T, down, up, tokens, upstream, frozen, orders_a, orders_b)
    )
    split_at = keep_a.shape[1]
    recv_b = swap(send_b, (1, 1))
    recv_a = swap(send_a, (1, 1))
    filled = ()
    for step in range(bits):
        if step < depth:
            keep_b, send_b = halve(keep_b, recv_b)
            keep_a, send_a = halve(keep_a, recv_a)
        else:
            keep_b = send_b = keep_b + recv_b
            keep_a = send_a = keep_a + recv_a
        if step < 2:
            weighted, send_a, send_b, filled = lax.optimization_barrier(
                (weighted, send_a, send_b, filled)
            )
            filled = (project(tok, weighted, near, up_v, 2 * step, 2, filled),)
        if masks_a[step] == masks_b[step]:
            recv = swap(jnp.concatenate([send_a, send_b], axis=1), masks_a[step])
            recv_a, recv_b = recv[:, :split_at], recv[:, split_at:]
        else:
            recv_b = swap(send_b, masks_b[step])
            recv_a = swap(send_a, masks_a[step])
        if step < 2:
            recv_a, recv_b, filled = lax.optimization_barrier((recv_a, recv_b, filled))
    projected = filled[0]
    own, stats = owner_rows(keep_a, keep_b, recv, experts)
    own_a, own_b = own[:, :split_at], own[:, split_at:]
    lefts = (low_grad, plain, share, stats)
    filled = ()
    turns = tuple(reversed(range(depth)))
    chunk = tokens.shape[1] // (4 * LANES * depth)
    for turn, step in enumerate(turns):
        together = turn == 0 and masks_a[step] == masks_b[step]
        if together:
            lefts, own, filled = lax.optimization_barrier((lefts, own, filled))
        else:
            lefts, own_a, own_b, filled = lax.optimization_barrier((lefts, own_a, own_b, filled))
        made = input_grads(masked, lefts, near, wide, experts, turn * chunk, chunk, filled)
        if turn == 0:
            filled, lefts = (made[0],), (made[1],)
        else:
            filled = (made,)
        if together:
            recv = swap(own, masks_a[step])
            recv, filled = lax.optimization_barrier((recv, filled))
            recv_a, recv_b = recv[:, :split_at], recv[:, split_at:]
        else:
            recv_b = swap(own_b, masks_b[step])
            recv_a = swap(own_a, masks_a[step])
            recv_a, recv_b, filled = lax.optimization_barrier((recv_a, recv_b, filled))
        own_b = jnp.concatenate([own_b, recv_b], axis=0)
        own_a = jnp.concatenate([own_a, recv_a], axis=0)
    input_grad = filled[0]
    stat_other = swap(stats, (1, 1))
    other_b = swap(own_b, (1, 1))
    other_a = swap(own_a, (1, 1))
    clipped_down, clipped_up, clipped_gate, summary = clip_write(
        where, own_a, other_a, own_b, other_b, stats, stat_other, outs, experts, orders_a, orders_b
    )
    return (
        projected,
        input_grad,
        clipped_down,
        clipped_up,
        clipped_gate.T,
        summary[0, :experts],
        summary[0, LANES // 2],
    )


def solution(mesh):
    placed = (P("dp"), P("dp", None), P(), P(), P(), P(), P("dp", None))
    return jax.shard_map(
        on_device,
        mesh=mesh,
        in_specs=placed,
        out_specs=(P("dp", None), P("dp", None), P(), P(), P(), P(), P()),
        check_vma=False,
    )
```

time: 126 us -> 93.1 us (0.74)
  Pallas kernels: 56 us -> 44 us
  starting transfers between devices: 31.5 us -> 23.9 us
  waiting for transfers between devices: 26.9 us -> 22.3 us
  local copies, waits for them, and re-layouts: 5.64 us -> 1.21 us
  other arithmetic: 4.38 us -> 0.6 us
    pallas_call x3 -> x7, Pallas kernels: 49 us -> 40.5 us  [the longest x4 15.7 us: input_grads(): pl.pallas_call(functools.partial(input_kernel, experts, begin, first), ou...]
    ppermute x21 -> x19, starting transfers between devices: 31.5 us -> 23.9 us  [swap(): lax.ppermute(array, 'dp', [(i, i ^ masks[i & 1]) for i in range(size)])]
    ppermute x21 -> x19, waiting for transfers between devices: 26.9 us -> 22.3 us  [swap(): lax.ppermute(array, 'dp', [(i, i ^ masks[i & 1]) for i in range(size)])]
    unnamed x23 -> x2, local copies, waits for them, and re-layouts: 3.13 us -> 0.05 us
    pallas_call x1, Pallas kernels: 5.5 us -> 3.47 us  [clip_write(): pl.pallas_call(functools.partial(clip_kernel, orders_a, orders_b, experts...]
    slice x2 -> x5, local copies, waits for them, and re-layouts: 2.47 us -> 0.6 us  [the longest x1 0.58 us: on_device(): summary[0, LANES // 2]]
    concatenate x6 -> x7, other arithmetic: 1.56 us -> 0.1 us  [the longest x3 0.07 us: on_device(): own_a = jnp.concatenate([own_a, recv_a], axis=0)]
    pallas_call x1, Pallas kernels: 1.49 us -> 0.09 us  [owner_rows(): pl.pallas_call(functools.partial(owner_kernel, experts), out_shape=[jax.S...]
  transfers between devices with their start and end apart: 21 -> 19, of which waited for: 11 -> 11; matrix products, arithmetic and copies ran while one was open for 4% -> 0% of each run, Pallas kernels for 27% -> 29%
where the time goes in v2:
time: 93.1 us; the launch traced here: 92.9 us
  Pallas kernels  44 us (47%)
  starting transfers between devices  23.9 us (26%)
  waiting for transfers between devices  22.3 us (24%)
  local copies, waits for them, and re-layouts  1.21 us (1%)
    ppermute x19, starting transfers between devices, swap(): lax.ppermute(array, 'dp', [(i, i ^ masks[i & 1]) for i in range(size)])  23.9 us
    ppermute x19, waiting for transfers between devices, swap(): lax.ppermute(array, 'dp', [(i, i ^ masks[i & 1]) for i in range(size)])  22.3 us
    pallas_call x4, Pallas kernels, input_grads(): pl.pallas_call(functools.partial(input_kernel, experts, begin, first), ou...  15.7 us
    pallas_call x1, Pallas kernels, local_grads(): pl.pallas_call(functools.partial(local_kernel, orders_a, orders_b), out_s...  13.3 us
    pallas_call x2, Pallas kernels, project(): pl.pallas_call(functools.partial(project_kernel, begin), out_shape=HBM((r...  11.5 us
    pallas_call x1, Pallas kernels, clip_write(): pl.pallas_call(functools.partial(clip_kernel, orders_a, orders_b, experts...  3.47 us
  transfers between devices with their start and end apart: 19, of which 11 were waited for; matrix products, arithmetic and copies ran while one was open for 0% of the time, Pallas kernels for 29%

profile of v2, /device:TPU:0, one launch (start us, length us, event | category | flops | bytes accessed | tf_op | source)
XLA Modules:
  0.0 92.9 jit_solution(16016523979701724036)
XLA Ops:
  0.7 13.3 %local_grads.1 = (f32[16,128,128]{2,1,0:T(8,128)S(1)}, f32[16,128,128]{2,1,0:T(8,128)S(1)}, f32[16,80,128]{2,1,0:T(8,128)S(1)}, f32[16,80,128]{2,1,0:T(8,128)S(1...) custom-call(s32[2]{0:T(128)S(1)} %pad_add_fusion.where_ref, ...), custom_call_target="tpu_custom_call" | custom-call | flops 4294967296 | bytes 10485760 | tf_op jit(solution)/shard_map/local_grads/pallas_call | solution.py:199
  14.0 0.6 collective-permute-start
  14.7 3.1 %collective-permute-done.1 = f32[16,80,128]{2,1,0:T(8,128)S(1)} collective-permute-done((f32[16,80,128]{2,1,0:T(8,128)S(1)}, f32[16,80,128]{2,1,0:T(8,128)S(1)}, u32[]{:S(2)}, u32[]{:S(2)}) %collective-permute-start.1) | collective-permute-done | bytes 655392 | tf_op jit(solution)/shard_map/ppermute | solution.py:447
  18.1 2.9 %collective-permute-start.2 = (f32[8,128,128]{2,1,0:T(8,128)S(1)}, f32[8,128,128]{2,1,0:T(8,128)S(1)}, u32[]{:S(2)}, u32[]{:S(2)}) collective-permute-start(f32[8,128,128]{2,1,0:T(8,128)S(1)} %get-tuple-element.75), channel_id=1, source_target_pairs={{0,2},{1,5},{2,0},{3,7},{4,6},{5,1},{6,4},{7,3},{8,10},{9,13},{10,... | collective-permute-start | bytes 1572872 | tf_op jit(solution)/shard_map/ppermute | solution.py:447
  21.0 1.6 %collective-permute-start.3 = (f32[8,80,128]{2,1,0:T(8,128)S(1)}, f32[8,80,128]{2,1,0:T(8,128)S(1)}, u32[]{:S(2)}, u32[]{:S(2)}) collective-permute-start(f32[8,80,128]{2,1,0:T(8,128)S(1)} %get-tuple-element.76), channel_id=1, source_target_pairs={{0,8},{1,9},{2,10},{3,11},{4,12},{5,13},{6,14},{7,15},{8,0},{9,1},... | collective-permute-start | bytes 983048 | tf_op jit(solution)/shard_map/ppermute | solution.py:447
  22.5 5.7 %project.2.rest_0_ = bf16[1024,1024]{1,0:T(8,128)(2,1)} custom-call(bf16[1024,4096]{1,0:T(8,128)(2,1)S(1)} %get-tuple-element.77.tok, bf16[1024,128]{1,0:T(8,128)(2,1)S(1)} %get-tuple-element.85.weighted_ref, bf16[4096,1024]{1,0:T(8,128)(2,1)S(1)} %get-tuple-element.78.frozen.refs_5_.refs_2_, bf16[128,1024]{1,0:T(8,128)(2,1)S(1)} %get-tuple-element.79.up_ref), custom_call_target="tpu_custom_call" | custom-call | flops 4429185024 | bytes 13631488 | tf_op jit(solution)/shard_map/project/pallas_call | solution.py:263
  28.3 2.2 %collective-permute-done.3 = f32[8,80,128]{2,1,0:T(8,128)S(1)} collective-permute-done((f32[8,80,128]{2,1,0:T(8,128)S(1)}, f32[8,80,128]{2,1,0:T(8,128)S(1)}, u32[]{:S(2)}, u32[]{:S(2)}) %collective-permute-start.3) | collective-permute-done | bytes 327712 | tf_op jit(solution)/shard_map/ppermute | solution.py:447
  30.6 0.4 collective-permute-start.4
  31.0 1.6 %collective-permute-start.5 = (f32[4,80,128]{2,1,0:T(8,128)S(1)}, f32[4,80,128]{2,1,0:T(8,128)S(1)}, u32[]{:S(2)}, u32[]{:S(2)}) collective-permute-start(f32[4,80,128]{2,1,0:T(8,128)S(1)} %get-tuple-element.84), channel_id=1, source_target_pairs={{0,2},{1,5},{2,0},{3,7},{4,6},{5,1},{6,4},{7,3},{8,10},{9,13},{10,... | collective-permute-start | bytes 491528 | tf_op jit(solution)/shard_map/ppermute | solution.py:447
  32.7 5.7 %project.3 = bf16[1024,1024]{1,0:T(8,128)(2,1)} custom-call(bf16[1024,4096]{1,0:T(8,128)(2,1)S(1)} %get-tuple-element.77.tok, bf16[1024,128]{1,0:T(8,128)(2,1)S(1)} %get-tuple-element.85.weighted_ref, bf16[4096,1024]{1,0:T(8,128)(2,1)S(1)} %get-tuple-element.78.frozen.refs_5_.refs_2_, ...), custom_call_target="tpu_custom_call", output_to_operand_aliasing={{}: (4, {})} | custom-call | flops 4429185024 | bytes 13631488 | tf_op jit(solution)/shard_map/project/pallas_call | solution.py:263
  38.6 0.8 collective-permute-start.7
  39.4 2.5 %collective-permute-start.6 = (f32[2,128,128]{2,1,0:T(8,128)S(1)}, f32[2,128,128]{2,1,0:T(8,128)S(1)}, u32[]{:S(2)}, u32[]{:S(2)}) collective-permute-start(f32[2,128,128]{2,1,0:T(8,128)S(1)} %get-tuple-element.140), channel_id=1, source_target_pairs={{0,8},{1,9},{2,10},{3,11},{4,12},{5,13},{6,14},{7,15},{8,0},{9,1},... | collective-permute-start | bytes 393224 | tf_op jit(solution)/shard_map/ppermute | solution.py:447
  41.9 1.2 %collective-permute-done.7 = f32[2,80,128]{2,1,0:T(8,128)S(1)} collective-permute-done((f32[2,80,128]{2,1,0:T(8,128)S(1)}, f32[2,80,128]{2,1,0:T(8,128)S(1)}, u32[]{:S(2)}, u32[]{:S(2)}) %collective-permute-start.7) | collective-permute-done | bytes 81952 | tf_op jit(solution)/shard_map/ppermute | solution.py:447
  43.1 1.8 %collective-permute-done.6 = f32[2,128,128]{2,1,0:T(8,128)S(1)} collective-permute-done((f32[2,128,128]{2,1,0:T(8,128)S(1)}, f32[2,128,128]{2,1,0:T(8,128)S(1)}, u32[]{:S(2)}, u32[]{:S(2)}) %collective-permute-start.6) | collective-permute-done | bytes 131104 | tf_op jit(solution)/shard_map/ppermute | solution.py:447
  44.9 3.1 %collective-permute-start.8 = (f32[1,208,128]{2,1,0:T(8,128)S(1)}, f32[1,208,128]{2,1,0:T(8,128)S(1)}, u32[]{:S(2)}, u32[]{:S(2)}) collective-permute-start(f32[1,208,128]{2,1,0:T(8,128)S(1)} %pad_maximum_fusion.4), channel_id=1, source_target_pairs={{0,16},{1,17},{2,18},{3,19},{4,20},{5,21},{6,22},{7,23},{8,24},{9,... | collective-permute-start | bytes 319496 | tf_op jit(solution)/shard_map/ppermute | solution.py:447
  48.0 2.7 %collective-permute-done.8.recv = f32[1,208,128]{2,1,0:T(8,128)S(1)} collective-permute-done((f32[1,208,128]{2,1,0:T(8,128)S(1)}, f32[1,208,128]{2,1,0:T(8,128)S(1)}, u32[]{:S(2)}, u32[]{:S(2)}) %collective-permute-start.8) | collective-permute-done | bytes 106528 | tf_op jit(solution)/shard_map/ppermute | solution.py:447
  50.7 3.0 %collective-permute-start.9 = (f32[1,168,128]{2,1,0:T(8,128)S(1)}, f32[1,168,128]{2,1,0:T(8,128)S(1)}, u32[]{:S(2)}, u32[]{:S(2)}) collective-permute-start(f32[1,168,128]{2,1,0:T(8,128)S(1)} %get-tuple-element.102), channel_id=1, source_target_pairs={{0,16},{1,17},{2,18},{3,19},{4,20},{5,21},{6,22},{7,23},{8,24},{9,... | collective-permute-start | bytes 258056 | tf_op jit(solution)/shard_map/ppermute | solution.py:447
  53.8 4.0 %input_grads.4 = (bf16[1024,4096]{1,0:T(8,128)(2,1)}, bf16[1024,256]{1,0:T(8,128)(2,1)S(1)}) custom-call(bf16[1024,1024]{1,0:T(8,128)(2,1)S(1)} %get-tuple-element.88.refs_0_, bf16[1024,128]{1,0:T(8,128)(2,1)S(1)} %get-tuple-element.96.refs_1_, f32[8,1024]{1,0:T(8,128)S(1)} %get-tuple-element.97.refs_2_, f32[8,1024]{1,0:T(8,128)S(1)} %get-tuple-element.98.refs_3_, ...), custom_call_target="tpu_custom_call" | custom-call | flops 2684354560 | bytes 6291456 | tf_op jit(solution)/shard_map/input_grads/pallas_call | solution.py:358
  57.9 4.1 %collective-permute-start.10 = (f32[2,128,128]{2,1,0:T(8,128)S(1)}, f32[2,128,128]{2,1,0:T(8,128)S(1)}, u32[]{:S(2)}, u32[]{:S(2)}) collective-permute-start(f32[2,128,128]{2,1,0:T(8,128)S(1)} %pad_maximum_fusion.3), channel_id=1, source_target_pairs={{0,8},{1,9},{2,10},{3,11},{4,12},{5,13},{6,14},{7,15},{8,0},{9,1},... | collective-permute-start | bytes 393224 | tf_op jit(solution)/shard_map/ppermute | solution.py:447
  62.0 1.0 %collective-permute-start.11 = (f32[2,40,128]{2,1,0:T(8,128)S(1)}, f32[2,40,128]{2,1,0:T(8,128)S(1)}, u32[]{:S(2)}, u32[]{:S(2)}) collective-permute-start(f32[2,40,128]{2,1,0:T(8,128)S(1)} %pad_maximum_fusion.6), channel_id=1, source_target_pairs={{0,4},{1,3},{2,6},{3,1},{4,0},{5,7},{6,2},{7,5},{8,12},{9,11},{10,... | collective-permute-start | bytes 122888 | tf_op jit(solution)/shard_map/ppermute | solution.py:447
  63.0 3.9 %input_grads.5.refs_4_ = bf16[1024,4096]{1,0:T(8,128)(2,1)} custom-call(bf16[1024,1024]{1,0:T(8,128)(2,1)S(1)} %get-tuple-element.88.refs_0_, bf16[1024,256]{1,0:T(8,128)(2,1)S(1)} %get-tuple-element.122.refs_1_, bf16[4096,1024]{1,0:T(8,128)(2,1)S(1)} %get-tuple-element.78.frozen.refs_5_.refs_2_, ...), custom_call_target="tpu_custom_call", output_to_operand_aliasing={{}: (4, {})} | custom-call | flops 2684354560 | bytes 6291456 | tf_op jit(solution)/shard_map/input_grads/pallas_call | solution.py:358
  66.9 1.1 %collective-permute-start.12 = (f32[4,128,128]{2,1,0:T(8,128)S(1)}, f32[4,128,128]{2,1,0:T(8,128)S(1)}, u32[]{:S(2)}, u32[]{:S(2)}) collective-permute-start(f32[4,128,128]{2,1,0:T(8,128)S(1)} %pad_maximum_fusion.1), channel_id=1, source_target_pairs={{0,4},{1,3},{2,6},{3,1},{4,0},{5,7},{6,2},{7,5},{8,12},{9,11},{10,... | collective-permute-start | bytes 786440 | tf_op jit(solution)/shard_map/ppermute | solution.py:447
  68.3 3.9 %input_grads.6.refs_4_ = bf16[1024,4096]{1,0:T(8,128)(2,1)} custom-call(bf16[1024,1024]{1,0:T(8,128)(2,1)S(1)} %get-tuple-element.88.refs_0_, bf16[1024,256]{1,0:T(8,128)(2,1)S(1)} %get-tuple-element.122.refs_1_, bf16[4096,1024]{1,0:T(8,128)(2,1)S(1)} %get-tuple-element.78.frozen.refs_5_.refs_2_, ...), custom_call_target="tpu_custom_call", output_to_operand_aliasing={{}: (4, {})} | custom-call | flops 2684354560 | bytes 6291456 | tf_op jit(solution)/shard_map/input_grads/pallas_call | solution.py:358
  72.5 3.3 %collective-permute-done.12 = f32[4,128,128]{2,1,0:T(8,128)S(1)} collective-permute-done((f32[4,128,128]{2,1,0:T(8,128)S(1)}, f32[4,128,128]{2,1,0:T(8,128)S(1)}, u32[]{:S(2)}, u32[]{:S(2)}) %collective-permute-start.12) | collective-permute-done | bytes 262176 | tf_op jit(solution)/shard_map/ppermute | solution.py:447
  76.0 3.9 %input_grads.7 = bf16[1024,4096]{1,0:T(8,128)(2,1)} custom-call(bf16[1024,1024]{1,0:T(8,128)(2,1)S(1)} %get-tuple-element.88.refs_0_, bf16[1024,256]{1,0:T(8,128)(2,1)S(1)} %get-tuple-element.122.refs_1_, bf16[4096,1024]{1,0:T(8,128)(2,1)S(1)} %get-tuple-element.78.frozen.refs_5_.refs_2_, ...), custom_call_target="tpu_custom_call", output_to_operand_aliasing={{}: (4, {})} | custom-call | flops 2684354560 | bytes 6291456 | tf_op jit(solution)/shard_map/input_grads/pallas_call | solution.py:358
  80.0 1.4 %collective-permute-done.15 = f32[8,40,128]{2,1,0:T(8,128)S(1)} collective-permute-done((f32[8,40,128]{2,1,0:T(8,128)S(1)}, f32[8,40,128]{2,1,0:T(8,128)S(1)}, u32[]{:S(2)}, u32[]{:S(2)}) %collective-permute-start.15) | collective-permute-done | bytes 163872 | tf_op jit(solution)/shard_map/ppermute | solution.py:447
  81.3 3.8 %collective-permute-done.14 = f32[8,128,128]{2,1,0:T(8,128)S(1)} collective-permute-done((f32[8,128,128]{2,1,0:T(8,128)S(1)}, f32[8,128,128]{2,1,0:T(8,128)S(1)}, u32[]{:S(2)}, u32[]{:S(2)}) %collective-permute-start.14) | collective-permute-done | bytes 524320 | tf_op jit(solution)/shard_map/ppermute | solution.py:447
  85.3 0.6 collective-permute-start.17
  85.9 2.4 %collective-permute-done.18.stat_other = f32[8,128]{1,0:T(8,128)S(1)} collective-permute-done((f32[8,128]{1,0:T(8,128)S(1)}, f32[8,128]{1,0:T(8,128)S(1)}, u32[]{:S(2)}, u32[]{:S(2)}) %collective-permute-start.18) | collective-permute-done | bytes 4128 | tf_op jit(solution)/shard_map/ppermute | solution.py:447
  88.3 3.5 %clip_write.1 = (f32[4096,128]{1,0:T(8,128)}, f32[128,1024]{1,0:T(8,128)}, f32[8,4096]{1,0:T(8,128)}, f32[8,128]{1,0:T(8,128)S(1)}) custom-call(s32[2]{0:T(128)S(1)} %pad_add_fusion.where_ref, f32[16,128,128]{2,1,0:T(8,128)S(1)} %constant_dynamic-update-slice_fusion.own_a, f32[16,128,128]{2,1,0:T(8,128)S(1)} %collective-permute-done.16.other_a, ...), custom_call_target="tpu_custom_call" | custom-call | tf_op jit(solution)/shard_map/clip_write/pallas_call | solution.py:430
  91.8 0.6 slice.151
  92.4 0.5 slice_bitcast_fusion
  (41 shorter events, 1.9 us)
Async XLA Ops:
  14.0 3.9 %collective-permute-start = (f32[16,128,128]{2,1,0:T(8,128)S(1)}, f32[16,128,128]{2,1,0:T(8,128)S(1)}, u32[]{:S(2)}, u32[]{:S(2)}) collective-permute-start(f32[16,128,128]{2,1,0:T(8,128)S(1)} %get-tuple-element.71), channel_id=1, source_target_pairs={{0,1},{1,0},{2,3},{3,2},{4,5},{5,4},{6,7},{7,6},{8,9},{9,8},{10,11... | collective-permute-start | bytes 3145736 | tf_op jit(solution)/shard_map/ppermute | solution.py:447
  14.6 3.2 %collective-permute-start.1 = (f32[16,80,128]{2,1,0:T(8,128)S(1)}, f32[16,80,128]{2,1,0:T(8,128)S(1)}, u32[]{:S(2)}, u32[]{:S(2)}) collective-permute-start(f32[16,80,128]{2,1,0:T(8,128)S(1)} %get-tuple-element.73), channel_id=1, source_target_pairs={{0,1},{1,0},{2,3},{3,2},{4,5},{5,4},{6,7},{7,6},{8,9},{9,8},{10,11... | collective-permute-start | bytes 1966088 | tf_op jit(solution)/shard_map/ppermute | solution.py:447
  18.1 12.4 %collective-permute-start.2 = (f32[8,128,128]{2,1,0:T(8,128)S(1)}, f32[8,128,128]{2,1,0:T(8,128)S(1)}, u32[]{:S(2)}, u32[]{:S(2)}) collective-permute-start(f32[8,128,128]{2,1,0:T(8,128)S(1)} %get-tuple-element.75), channel_id=1, source_target_pairs={{0,2},{1,5},{2,0},{3,7},{4,6},{5,1},{6,4},{7,3},{8,10},{9,13},{10,... | collective-permute-start | bytes 1572872 | tf_op jit(solution)/shard_map/ppermute | solution.py:447
  21.0 9.5 %collective-permute-start.3 = (f32[8,80,128]{2,1,0:T(8,128)S(1)}, f32[8,80,128]{2,1,0:T(8,128)S(1)}, u32[]{:S(2)}, u32[]{:S(2)}) collective-permute-start(f32[8,80,128]{2,1,0:T(8,128)S(1)} %get-tuple-element.76), channel_id=1, source_target_pairs={{0,8},{1,9},{2,10},{3,11},{4,12},{5,13},{6,14},{7,15},{8,0},{9,1},... | collective-permute-start | bytes 983048 | tf_op jit(solution)/shard_map/ppermute | solution.py:447
  30.6 7.9 %collective-permute-start.4 = (f32[4,128,128]{2,1,0:T(8,128)S(1)}, f32[4,128,128]{2,1,0:T(8,128)S(1)}, u32[]{:S(2)}, u32[]{:S(2)}) collective-permute-start(f32[4,128,128]{2,1,0:T(8,128)S(1)} %get-tuple-element.83), channel_id=1, source_target_pairs={{0,4},{1,3},{2,6},{3,1},{4,0},{5,7},{6,2},{7,5},{8,12},{9,11},{10,... | collective-permute-start | bytes 786440 | tf_op jit(solution)/shard_map/ppermute | solution.py:447
  31.0 7.4 %collective-permute-start.5 = (f32[4,80,128]{2,1,0:T(8,128)S(1)}, f32[4,80,128]{2,1,0:T(8,128)S(1)}, u32[]{:S(2)}, u32[]{:S(2)}) collective-permute-start(f32[4,80,128]{2,1,0:T(8,128)S(1)} %get-tuple-element.84), channel_id=1, source_target_pairs={{0,2},{1,5},{2,0},{3,7},{4,6},{5,1},{6,4},{7,3},{8,10},{9,13},{10,... | collective-permute-start | bytes 491528 | tf_op jit(solution)/shard_map/ppermute | solution.py:447
  38.6 4.5 %collective-permute-start.7 = (f32[2,80,128]{2,1,0:T(8,128)S(1)}, f32[2,80,128]{2,1,0:T(8,128)S(1)}, u32[]{:S(2)}, u32[]{:S(2)}) collective-permute-start(f32[2,80,128]{2,1,0:T(8,128)S(1)} %get-tuple-element.142), channel_id=1, source_target_pairs={{0,4},{1,3},{2,6},{3,1},{4,0},{5,7},{6,2},{7,5},{8,12},{9,11},{10,... | collective-permute-start | bytes 245768 | tf_op jit(solution)/shard_map/ppermute | solution.py:447
  39.4 5.4 %collective-permute-start.6 = (f32[2,128,128]{2,1,0:T(8,128)S(1)}, f32[2,128,128]{2,1,0:T(8,128)S(1)}, u32[]{:S(2)}, u32[]{:S(2)}) collective-permute-start(f32[2,128,128]{2,1,0:T(8,128)S(1)} %get-tuple-element.140), channel_id=1, source_target_pairs={{0,8},{1,9},{2,10},{3,11},{4,12},{5,13},{6,14},{7,15},{8,0},{9,1},... | collective-permute-start | bytes 393224 | tf_op jit(solution)/shard_map/ppermute | solution.py:447
  44.9 5.8 %collective-permute-start.8 = (f32[1,208,128]{2,1,0:T(8,128)S(1)}, f32[1,208,128]{2,1,0:T(8,128)S(1)}, u32[]{:S(2)}, u32[]{:S(2)}) collective-permute-start(f32[1,208,128]{2,1,0:T(8,128)S(1)} %pad_maximum_fusion.4), channel_id=1, source_target_pairs={{0,16},{1,17},{2,18},{3,19},{4,20},{5,21},{6,22},{7,23},{8,24},{9,... | collective-permute-start | bytes 319496 | tf_op jit(solution)/shard_map/ppermute | solution.py:447
  50.7 7.1 %collective-permute-start.9 = (f32[1,168,128]{2,1,0:T(8,128)S(1)}, f32[1,168,128]{2,1,0:T(8,128)S(1)}, u32[]{:S(2)}, u32[]{:S(2)}) collective-permute-start(f32[1,168,128]{2,1,0:T(8,128)S(1)} %get-tuple-element.102), channel_id=1, source_target_pairs={{0,16},{1,17},{2,18},{3,19},{4,20},{5,21},{6,22},{7,23},{8,24},{9,... | collective-permute-start | bytes 258056 | tf_op jit(solution)/shard_map/ppermute | solution.py:447
  57.9 9.0 %collective-permute-start.10 = (f32[2,128,128]{2,1,0:T(8,128)S(1)}, f32[2,128,128]{2,1,0:T(8,128)S(1)}, u32[]{:S(2)}, u32[]{:S(2)}) collective-permute-start(f32[2,128,128]{2,1,0:T(8,128)S(1)} %pad_maximum_fusion.3), channel_id=1, source_target_pairs={{0,8},{1,9},{2,10},{3,11},{4,12},{5,13},{6,14},{7,15},{8,0},{9,1},... | collective-permute-start | bytes 393224 | tf_op jit(solution)/shard_map/ppermute | solution.py:447
  62.0 4.9 %collective-permute-start.11 = (f32[2,40,128]{2,1,0:T(8,128)S(1)}, f32[2,40,128]{2,1,0:T(8,128)S(1)}, u32[]{:S(2)}, u32[]{:S(2)}) collective-permute-start(f32[2,40,128]{2,1,0:T(8,128)S(1)} %pad_maximum_fusion.6), channel_id=1, source_target_pairs={{0,4},{1,3},{2,6},{3,1},{4,0},{5,7},{6,2},{7,5},{8,12},{9,11},{10,... | collective-permute-start | bytes 122888 | tf_op jit(solution)/shard_map/ppermute | solution.py:447
  66.9 8.9 %collective-permute-start.12 = (f32[4,128,128]{2,1,0:T(8,128)S(1)}, f32[4,128,128]{2,1,0:T(8,128)S(1)}, u32[]{:S(2)}, u32[]{:S(2)}) collective-permute-start(f32[4,128,128]{2,1,0:T(8,128)S(1)} %pad_maximum_fusion.1), channel_id=1, source_target_pairs={{0,4},{1,3},{2,6},{3,1},{4,0},{5,7},{6,2},{7,5},{8,12},{9,11},{10,... | collective-permute-start | bytes 786440 | tf_op jit(solution)/shard_map/ppermute | solution.py:447
  68.0 4.4 %collective-permute-start.13 = (f32[4,40,128]{2,1,0:T(8,128)S(1)}, f32[4,40,128]{2,1,0:T(8,128)S(1)}, u32[]{:S(2)}, u32[]{:S(2)}) collective-permute-start(f32[4,40,128]{2,1,0:T(8,128)S(1)} %pad_maximum_fusion.5), channel_id=1, source_target_pairs={{0,2},{1,5},{2,0},{3,7},{4,6},{5,1},{6,4},{7,3},{8,10},{9,13},{10,... | collective-permute-start | bytes 245768 | tf_op jit(solution)/shard_map/ppermute | solution.py:447
  75.9 9.2 %collective-permute-start.14 = (f32[8,128,128]{2,1,0:T(8,128)S(1)}, f32[8,128,128]{2,1,0:T(8,128)S(1)}, u32[]{:S(2)}, u32[]{:S(2)}) collective-permute-start(f32[8,128,128]{2,1,0:T(8,128)S(1)} %pad_maximum_fusion), channel_id=1, source_target_pairs={{0,2},{1,5},{2,0},{3,7},{4,6},{5,1},{6,4},{7,3},{8,10},{9,13},{10,... | collective-permute-start | bytes 1572872 | tf_op jit(solution)/shard_map/ppermute | solution.py:447
  75.9 5.4 %collective-permute-start.15 = (f32[8,40,128]{2,1,0:T(8,128)S(1)}, f32[8,40,128]{2,1,0:T(8,128)S(1)}, u32[]{:S(2)}, u32[]{:S(2)}) collective-permute-start(f32[8,40,128]{2,1,0:T(8,128)S(1)} %pad_maximum_fusion.2), channel_id=1, source_target_pairs={{0,8},{1,9},{2,10},{3,11},{4,12},{5,13},{6,14},{7,15},{8,0},{9,1},... | collective-permute-start | bytes 491528 | tf_op jit(solution)/shard_map/ppermute | solution.py:447
  85.1 3.2 %collective-permute-start.16 = (f32[16,128,128]{2,1,0:T(8,128)S(1)}, f32[16,128,128]{2,1,0:T(8,128)S(1)}, u32[]{:S(2)}, u32[]{:S(2)}) collective-permute-start(f32[16,128,128]{2,1,0:T(8,128)S(1)} %constant_dynamic-update-slice_fusion.own_a), channel_id=1, source_target_pairs={{0,1},{1,0},{2,3},{3,2},{4,5},{5,4},{6,7},{7,6},{8,9},{9,8},{10,11... | collective-permute-start | bytes 3145736 | tf_op jit(solution)/shard_map/ppermute | solution.py:447
  85.3 3.1 %collective-permute-start.17 = (f32[16,40,128]{2,1,0:T(8,128)S(1)}, f32[16,40,128]{2,1,0:T(8,128)S(1)}, u32[]{:S(2)}, u32[]{:S(2)}) collective-permute-start(f32[16,40,128]{2,1,0:T(8,128)S(1)} %constant_dynamic-update-slice_fusion.2.own_b), channel_id=1, source_target_pairs={{0,1},{1,0},{2,3},{3,2},{4,5},{5,4},{6,7},{7,6},{8,9},{9,8},{10,11... | collective-permute-start | bytes 983048 | tf_op jit(solution)/shard_map/ppermute | solution.py:447
  85.8 2.5 %collective-permute-start.18 = (f32[8,128]{1,0:T(8,128)S(1)}, f32[8,128]{1,0:T(8,128)S(1)}, u32[]{:S(2)}, u32[]{:S(2)}) collective-permute-start(f32[8,128]{1,0:T(8,128)S(1)} %get-tuple-element.99.refs_4_.stat_own), channel_id=1, source_target_pairs={{0,1},{1,0},{2,3},{3,2},{4,5},{5,4},{6,7},{7,6},{8,9},{9,8},{10,11... | collective-permute-start | bytes 12296 | tf_op jit(solution)/shard_map/ppermute | solution.py:447

commit v3 on v2

--- a/solution.py
+++ b/solution.py
@@ -8,10 +8,13 @@
 from jax.experimental.pallas import tpu as pltpu
 from jax.sharding import PartitionSpec as P
 
+
 F32 = jnp.float32
 BF16 = jnp.bfloat16
 LANES = 128
 TILES = 4
+AHEAD = (1, 1, 1, 1)
+CHUNKS = (0, 1, 2)
 VMEM = pltpu.VMEM
 SMEM = pltpu.SMEM
 HBM = pltpu.HBM
@@ -78,9 +81,7 @@
     up_copy.start()
     for t in range(TILES):
         tok_copy(t).start()
-        ups_copy(t).start()
     frozen_copy = fetch(frozen_hbm, frozen, sem.at[4])
-    frozen_copy.start()
     mine, side = where_ref[0], where_ref[1]
     row_i = lax.broadcasted_iota(jnp.int32, (experts, ranks), 0)
     col_i = lax.broadcasted_iota(jnp.int32, (experts, ranks), 1)
@@ -91,11 +92,18 @@
     wide_ref[:, :ranks] = down[...]
     ids_copy.wait()
     count = jnp.sum((ids[...] != 0).astype(jnp.int32))
+    for t in range(TILES):
+        part = pl.ds(t * tile, tile)
+        tok_copy(t).wait()
+        if t == 1:
+            for later in range(TILES):
+                ups_copy(later).start()
+        if t == TILES - 1:
+            frozen_copy.start()
+        both[part, :] = nn(tok[part, :], wide_ref[...])
     up_copy.wait()
     for t in range(TILES):
         part = pl.ds(t * tile, tile)
-        tok_copy(t).wait()
-        both[part, :] = nn(tok[part, :], wide_ref[...])
         ups_copy(t).wait()
         live = lax.broadcasted_iota(jnp.int32, (tile, 1), 0) + t * tile < count
         ups[part, :] = ups[part, :] * live.astype(F32).astype(BF16)
@@ -375,71 +383,90 @@
     )(*in_vmem(masked, *lefts, frozen, wide), *in_hbm(*past))
 
 
-def clip_kernel(orders_a, orders_b, experts, limit, where_ref, own_a, other_a, own_b, other_b, stat_own, stat_other, down_ref, up_ref, gate_ref, load_ref):
+def clip_kernel(orders, experts, limit, where_ref, *refs):
+    near, far = refs[:2], refs[2:5]
+    stat_own, stat_other = refs[5:7]
+    down_hbm, up_hbm, gate_hbm, load_ref, entropy_ref = refs[7:12]
+    down, up, gate, squares, down_sem, sem = refs[12:]
     mine, side = where_ref[0], where_ref[1]
-    pairs, ranks = own_a.shape[0], own_a.shape[1]
-    depth = pairs.bit_length() - 1
-    up_rows = own_b.shape[1] - experts
+    half = near[0].shape[0]
+    near = [(ref, spot) for ref in near for spot in range(ref.shape[0])]
+    far = [(ref, spot) for ref in far for spot in range(ref.shape[0])]
+    depth = (2 * half).bit_length() - 1
+    ranks = down.shape[1]
+    up_rows = near[0][0].shape[1] - ranks - experts
     per = ranks // up_rows
-
-    def fold(block):
+    blocks = []
+    for spot in range(2 * half):
+        words = []
+        for order in orders:
+            word = 0
+            for step in range(depth):
+                word += ((spot >> (depth - 1 - step)) & 1) << order[step]
+            words.append(word)
+        base = mine & (2 * half - 1)
+        own = base ^ jnp.where(side == 0, words[0], words[1])
+        other = base ^ jnp.where(side == 0, words[1], words[0])
+        blocks.append((*near[spot], 2 * own + side))
+        blocks.append((*far[spot], 2 * other + 1 - side))
+    for ref, spot, at in blocks:
+        block = ref[spot]
         square = block * block
-        return jnp.sum(square.reshape(block.shape[0] // 8, 8, LANES), axis=0)
-
-    def measure(pair, sums):
-        kept_a, sent_a = spots(mine, pair, side, orders_a, depth)
-        kept_b, sent_b = spots(mine, pair, side, orders_b, depth)
-        first = sums[0] + fold(own_a[kept_a]) + fold(own_b[kept_b])
-        second = sums[1] + fold(other_a[sent_a]) + fold(other_b[sent_b])
-        return first, second
-
-    zero = jnp.zeros((8, LANES), F32)
-    sums = lax.fori_loop(0, pairs, measure, (zero, zero), unroll=4)
-    total = jnp.sum(sums[0] + sums[1], axis=(0, 1), keepdims=True)
+        squares[at] = jnp.sum(square.reshape(block.shape[0] // 8, 8, LANES), axis=0)
+    total = jnp.sum(jnp.sum(squares[...], axis=0), axis=(0, 1), keepdims=True)
     factor = jnp.minimum(1.0, limit / jnp.sqrt(total))
-
-    def emit(block_a, block_b, at):
-        down_ref[pl.ds(pl.multiple_of(at * LANES, LANES), LANES), :] = (block_a * factor).T
-        lanes = pl.ds(pl.multiple_of(at * LANES, LANES), LANES)
-        gate_ref[:, lanes] = block_b[:experts] * factor
+    copies = []
+    for number, (ref, spot, at) in enumerate(blocks):
+        rows = pl.ds(pl.multiple_of(at * LANES, LANES), LANES)
+        down[rows, :] = (ref[spot, :ranks] * factor).T
+        copies.append(pltpu.make_async_copy(down.at[rows], down_hbm.at[rows], down_sem.at[number]))
+        copies[-1].start()
+        gate[:, rows] = ref[spot, ranks : ranks + experts] * factor
         rows = pl.ds(pl.multiple_of(at % per * up_rows, up_rows), up_rows)
         lanes = pl.ds(pl.multiple_of(at // per * LANES, LANES), LANES)
-        up_ref[rows, lanes] = block_b[experts:] * factor
-
-    def write(pair, carry):
-        kept_a, sent_a = spots(mine, pair, side, orders_a, depth)
-        kept_b, sent_b = spots(mine, pair, side, orders_b, depth)
-        emit(own_a[kept_a], own_b[kept_b], 2 * pair + side)
-        emit(other_a[sent_a], other_b[sent_b], 2 * pair + 1 - side)
-        return carry
-
-    lax.fori_loop(0, pairs, write, 0, unroll=4)
+        up[rows, lanes] = ref[spot, ranks + experts :] * factor
+    copies.append(pltpu.make_async_copy(up, up_hbm, sem.at[0]))
+    copies[-1].start()
+    copies.append(pltpu.make_async_copy(gate, gate_hbm, sem.at[1]))
+    copies[-1].start()
     stats = jnp.where(side == 0, stat_own[...], stat_other[...])
     stats = stats / stats[:, LANES - 1 :]
-    row = lax.broadcasted_iota(jnp.int32, stats.shape, 0)
-    lane = lax.broadcasted_iota(jnp.int32, stats.shape, 1)
-    load = jnp.sum(jnp.where(row == lane, stats, 0.0), axis=0, keepdims=True)
-    load_ref[...] = jnp.where(lane < LANES // 2, load, stats)
-
-
-def clip_write(where, own_a, other_a, own_b, other_b, stat_own, stat_other, outs, experts, orders_a, orders_b):
-    pairs, ranks = own_a.shape[0], own_a.shape[1]
-    width = 2 * pairs * LANES
+    for expert in range(experts):
+        load_ref[expert] = jnp.sum(stats[expert : expert + 1, :1])
+    entropy_ref[0] = jnp.sum(stats[:1, LANES // 2 : LANES // 2 + 1])
+    for copy in copies:
+        copy.wait()
+
+
+def clip_write(where, near, far, stat_own, stat_other, ranks, outs, experts, orders):
+    half = near[0].shape[0]
+    width = 4 * half * LANES
     limit = math.sqrt(width * ranks + ranks * outs + width * experts)
     vmem = pl.BlockSpec(memory_space=VMEM)
+    smem = pl.BlockSpec(memory_space=SMEM)
+    hbm = pl.BlockSpec(memory_space=HBM)
     return pl.pallas_call(
-        functools.partial(clip_kernel, orders_a, orders_b, experts, limit),
+        functools.partial(clip_kernel, orders, experts, limit),
         out_shape=[
-            jax.ShapeDtypeStruct((width, ranks), F32),
-            jax.ShapeDtypeStruct((ranks, outs), F32),
-            jax.ShapeDtypeStruct((experts, width), F32),
-            jax.ShapeDtypeStruct((experts, LANES), F32),
-        ],
-        in_specs=[pl.BlockSpec(memory_space=SMEM)] + [vmem] * 6,
-        out_specs=[vmem] * 4,
-        compiler_params=pltpu.CompilerParams(vmem_limit_bytes=24 * MIB),
+            HBM((width, ranks), F32),
+            HBM((ranks, outs), F32),
+            HBM((experts, width), F32),
+            jax.ShapeDtypeStruct((experts,), F32),
+            jax.ShapeDtypeStruct((1,), F32),
+        ],
+        in_specs=[smem] + [vmem] * 7,
+        out_specs=[hbm] * 3 + [smem] * 2,
+        scratch_shapes=[
+            VMEM((width, ranks), F32),
+            VMEM((ranks, outs), F32),
+            VMEM((experts, width), F32),
+            VMEM((4 * half, 8, LANES), F32),
+            pltpu.SemaphoreType.DMA((4 * half,)),
+            pltpu.SemaphoreType.DMA((2,)),
+        ],
+        compiler_params=pltpu.CompilerParams(vmem_limit_bytes=8 * MIB),
         name="clip_write",
-    )(where, own_a, other_a, own_b, other_b, stat_own, stat_other)
+    )(where, *in_vmem(*near, *far, stat_own, stat_other))
 
 
 def swap(array, masks):
@@ -466,6 +493,8 @@
     me = lax.axis_index("dp")
     where = jnp.stack([me >> 1, me & 1]).astype(jnp.int32)
     ids = token_ids.reshape(rows // LANES, LANES)
+    orders_g = orders_a
+    masks_g = [(2 << orders_g[0][s], 2 << orders_g[1][s]) for s in range(bits)]
     masks_a = [(2 << orders_a[0][s], 2 << orders_a[1][s]) for s in range(bits)]
     masks_b = [(2 << orders_b[0][s], 2 << orders_b[1][s]) for s in range(bits)]
 
@@ -473,63 +502,64 @@
         local_grads(where, ids, gate.T, down, up, tokens, upstream, frozen, orders_a, orders_b)
     )
     split_at = keep_a.shape[1]
-    recv_b = swap(send_b, (1, 1))
-    recv_a = swap(send_a, (1, 1))
     filled = ()
-    for step in range(bits):
-        if step < depth:
+    begin = 0
+    for step in range(-1, bits):
+        if step >= depth:
+            keep_b = send_b = keep_b + recv_b
+            keep_a = send_a = keep_a + recv_a
+        elif step >= 0:
             keep_b, send_b = halve(keep_b, recv_b)
             keep_a, send_a = halve(keep_a, recv_a)
-        else:
-            keep_b = send_b = keep_b + recv_b
-            keep_a = send_a = keep_a + recv_a
-        if step < 2:
+        parts = AHEAD[step + 1] if step + 1 < len(AHEAD) else 0
+        if parts:
             weighted, send_a, send_b, filled = lax.optimization_barrier(
                 (weighted, send_a, send_b, filled)
             )
-            filled = (project(tok, weighted, near, up_v, 2 * step, 2, filled),)
-        if masks_a[step] == masks_b[step]:
-            recv = swap(jnp.concatenate([send_a, send_b], axis=1), masks_a[step])
+            filled = (project(tok, weighted, near, up_v, begin, parts, filled),)
+            begin += parts
+        mask_a, mask_b = ((1, 1), (1, 1)) if step < 0 else (masks_a[step], masks_b[step])
+        if step >= 0 and mask_a == mask_b:
+            recv = swap(jnp.concatenate([send_a, send_b], axis=1), mask_a)
             recv_a, recv_b = recv[:, :split_at], recv[:, split_at:]
         else:
-            recv_b = swap(send_b, masks_b[step])
-            recv_a = swap(send_a, masks_a[step])
-        if step < 2:
+            recv_b = swap(send_b, mask_b)
+            recv_a = swap(send_a, mask_a)
+        if parts:
             recv_a, recv_b, filled = lax.optimization_barrier((recv_a, recv_b, filled))
     projected = filled[0]
     own, stats = owner_rows(keep_a, keep_b, recv, experts)
-    own_a, own_b = own[:, :split_at], own[:, split_at:]
     lefts = (low_grad, plain, share, stats)
     filled = ()
+    begin = 0
+    tiles = tokens.shape[1] // (4 * LANES)
     turns = tuple(reversed(range(depth)))
-    chunk = tokens.shape[1] // (4 * LANES * depth)
     for turn, step in enumerate(turns):
-        together = turn == 0 and masks_a[step] == masks_b[step]
-        if together:
-            lefts, own, filled = lax.optimization_barrier((lefts, own, filled))
+        lefts, own, filled = lax.optimization_barrier((lefts, own, filled))
+        last = turn == depth - 1
+        parts = tiles - begin if last else CHUNKS[turn]
+        if parts:
+            made = input_grads(masked, lefts, near, wide, experts, begin, parts, filled)
+            begin += parts
+            if isinstance(made, (list, tuple)):
+                filled, lefts = (made[0],), (made[1],)
+            else:
+                filled = (made,)
+        if turn == depth - 2:
+            far = (swap(own, (1, 1)),)
+            recv = swap(own, masks_g[step])
         else:
-            lefts, own_a, own_b, filled = lax.optimization_barrier((lefts, own_a, own_b, filled))
-        made = input_grads(masked, lefts, near, wide, experts, turn * chunk, chunk, filled)
-        if turn == 0:
-            filled, lefts = (made[0],), (made[1],)
-        else:
-            filled = (made,)
-        if together:
-            recv = swap(own, masks_a[step])
-            recv, filled = lax.optimization_barrier((recv, filled))
-            recv_a, recv_b = recv[:, :split_at], recv[:, split_at:]
-        else:
-            recv_b = swap(own_b, masks_b[step])
-            recv_a = swap(own_a, masks_a[step])
-            recv_a, recv_b, filled = lax.optimization_barrier((recv_a, recv_b, filled))
-        own_b = jnp.concatenate([own_b, recv_b], axis=0)
-        own_a = jnp.concatenate([own_a, recv_a], axis=0)
+            recv = swap(own, masks_g[step])
+        if last:
+            far += (swap(own[own.shape[0] // 2 :], (1, 1)),)
+            stat_other = swap(stats, (1, 1))
+        recv, filled = lax.optimization_barrier((recv, filled))
+        if not last:
+            own = jnp.concatenate([own, recv], axis=0)
     input_grad = filled[0]
-    stat_other = swap(stats, (1, 1))
-    other_b = swap(own_b, (1, 1))
-    other_a = swap(own_a, (1, 1))
-    clipped_down, clipped_up, clipped_gate, summary = clip_write(
-        where, own_a, other_a, own_b, other_b, stats, stat_other, outs, experts, orders_a, orders_b
+    far += (swap(recv, (1, 1)),)
+    clipped_down, clipped_up, clipped_gate, load, entropy = clip_write(
+        where, (own, recv), far, stats, stat_other, split_at, outs, experts, orders_g
     )
     return (
         projected,
@@ -537,8 +567,8 @@
         clipped_down,
         clipped_up,
         clipped_gate.T,
-        summary[0, :experts],
-        summary[0, LANES // 2],
+        load,
+        entropy.reshape(()),
     )
 
 

time: 93.1 us -> 90.9 us (0.976)
  starting transfers between devices: 23.9 us -> 15.6 us
  waiting for transfers between devices: 22.3 us -> 29.4 us
  local copies, waits for them, and re-layouts: 1.21 us -> 0.02 us
    ppermute x19 -> x17, starting transfers between devices: 23.9 us -> 15.6 us  [swap(): lax.ppermute(array, 'dp', [(i, i ^ masks[i & 1]) for i in range(size)])]
    ppermute x19 -> x17, waiting for transfers between devices: 22.3 us -> 29.4 us  [swap(): lax.ppermute(array, 'dp', [(i, i ^ masks[i & 1]) for i in range(size)])]
    pallas_call x2 -> x4, Pallas kernels: 11.5 us -> 13.3 us  [project(): pl.pallas_call(functools.partial(project_kernel, begin), out_shape=HBM((r...]
    pallas_call x4 -> x3, Pallas kernels: 15.7 us -> 14.5 us  [input_grads(): pl.pallas_call(functools.partial(input_kernel, experts, begin, first), ou...]
  transfers between devices with their start and end apart: 19 -> 17, of which waited for: 11 -> 10; matrix products, arithmetic and copies ran while one was open for 0% -> 0% of each run, Pallas kernels for 29% -> 31%
where the time goes in v3:
time: 90.9 us; the launch traced here: 90.7 us
  Pallas kernels  44.1 us (49%)
  waiting for transfers between devices  29.4 us (32%)
  starting transfers between devices  15.6 us (17%)
  between operations  0.97 us (1%)
    ppermute x17, waiting for transfers between devices, swap(): lax.ppermute(array, 'dp', [(i, i ^ masks[i & 1]) for i in range(size)])  29.4 us
    ppermute x17, starting transfers between devices, swap(): lax.ppermute(array, 'dp', [(i, i ^ masks[i & 1]) for i in range(size)])  15.6 us
    pallas_call x3, Pallas kernels, input_grads(): pl.pallas_call(functools.partial(input_kernel, experts, begin, first), ou...  14.5 us
    pallas_call x4, Pallas kernels, project(): pl.pallas_call(functools.partial(project_kernel, begin), out_shape=HBM((r...  13.3 us
    pallas_call x1, Pallas kernels, local_grads(): pl.pallas_call(functools.partial(local_kernel, orders_a, orders_b), out_s...  12.8 us
    pallas_call x1, Pallas kernels, clip_write(): pl.pallas_call(functools.partial(clip_kernel, orders, experts, limit), ou...  3.41 us
  transfers between devices with their start and end apart: 17, of which 10 were waited for; matrix products, arithmetic and copies ran while one was open for 0% of the time, Pallas kernels for 31%

profile of v3, /device:TPU:0, one launch (start us, length us, event | category | flops | bytes accessed | tf_op | source)
XLA Modules:
  0.0 90.7 jit_solution(1208107865464278682)
XLA Ops:
  0.7 12.8 %local_grads.1 = (f32[16,128,128]{2,1,0:T(8,128)S(1)}, f32[16,128,128]{2,1,0:T(8,128)S(1)}, f32[16,80,128]{2,1,0:T(8,128)S(1)}, f32[16,80,128]{2,1,0:T(8,128)S(1...) custom-call(s32[2]{0:T(128)S(1)} %pad_add_fusion.where_ref, ...), custom_call_target="tpu_custom_call" | custom-call | flops 4294967296 | bytes 10485760 | tf_op jit(solution)/shard_map/local_grads/pallas_call | solution.py:207
  13.5 0.6 collective-permute-start
  14.2 3.3 %project.4.rest_0_ = bf16[1024,1024]{1,0:T(8,128)(2,1)} custom-call(bf16[1024,4096]{1,0:T(8,128)(2,1)S(1)} %get-tuple-element.85.tok, bf16[1024,128]{1,0:T(8,128)(2,1)S(1)} %get-tuple-element.108.weighted_ref, bf16[4096,1024]{1,0:T(8,128)(2,1)S(1)} %get-tuple-element.86.frozen.refs_5_.refs_2_, bf16[128,1024]{1,0:T(8,128)(2,1)S(1)} %get-tuple-element.87.up_ref), custom_call_target="tpu_custom_call" | custom-call | flops 2214592512 | bytes 11010048 | tf_op jit(solution)/shard_map/project/pallas_call | solution.py:271
  17.7 3.0 %collective-permute-start.2 = (f32[8,128,128]{2,1,0:T(8,128)S(1)}, f32[8,128,128]{2,1,0:T(8,128)S(1)}, u32[]{:S(2)}, u32[]{:S(2)}) collective-permute-start(f32[8,128,128]{2,1,0:T(8,128)S(1)} %get-tuple-element.93), channel_id=1, source_target_pairs={{0,2},{1,5},{2,0},{3,7},{4,6},{5,1},{6,4},{7,3},{8,10},{9,13},{10,... | collective-permute-start | bytes 1572872 | tf_op jit(solution)/shard_map/ppermute | solution.py:474
  20.7 1.6 %collective-permute-start.3 = (f32[8,80,128]{2,1,0:T(8,128)S(1)}, f32[8,80,128]{2,1,0:T(8,128)S(1)}, u32[]{:S(2)}, u32[]{:S(2)}) collective-permute-start(f32[8,80,128]{2,1,0:T(8,128)S(1)} %get-tuple-element.94), channel_id=1, source_target_pairs={{0,8},{1,9},{2,10},{3,11},{4,12},{5,13},{6,14},{7,15},{8,0},{9,1},... | collective-permute-start | bytes 983048 | tf_op jit(solution)/shard_map/ppermute | solution.py:474
  22.2 3.3 %project.5.rest_0_ = bf16[1024,1024]{1,0:T(8,128)(2,1)} custom-call(bf16[1024,4096]{1,0:T(8,128)(2,1)S(1)} %get-tuple-element.85.tok, bf16[1024,128]{1,0:T(8,128)(2,1)S(1)} %get-tuple-element.108.weighted_ref, bf16[4096,1024]{1,0:T(8,128)(2,1)S(1)} %get-tuple-element.86.frozen.refs_5_.refs_2_, ...), custom_call_target="tpu_custom_call", output_to_operand_aliasing={{}: (4, {})} | custom-call | flops 2214592512 | bytes 11010048 | tf_op jit(solution)/shard_map/project/pallas_call | solution.py:271
  25.5 4.6 %collective-permute-done.3 = f32[8,80,128]{2,1,0:T(8,128)S(1)} collective-permute-done((f32[8,80,128]{2,1,0:T(8,128)S(1)}, f32[8,80,128]{2,1,0:T(8,128)S(1)}, u32[]{:S(2)}, u32[]{:S(2)}) %collective-permute-start.3) | collective-permute-done | bytes 327712 | tf_op jit(solution)/shard_map/ppermute | solution.py:474
  30.2 0.4 collective-permute-start.4
  30.6 1.6 %collective-permute-start.5 = (f32[4,80,128]{2,1,0:T(8,128)S(1)}, f32[4,80,128]{2,1,0:T(8,128)S(1)}, u32[]{:S(2)}, u32[]{:S(2)}) collective-permute-start(f32[4,80,128]{2,1,0:T(8,128)S(1)} %get-tuple-element.101), channel_id=1, source_target_pairs={{0,2},{1,5},{2,0},{3,7},{4,6},{5,1},{6,4},{7,3},{8,10},{9,13},{10,... | collective-permute-start | bytes 491528 | tf_op jit(solution)/shard_map/ppermute | solution.py:474
  32.3 3.5 %project.6.rest_0_ = bf16[1024,1024]{1,0:T(8,128)(2,1)} custom-call(bf16[1024,4096]{1,0:T(8,128)(2,1)S(1)} %get-tuple-element.85.tok, bf16[1024,128]{1,0:T(8,128)(2,1)S(1)} %get-tuple-element.108.weighted_ref, bf16[4096,1024]{1,0:T(8,128)(2,1)S(1)} %get-tuple-element.86.frozen.refs_5_.refs_2_, ...), custom_call_target="tpu_custom_call", output_to_operand_aliasing={{}: (4, {})} | custom-call | flops 2214592512 | bytes 11010048 | tf_op jit(solution)/shard_map/project/pallas_call | solution.py:271
  35.7 1.0 %collective-permute-done.5 = f32[4,80,128]{2,1,0:T(8,128)S(1)} collective-permute-done((f32[4,80,128]{2,1,0:T(8,128)S(1)}, f32[4,80,128]{2,1,0:T(8,128)S(1)}, u32[]{:S(2)}, u32[]{:S(2)}) %collective-permute-start.5) | collective-permute-done | bytes 163872 | tf_op jit(solution)/shard_map/ppermute | solution.py:474
  36.8 1.5 %collective-permute-done.4 = f32[4,128,128]{2,1,0:T(8,128)S(1)} collective-permute-done((f32[4,128,128]{2,1,0:T(8,128)S(1)}, f32[4,128,128]{2,1,0:T(8,128)S(1)}, u32[]{:S(2)}, u32[]{:S(2)}) %collective-permute-start.4) | collective-permute-done | bytes 262176 | tf_op jit(solution)/shard_map/ppermute | solution.py:474
  38.3 1.8 %collective-permute-start.6 = (f32[2,128,128]{2,1,0:T(8,128)S(1)}, f32[2,128,128]{2,1,0:T(8,128)S(1)}, u32[]{:S(2)}, u32[]{:S(2)}) collective-permute-start(f32[2,128,128]{2,1,0:T(8,128)S(1)} %get-tuple-element.106), channel_id=1, source_target_pairs={{0,8},{1,9},{2,10},{3,11},{4,12},{5,13},{6,14},{7,15},{8,0},{9,1},... | collective-permute-start | bytes 393224 | tf_op jit(solution)/shard_map/ppermute | solution.py:474
  40.1 0.5 collective-permute-start.7
  40.6 3.3 %project.7 = bf16[1024,1024]{1,0:T(8,128)(2,1)} custom-call(bf16[1024,4096]{1,0:T(8,128)(2,1)S(1)} %get-tuple-element.85.tok, bf16[1024,128]{1,0:T(8,128)(2,1)S(1)} %get-tuple-element.108.weighted_ref, bf16[4096,1024]{1,0:T(8,128)(2,1)S(1)} %get-tuple-element.86.frozen.refs_5_.refs_2_, ...), custom_call_target="tpu_custom_call", output_to_operand_aliasing={{}: (4, {})} | custom-call | flops 2214592512 | bytes 11010048 | tf_op jit(solution)/shard_map/project/pallas_call | solution.py:271
  43.8 0.7 collective-permute-done.7
  44.6 2.7 %collective-permute-start.8 = (f32[1,208,128]{2,1,0:T(8,128)S(1)}, f32[1,208,128]{2,1,0:T(8,128)S(1)}, u32[]{:S(2)}, u32[]{:S(2)}) collective-permute-start(f32[1,208,128]{2,1,0:T(8,128)S(1)} %pad_maximum_fusion.3), channel_id=1, source_target_pairs={{0,16},{1,17},{2,18},{3,19},{4,20},{5,21},{6,22},{7,23},{8,24},{9,... | collective-permute-start | bytes 319496 | tf_op jit(solution)/shard_map/ppermute | solution.py:474
  47.3 4.1 %collective-permute-done.8.recv = f32[1,208,128]{2,1,0:T(8,128)S(1)} collective-permute-done((f32[1,208,128]{2,1,0:T(8,128)S(1)}, f32[1,208,128]{2,1,0:T(8,128)S(1)}, u32[]{:S(2)}, u32[]{:S(2)}) %collective-permute-start.8) | collective-permute-done | bytes 106528 | tf_op jit(solution)/shard_map/ppermute | solution.py:474
  51.5 1.6 %collective-permute-start.9 = (f32[1,168,128]{2,1,0:T(8,128)S(1)}, f32[1,168,128]{2,1,0:T(8,128)S(1)}, u32[]{:S(2)}, u32[]{:S(2)}) collective-permute-start(f32[1,168,128]{2,1,0:T(8,128)S(1)} %get-tuple-element.123), channel_id=1, source_target_pairs={{0,16},{1,17},{2,18},{3,19},{4,20},{5,21},{6,22},{7,23},{8,24},{9,... | collective-permute-start | bytes 258056 | tf_op jit(solution)/shard_map/ppermute | solution.py:474
  53.1 4.5 %collective-permute-done.9 = f32[1,168,128]{2,1,0:T(8,128)S(1)} collective-permute-done((f32[1,168,128]{2,1,0:T(8,128)S(1)}, f32[1,168,128]{2,1,0:T(8,128)S(1)}, u32[]{:S(2)}, u32[]{:S(2)}) %collective-permute-start.9) | collective-permute-done | bytes 86048 | tf_op jit(solution)/shard_map/ppermute | solution.py:474
  57.7 2.7 %input_grads.3 = (bf16[1024,4096]{1,0:T(8,128)(2,1)}, bf16[1024,256]{1,0:T(8,128)(2,1)S(1)}) custom-call(bf16[1024,1024]{1,0:T(8,128)(2,1)S(1)} %get-tuple-element.111.refs_0_, bf16[1024,128]{1,0:T(8,128)(2,1)S(1)} %get-tuple-element.124.refs_1_, f32[8,1024]{1,0:T(8,128)S(1)} %get-tuple-element.125.refs_2_, f32[8,1024]{1,0:T(8,128)S(1)} %get-tuple-element.126.refs_3_, ...), custom_call_target="tpu_custom_call" | custom-call | flops 1342177280 | bytes 4194304 | tf_op jit(solution)/shard_map/input_grads/pallas_call | solution.py:366
  60.3 2.7 %collective-permute-done.10 = f32[2,168,128]{2,1,0:T(8,128)S(1)} collective-permute-done((f32[2,168,128]{2,1,0:T(8,128)S(1)}, f32[2,168,128]{2,1,0:T(8,128)S(1)}, u32[]{:S(2)}, u32[]{:S(2)}) %collective-permute-start.10) | collective-permute-done | bytes 172064 | tf_op jit(solution)/shard_map/ppermute | solution.py:474
  63.1 0.3 collective-permute-start.11
  63.4 3.9 %input_grads.4.refs_4_ = bf16[1024,4096]{1,0:T(8,128)(2,1)} custom-call(bf16[1024,1024]{1,0:T(8,128)(2,1)S(1)} %get-tuple-element.111.refs_0_, bf16[1024,256]{1,0:T(8,128)(2,1)S(1)} %get-tuple-element.140.refs_1_, bf16[4096,1024]{1,0:T(8,128)(2,1)S(1)} %get-tuple-element.86.frozen.refs_5_.refs_2_, ...), custom_call_target="tpu_custom_call", output_to_operand_aliasing={{}: (4, {})} | custom-call | flops 2684354560 | bytes 6291456 | tf_op jit(solution)/shard_map/input_grads/pallas_call | solution.py:366
  67.3 5.7 %collective-permute-done.11 = f32[4,168,128]{2,1,0:T(8,128)S(1)} collective-permute-done((f32[4,168,128]{2,1,0:T(8,128)S(1)}, f32[4,168,128]{2,1,0:T(8,128)S(1)}, u32[]{:S(2)}, u32[]{:S(2)}) %collective-permute-start.11) | collective-permute-done | bytes 344096 | tf_op jit(solution)/shard_map/ppermute | solution.py:474
  73.0 0.4 collective-permute-start.12
  73.4 8.0 %input_grads.5 = bf16[1024,4096]{1,0:T(8,128)(2,1)} custom-call(bf16[1024,1024]{1,0:T(8,128)(2,1)S(1)} %get-tuple-element.111.refs_0_, bf16[1024,256]{1,0:T(8,128)(2,1)S(1)} %get-tuple-element.140.refs_1_, bf16[4096,1024]{1,0:T(8,128)(2,1)S(1)} %get-tuple-element.86.frozen.refs_5_.refs_2_, ...), custom_call_target="tpu_custom_call", output_to_operand_aliasing={{}: (4, {})} | custom-call | flops 6710886400 | bytes 12582912 | tf_op jit(solution)/shard_map/input_grads/pallas_call | solution.py:366
  81.4 2.6 %collective-permute-done.12.refs_1_ = f32[8,168,128]{2,1,0:T(8,128)S(1)} collective-permute-done((f32[8,168,128]{2,1,0:T(8,128)S(1)}, f32[8,168,128]{2,1,0:T(8,128)S(1)}, u32[]{:S(2)}, u32[]{:S(2)}) %collective-permute-start.12) | collective-permute-done | bytes 688160 | tf_op jit(solution)/shard_map/ppermute | solution.py:474
  84.0 0.5 collective-permute-start.13
  84.6 0.5 collective-permute-start.16
  85.1 2.0 %collective-permute-done.16.refs_6_ = f32[8,128]{1,0:T(8,128)S(1)} collective-permute-done((f32[8,128]{1,0:T(8,128)S(1)}, f32[8,128]{1,0:T(8,128)S(1)}, u32[]{:S(2)}, u32[]{:S(2)}) %collective-permute-start.16) | collective-permute-done | bytes 4128 | tf_op jit(solution)/shard_map/ppermute | solution.py:474
  87.1 3.4 %clip_write.1 = (f32[4096,128]{1,0:T(8,128)}, f32[128,1024]{1,0:T(8,128)}, f32[8,4096]{1,0:T(8,128)}, f32[8]{0:T(128)}, f32[1]{0:T(128)}) custom-call(s32[2]{0:T(128)S(1)} %pad_add_fusion.where_ref, f32[8,168,128]{2,1,0:T(8,128)S(1)} %pad_maximum_fusion.refs_0_, f32[8,168,128]{2,1,0:T(8,128)S(1)} %collective-permute-done.12.refs_1_, ...), custom_call_target="tpu_custom_call" | custom-call | tf_op jit(solution)/shard_map/clip_write/pallas_call | solution.py:448
  (26 shorter events, 0.9 us)
Async XLA Ops:
  13.5 3.9 %collective-permute-start = (f32[16,128,128]{2,1,0:T(8,128)S(1)}, f32[16,128,128]{2,1,0:T(8,128)S(1)}, u32[]{:S(2)}, u32[]{:S(2)}) collective-permute-start(f32[16,128,128]{2,1,0:T(8,128)S(1)} %get-tuple-element.83), channel_id=1, source_target_pairs={{0,1},{1,0},{2,3},{3,2},{4,5},{5,4},{6,7},{7,6},{8,9},{9,8},{10,11... | collective-permute-start | bytes 3145736 | tf_op jit(solution)/shard_map/ppermute | solution.py:474
  14.1 3.4 %collective-permute-start.1 = (f32[16,80,128]{2,1,0:T(8,128)S(1)}, f32[16,80,128]{2,1,0:T(8,128)S(1)}, u32[]{:S(2)}, u32[]{:S(2)}) collective-permute-start(f32[16,80,128]{2,1,0:T(8,128)S(1)} %get-tuple-element.84), channel_id=1, source_target_pairs={{0,1},{1,0},{2,3},{3,2},{4,5},{5,4},{6,7},{7,6},{8,9},{9,8},{10,11... | collective-permute-start | bytes 1966088 | tf_op jit(solution)/shard_map/ppermute | solution.py:474
  17.7 12.4 %collective-permute-start.2 = (f32[8,128,128]{2,1,0:T(8,128)S(1)}, f32[8,128,128]{2,1,0:T(8,128)S(1)}, u32[]{:S(2)}, u32[]{:S(2)}) collective-permute-start(f32[8,128,128]{2,1,0:T(8,128)S(1)} %get-tuple-element.93), channel_id=1, source_target_pairs={{0,2},{1,5},{2,0},{3,7},{4,6},{5,1},{6,4},{7,3},{8,10},{9,13},{10,... | collective-permute-start | bytes 1572872 | tf_op jit(solution)/shard_map/ppermute | solution.py:474
  20.7 9.4 %collective-permute-start.3 = (f32[8,80,128]{2,1,0:T(8,128)S(1)}, f32[8,80,128]{2,1,0:T(8,128)S(1)}, u32[]{:S(2)}, u32[]{:S(2)}) collective-permute-start(f32[8,80,128]{2,1,0:T(8,128)S(1)} %get-tuple-element.94), channel_id=1, source_target_pairs={{0,8},{1,9},{2,10},{3,11},{4,12},{5,13},{6,14},{7,15},{8,0},{9,1},... | collective-permute-start | bytes 983048 | tf_op jit(solution)/shard_map/ppermute | solution.py:474
  30.2 8.0 %collective-permute-start.4 = (f32[4,128,128]{2,1,0:T(8,128)S(1)}, f32[4,128,128]{2,1,0:T(8,128)S(1)}, u32[]{:S(2)}, u32[]{:S(2)}) collective-permute-start(f32[4,128,128]{2,1,0:T(8,128)S(1)} %get-tuple-element.100), channel_id=1, source_target_pairs={{0,4},{1,3},{2,6},{3,1},{4,0},{5,7},{6,2},{7,5},{8,12},{9,11},{10,... | collective-permute-start | bytes 786440 | tf_op jit(solution)/shard_map/ppermute | solution.py:474
  30.6 6.1 %collective-permute-start.5 = (f32[4,80,128]{2,1,0:T(8,128)S(1)}, f32[4,80,128]{2,1,0:T(8,128)S(1)}, u32[]{:S(2)}, u32[]{:S(2)}) collective-permute-start(f32[4,80,128]{2,1,0:T(8,128)S(1)} %get-tuple-element.101), channel_id=1, source_target_pairs={{0,2},{1,5},{2,0},{3,7},{4,6},{5,1},{6,4},{7,3},{8,10},{9,13},{10,... | collective-permute-start | bytes 491528 | tf_op jit(solution)/shard_map/ppermute | solution.py:474
  38.3 6.3 %collective-permute-start.6 = (f32[2,128,128]{2,1,0:T(8,128)S(1)}, f32[2,128,128]{2,1,0:T(8,128)S(1)}, u32[]{:S(2)}, u32[]{:S(2)}) collective-permute-start(f32[2,128,128]{2,1,0:T(8,128)S(1)} %get-tuple-element.106), channel_id=1, source_target_pairs={{0,8},{1,9},{2,10},{3,11},{4,12},{5,13},{6,14},{7,15},{8,0},{9,1},... | collective-permute-start | bytes 393224 | tf_op jit(solution)/shard_map/ppermute | solution.py:474
  40.1 4.4 %collective-permute-start.7 = (f32[2,80,128]{2,1,0:T(8,128)S(1)}, f32[2,80,128]{2,1,0:T(8,128)S(1)}, u32[]{:S(2)}, u32[]{:S(2)}) collective-permute-start(f32[2,80,128]{2,1,0:T(8,128)S(1)} %get-tuple-element.107), channel_id=1, source_target_pairs={{0,4},{1,3},{2,6},{3,1},{4,0},{5,7},{6,2},{7,5},{8,12},{9,11},{10,... | collective-permute-start | bytes 245768 | tf_op jit(solution)/shard_map/ppermute | solution.py:474
  44.6 6.8 %collective-permute-start.8 = (f32[1,208,128]{2,1,0:T(8,128)S(1)}, f32[1,208,128]{2,1,0:T(8,128)S(1)}, u32[]{:S(2)}, u32[]{:S(2)}) collective-permute-start(f32[1,208,128]{2,1,0:T(8,128)S(1)} %pad_maximum_fusion.3), channel_id=1, source_target_pairs={{0,16},{1,17},{2,18},{3,19},{4,20},{5,21},{6,22},{7,23},{8,24},{9,... | collective-permute-start | bytes 319496 | tf_op jit(solution)/shard_map/ppermute | solution.py:474
  51.5 6.1 %collective-permute-start.9 = (f32[1,168,128]{2,1,0:T(8,128)S(1)}, f32[1,168,128]{2,1,0:T(8,128)S(1)}, u32[]{:S(2)}, u32[]{:S(2)}) collective-permute-start(f32[1,168,128]{2,1,0:T(8,128)S(1)} %get-tuple-element.123), channel_id=1, source_target_pairs={{0,16},{1,17},{2,18},{3,19},{4,20},{5,21},{6,22},{7,23},{8,24},{9,... | collective-permute-start | bytes 258056 | tf_op jit(solution)/shard_map/ppermute | solution.py:474
  57.6 5.5 %collective-permute-start.10 = (f32[2,168,128]{2,1,0:T(8,128)S(1)}, f32[2,168,128]{2,1,0:T(8,128)S(1)}, u32[]{:S(2)}, u32[]{:S(2)}) collective-permute-start(f32[2,168,128]{2,1,0:T(8,128)S(1)} %pad_maximum_fusion.2), channel_id=1, source_target_pairs={{0,8},{1,9},{2,10},{3,11},{4,12},{5,13},{6,14},{7,15},{8,0},{9,1},... | collective-permute-start | bytes 516104 | tf_op jit(solution)/shard_map/ppermute | solution.py:474
  63.1 9.8 %collective-permute-start.11 = (f32[4,168,128]{2,1,0:T(8,128)S(1)}, f32[4,168,128]{2,1,0:T(8,128)S(1)}, u32[]{:S(2)}, u32[]{:S(2)}) collective-permute-start(f32[4,168,128]{2,1,0:T(8,128)S(1)} %pad_maximum_fusion.1), channel_id=1, source_target_pairs={{0,4},{1,3},{2,6},{3,1},{4,0},{5,7},{6,2},{7,5},{8,12},{9,11},{10,... | collective-permute-start | bytes 1032200 | tf_op jit(solution)/shard_map/ppermute | solution.py:474
  73.0 11.0 %collective-permute-start.12 = (f32[8,168,128]{2,1,0:T(8,128)S(1)}, f32[8,168,128]{2,1,0:T(8,128)S(1)}, u32[]{:S(2)}, u32[]{:S(2)}) collective-permute-start(f32[8,168,128]{2,1,0:T(8,128)S(1)} %pad_maximum_fusion.refs_0_), channel_id=1, source_target_pairs={{0,2},{1,5},{2,0},{3,7},{4,6},{5,1},{6,4},{7,3},{8,10},{9,13},{10,... | collective-permute-start | bytes 2064392 | tf_op jit(solution)/shard_map/ppermute | solution.py:474
  84.0 3.1 %collective-permute-start.15 = (f32[8,168,128]{2,1,0:T(8,128)S(1)}, f32[8,168,128]{2,1,0:T(8,128)S(1)}, u32[]{:S(2)}, u32[]{:S(2)}) collective-permute-start(f32[8,168,128]{2,1,0:T(8,128)S(1)} %collective-permute-done.12.refs_1_), channel_id=1, source_target_pairs={{0,1},{1,0},{2,3},{3,2},{4,5},{5,4},{6,7},{7,6},{8,9},{9,8},{10,11... | collective-permute-start | bytes 2064392 | tf_op jit(solution)/shard_map/ppermute | solution.py:474
  84.0 3.1 %collective-permute-start.13 = (f32[4,168,128]{2,1,0:T(8,128)S(1)}, f32[4,168,128]{2,1,0:T(8,128)S(1)}, u32[]{:S(2)}, u32[]{:S(2)}) collective-permute-start(f32[4,168,128]{2,1,0:T(8,128)S(1)} %pad_maximum_fusion.1), channel_id=1, source_target_pairs={{0,1},{1,0},{2,3},{3,2},{4,5},{5,4},{6,7},{7,6},{8,9},{9,8},{10,11... | collective-permute-start | bytes 1032200 | tf_op jit(solution)/shard_map/ppermute | solution.py:474
  84.5 2.6 %collective-permute-start.14 = (f32[4,168,128]{2,1,0:T(8,128)S(1)}, f32[4,168,128]{2,1,0:T(8,128)S(1)}, u32[]{:S(2)}, u32[]{:S(2)}) collective-permute-start(f32[4,168,128]{2,1,0:T(8,128)S(1)} %slice.131), channel_id=1, source_target_pairs={{0,1},{1,0},{2,3},{3,2},{4,5},{5,4},{6,7},{7,6},{8,9},{9,8},{10,11... | collective-permute-start | bytes 1032200 | tf_op jit(solution)/shard_map/ppermute | solution.py:474
  84.6 2.5 %collective-permute-start.16 = (f32[8,128]{1,0:T(8,128)S(1)}, f32[8,128]{1,0:T(8,128)S(1)}, u32[]{:S(2)}, u32[]{:S(2)}) collective-permute-start(f32[8,128]{1,0:T(8,128)S(1)} %get-tuple-element.127.refs_4_.refs_5_), channel_id=1, source_target_pairs={{0,1},{1,0},{2,3},{3,2},{4,5},{5,4},{6,7},{7,6},{8,9},{9,8},{10,11... | collective-permute-start | bytes 12296 | tf_op jit(solution)/shard_map/ppermute | solution.py:474

commit v4 on v3

--- a/solution.py
+++ b/solution.py
@@ -14,7 +14,7 @@
 LANES = 128
 TILES = 4
 AHEAD = (1, 1, 1, 1)
-CHUNKS = (0, 1, 2)
+CHUNKS = (1, 2)
 VMEM = pltpu.VMEM
 SMEM = pltpu.SMEM
 HBM = pltpu.HBM
@@ -90,8 +90,6 @@
     wide_ref[:, ranks:] = nn(gate[...].astype(F32).T.astype(BF16), twice).astype(BF16)
     down_copy.wait()
     wide_ref[:, :ranks] = down[...]
-    ids_copy.wait()
-    count = jnp.sum((ids[...] != 0).astype(jnp.int32))
     for t in range(TILES):
         part = pl.ds(t * tile, tile)
         tok_copy(t).wait()
@@ -101,13 +99,15 @@
         if t == TILES - 1:
             frozen_copy.start()
         both[part, :] = nn(tok[part, :], wide_ref[...])
+    ids_copy.wait()
+    count = jnp.sum((ids[...] != 0).astype(jnp.int32))
     up_copy.wait()
     for t in range(TILES):
         part = pl.ds(t * tile, tile)
         ups_copy(t).wait()
         live = lax.broadcasted_iota(jnp.int32, (tile, 1), 0) + t * tile < count
         ups[part, :] = ups[part, :] * live.astype(F32).astype(BF16)
-        back[part, :] = nt(ups[part, :], up[...])
+    back[...] = nt(ups[...], up[...])
     logits = both[:, ranks:].T[:experts, :]
     shifted = logits - jnp.max(logits, axis=0, keepdims=True)
     powers = jnp.exp(shifted)
@@ -153,10 +153,11 @@
         left_t[at, :] = jnp.concatenate([big, small], axis=0).astype(BF16)
     load = jnp.sum(share, axis=1, keepdims=True)
     entropy = jnp.sum(alive * ent, axis=1, keepdims=True)
-    lane = lax.broadcasted_iota(jnp.int32, (experts, LANES), 1)
-    stats[...] = jnp.where(
-        lane < LANES // 2, load, jnp.where(lane < LANES // 4 * 3, entropy, count.astype(F32))
-    )
+    half = experts // 2
+    lane = lax.broadcasted_iota(jnp.int32, (half, LANES), 1)
+    pair_load = jnp.where(lane < LANES // 4, load[:half], load[half:])
+    rest = jnp.where(lane < LANES // 4 * 3, entropy, count.astype(F32))
+    stats[...] = jnp.where(lane < LANES // 2, pair_load, rest)
     used = ranks + 2 * kinds * experts
     pairs = width // (2 * LANES)
     depth = pairs.bit_length() - 1
@@ -178,12 +179,12 @@
         to = pl.ds(0, gate_rows)
         keep_b[kept_b, to] = jnp.where(side == 0, gates[:, :LANES], gates[:, LANES:])
         send_b[sent_b, to] = jnp.where(side == 0, gates[:, LANES:], gates[:, :LANES])
-        keep_b[kept_b, pl.ds(gate_rows, experts)] = stats[...]
-        send_b[sent_b, pl.ds(gate_rows, experts)] = stats[...]
+        keep_b[kept_b, pl.ds(gate_rows - half, half)] = stats[...]
+        send_b[sent_b, pl.ds(gate_rows - half, half)] = stats[...]
         first, second = 2 * pair, 2 * pair + 1
         one = grad_up[pl.ds((first % per) * up_rows, up_rows), pl.ds(first // per * LANES, LANES)]
         two = grad_up[pl.ds((second % per) * up_rows, up_rows), pl.ds(second // per * LANES, LANES)]
-        to = pl.ds(gate_rows + experts, up_rows)
+        to = pl.ds(gate_rows, up_rows)
         keep_b[kept_b, to] = jnp.where(side == 0, one, two)
         send_b[sent_b, to] = jnp.where(side == 0, two, one)
     frozen_copy.wait()
@@ -203,7 +204,7 @@
     experts, ranks = gate_t.shape[0], down.shape[1]
     pairs = width // (2 * LANES)
     kinds = experts // 2 + 1
-    rows_b = (kinds + 1) * experts + ranks * outs // (2 * pairs * LANES)
+    rows_b = kinds * experts + ranks * outs // (2 * pairs * LANES)
     return pl.pallas_call(
         functools.partial(local_kernel, orders_a, orders_b),
         out_shape=[
@@ -232,7 +233,7 @@
             VMEM((2 * ranks, rows), BF16),
             VMEM((ranks, rows), BF16),
             VMEM((ranks, outs), F32),
-            VMEM((experts, LANES), F32),
+            VMEM((experts // 2, LANES), F32),
             pltpu.SemaphoreType.DMA((5,)),
             pltpu.SemaphoreType.DMA((TILES,)),
             pltpu.SemaphoreType.DMA((TILES,)),
@@ -289,32 +290,39 @@
 
 
 def owner_kernel(experts, keep_a, keep_b, recv, own_ref, stats_ref):
-    ranks = keep_a.shape[1]
-    own_ref[0, :ranks] = keep_a[0] + recv[0, :ranks]
-    block = keep_b[0] + recv[0, ranks:]
-    kinds = experts // 2 + 1
-    at = kinds * experts
-    stats = block[at : at + experts]
-    stats_ref[...] = stats
-    mine = jnp.broadcast_to(stats[:, :1], (experts, LANES))
-    total = jnp.zeros((experts, LANES), F32)
-    for step in range(1, kinds):
-        both = block[step * experts : (step + 1) * experts]
-        total = total + both * (mine - pltpu.roll(mine, experts - step, 0))
-        if 2 * step != experts:
+    count, ranks = keep_a.shape[:2]
+    half = experts // 2
+    at = (half + 1) * experts
+    lane = lax.broadcasted_iota(jnp.int32, (experts, LANES), 1)
+    shape = (half, LANES)
+    for spot in range(count):
+        own_ref[spot, :ranks] = keep_a[spot] + recv[spot, :ranks]
+        block = keep_b[spot] + recv[spot, ranks:]
+        stats = block[at - half : at]
+        first = jnp.broadcast_to(stats[:, :1], shape)
+        second = jnp.broadcast_to(stats[:, LANES // 4 : LANES // 4 + 1], shape)
+        mine = jnp.concatenate([first, second], axis=0)
+        if spot == 0:
+            stats_ref[...] = jnp.where(lane < LANES // 2, mine, stats[:1])
+        total = jnp.zeros((experts, LANES), F32)
+        for step in range(1, half):
+            both = block[step * experts : (step + 1) * experts]
+            total = total + both * (mine - pltpu.roll(mine, experts - step, 0))
             total = total + pltpu.roll(both, step, 0) * (mine - pltpu.roll(mine, step, 0))
-    scale = 2.0 * experts * 100.0 / stats[:, LANES - 1 :]
-    own_ref[0, ranks : ranks + experts] = block[:experts] + scale * total
-    own_ref[0, ranks + experts :] = block[at + experts :]
+        both = block[at - experts : at - half]
+        both = jnp.concatenate([both, both], axis=0)
+        total = total + both * (mine - pltpu.roll(mine, half, 0))
+        scale = 2.0 * experts * 100.0 / stats[:1, LANES - 1 :]
+        own_ref[spot, ranks : ranks + experts] = block[:experts] + scale * total
+        own_ref[spot, ranks + experts :] = block[at:]
 
 
 def owner_rows(keep_a, keep_b, recv, experts):
-    kinds = experts // 2 + 1
-    rows = recv.shape[1] - kinds * experts
+    rows = recv.shape[1] - experts // 2 * experts
     return pl.pallas_call(
         functools.partial(owner_kernel, experts),
         out_shape=[
-            jax.ShapeDtypeStruct((1, rows, LANES), F32),
+            jax.ShapeDtypeStruct((keep_a.shape[0], rows, LANES), F32),
             jax.ShapeDtypeStruct((experts, LANES), F32),
         ],
         compiler_params=pltpu.CompilerParams(vmem_limit_bytes=2 * MIB),
@@ -505,9 +513,12 @@
     filled = ()
     begin = 0
     for step in range(-1, bits):
-        if step >= depth:
+        if step >= depth - 1:
             keep_b = send_b = keep_b + recv_b
             keep_a = send_a = keep_a + recv_a
+            if step == depth - 1:
+                send_b = jnp.concatenate([send_b[1:], send_b[:1]], axis=0)
+                send_a = jnp.concatenate([send_a[1:], send_a[:1]], axis=0)
         elif step >= 0:
             keep_b, send_b = halve(keep_b, recv_b)
             keep_a, send_a = halve(keep_a, recv_a)
@@ -533,10 +544,10 @@
     filled = ()
     begin = 0
     tiles = tokens.shape[1] // (4 * LANES)
-    turns = tuple(reversed(range(depth)))
+    turns = tuple(reversed(range(depth - 1)))
     for turn, step in enumerate(turns):
         lefts, own, filled = lax.optimization_barrier((lefts, own, filled))
-        last = turn == depth - 1
+        last = turn == len(turns) - 1
         parts = tiles - begin if last else CHUNKS[turn]
         if parts:
             made = input_grads(masked, lefts, near, wide, experts, begin, parts, filled)
@@ -545,7 +556,7 @@
                 filled, lefts = (made[0],), (made[1],)
             else:
                 filled = (made,)
-        if turn == depth - 2:
+        if turn == len(turns) - 2:
             far = (swap(own, (1, 1)),)
             recv = swap(own, masks_g[step])
         else:

time: 90.9 us -> 85.8 us (0.944)
  waiting for transfers between devices: 29.4 us -> 25.6 us
  starting transfers between devices: 15.6 us -> 14.6 us
    ppermute x17 -> x16, waiting for transfers between devices: 29.4 us -> 25.6 us  [swap(): lax.ppermute(array, 'dp', [(i, i ^ masks[i & 1]) for i in range(size)])]
    ppermute x17 -> x16, starting transfers between devices: 15.6 us -> 14.6 us  [swap(): lax.ppermute(array, 'dp', [(i, i ^ masks[i & 1]) for i in range(size)])]
  transfers between devices with their start and end apart: 17 -> 16, of which waited for: 10 -> 9; matrix products, arithmetic and copies ran while one was open for 0% -> 0% of each run, Pallas kernels for 31% -> 32%
where the time goes in v4:
time: 85.8 us; the launch traced here: 85.7 us
  Pallas kernels  43.9 us (51%)
  waiting for transfers between devices  25.6 us (30%)
  starting transfers between devices  14.6 us (17%)
  between operations  0.99 us (1%)
    ppermute x16, waiting for transfers between devices, swap(): lax.ppermute(array, 'dp', [(i, i ^ masks[i & 1]) for i in range(size)])  25.6 us
    ppermute x16, starting transfers between devices, swap(): lax.ppermute(array, 'dp', [(i, i ^ masks[i & 1]) for i in range(size)])  14.6 us
    pallas_call x3, Pallas kernels, input_grads(): pl.pallas_call(functools.partial(input_kernel, experts, begin, first), ou...  14.5 us
    pallas_call x4, Pallas kernels, project(): pl.pallas_call(functools.partial(project_kernel, begin), out_shape=HBM((r...  13.3 us
    pallas_call x1, Pallas kernels, local_grads(): pl.pallas_call(functools.partial(local_kernel, orders_a, orders_b), out_s...  12.6 us
    pallas_call x1, Pallas kernels, clip_write(): pl.pallas_call(functools.partial(clip_kernel, orders, experts, limit), ou...  3.41 us
  transfers between devices with their start and end apart: 16, of which 9 were waited for; matrix products, arithmetic and copies ran while one was open for 0% of the time, Pallas kernels for 32%

profile of v4, /device:TPU:0, one launch (start us, length us, event | category | flops | bytes accessed | tf_op | source)
XLA Modules:
  0.0 85.7 jit_solution(17616962292430331431)
XLA Ops:
  0.7 12.6 %local_grads.1 = (f32[16,128,128]{2,1,0:T(8,128)S(1)}, f32[16,128,128]{2,1,0:T(8,128)S(1)}, f32[16,72,128]{2,1,0:T(8,128)S(1)}, f32[16,72,128]{2,1,0:T(8,128)S(1...) custom-call(s32[2]{0:T(128)S(1)} %pad_add_fusion.where_ref, ...), custom_call_target="tpu_custom_call" | custom-call | flops 4294967296 | bytes 10485760 | tf_op jit(solution)/shard_map/local_grads/pallas_call | solution.py:208
  13.3 0.6 collective-permute-start
  13.9 0.1 collective-permute-start.1
  14.0 3.3 %project.4.rest_0_ = bf16[1024,1024]{1,0:T(8,128)(2,1)} custom-call(bf16[1024,4096]{1,0:T(8,128)(2,1)S(1)} %get-tuple-element.80.tok, bf16[1024,128]{1,0:T(8,128)(2,1)S(1)} %get-tuple-element.103.weighted_ref, bf16[4096,1024]{1,0:T(8,128)(2,1)S(1)} %get-tuple-element.81.frozen.refs_5_.refs_2_, bf16[128,1024]{1,0:T(8,128)(2,1)S(1)} %get-tuple-element.82.up_ref), custom_call_target="tpu_custom_call" | custom-call | flops 2214592512 | bytes 11010048 | tf_op jit(solution)/shard_map/project/pallas_call | solution.py:272
  17.3 0.1 slice_add_fusion
  17.5 3.0 %collective-permute-start.2 = (f32[8,128,128]{2,1,0:T(8,128)S(1)}, f32[8,128,128]{2,1,0:T(8,128)S(1)}, u32[]{:S(2)}, u32[]{:S(2)}) collective-permute-start(f32[8,128,128]{2,1,0:T(8,128)S(1)} %get-tuple-element.88), channel_id=1, source_target_pairs={{0,2},{1,5},{2,0},{3,7},{4,6},{5,1},{6,4},{7,3},{8,10},{9,13},{10,... | collective-permute-start | bytes 1572872 | tf_op jit(solution)/shard_map/ppermute | solution.py:482
  20.4 1.6 %collective-permute-start.3 = (f32[8,72,128]{2,1,0:T(8,128)S(1)}, f32[8,72,128]{2,1,0:T(8,128)S(1)}, u32[]{:S(2)}, u32[]{:S(2)}) collective-permute-start(f32[8,72,128]{2,1,0:T(8,128)S(1)} %get-tuple-element.89), channel_id=1, source_target_pairs={{0,8},{1,9},{2,10},{3,11},{4,12},{5,13},{6,14},{7,15},{8,0},{9,1},... | collective-permute-start | bytes 884744 | tf_op jit(solution)/shard_map/ppermute | solution.py:482
  22.0 3.3 %project.5.rest_0_ = bf16[1024,1024]{1,0:T(8,128)(2,1)} custom-call(bf16[1024,4096]{1,0:T(8,128)(2,1)S(1)} %get-tuple-element.80.tok, bf16[1024,128]{1,0:T(8,128)(2,1)S(1)} %get-tuple-element.103.weighted_ref, bf16[4096,1024]{1,0:T(8,128)(2,1)S(1)} %get-tuple-element.81.frozen.refs_5_.refs_2_, ...), custom_call_target="tpu_custom_call", output_to_operand_aliasing={{}: (4, {})} | custom-call | flops 2214592512 | bytes 11010048 | tf_op jit(solution)/shard_map/project/pallas_call | solution.py:272
  25.3 3.9 %collective-permute-done.3 = f32[8,72,128]{2,1,0:T(8,128)S(1)} collective-permute-done((f32[8,72,128]{2,1,0:T(8,128)S(1)}, f32[8,72,128]{2,1,0:T(8,128)S(1)}, u32[]{:S(2)}, u32[]{:S(2)}) %collective-permute-start.3) | collective-permute-done | bytes 294944 | tf_op jit(solution)/shard_map/ppermute | solution.py:482
  29.3 0.5 collective-permute-start.4
  29.8 1.5 %collective-permute-start.5 = (f32[4,72,128]{2,1,0:T(8,128)S(1)}, f32[4,72,128]{2,1,0:T(8,128)S(1)}, u32[]{:S(2)}, u32[]{:S(2)}) collective-permute-start(f32[4,72,128]{2,1,0:T(8,128)S(1)} %get-tuple-element.96), channel_id=1, source_target_pairs={{0,2},{1,5},{2,0},{3,7},{4,6},{5,1},{6,4},{7,3},{8,10},{9,13},{10,... | collective-permute-start | bytes 442376 | tf_op jit(solution)/shard_map/ppermute | solution.py:482
  31.4 3.5 %project.6.rest_0_ = bf16[1024,1024]{1,0:T(8,128)(2,1)} custom-call(bf16[1024,4096]{1,0:T(8,128)(2,1)S(1)} %get-tuple-element.80.tok, bf16[1024,128]{1,0:T(8,128)(2,1)S(1)} %get-tuple-element.103.weighted_ref, bf16[4096,1024]{1,0:T(8,128)(2,1)S(1)} %get-tuple-element.81.frozen.refs_5_.refs_2_, ...), custom_call_target="tpu_custom_call", output_to_operand_aliasing={{}: (4, {})} | custom-call | flops 2214592512 | bytes 11010048 | tf_op jit(solution)/shard_map/project/pallas_call | solution.py:272
  34.8 0.9 %collective-permute-done.5 = f32[4,72,128]{2,1,0:T(8,128)S(1)} collective-permute-done((f32[4,72,128]{2,1,0:T(8,128)S(1)}, f32[4,72,128]{2,1,0:T(8,128)S(1)}, u32[]{:S(2)}, u32[]{:S(2)}) %collective-permute-start.5) | collective-permute-done | bytes 147488 | tf_op jit(solution)/shard_map/ppermute | solution.py:482
  35.7 1.5 %collective-permute-done.4 = f32[4,128,128]{2,1,0:T(8,128)S(1)} collective-permute-done((f32[4,128,128]{2,1,0:T(8,128)S(1)}, f32[4,128,128]{2,1,0:T(8,128)S(1)}, u32[]{:S(2)}, u32[]{:S(2)}) %collective-permute-start.4) | collective-permute-done | bytes 262176 | tf_op jit(solution)/shard_map/ppermute | solution.py:482
  37.2 1.8 %collective-permute-start.6 = (f32[2,128,128]{2,1,0:T(8,128)S(1)}, f32[2,128,128]{2,1,0:T(8,128)S(1)}, u32[]{:S(2)}, u32[]{:S(2)}) collective-permute-start(f32[2,128,128]{2,1,0:T(8,128)S(1)} %slice_add_fusion.9), channel_id=1, source_target_pairs={{0,8},{1,9},{2,10},{3,11},{4,12},{5,13},{6,14},{7,15},{8,0},{9,1},... | collective-permute-start | bytes 393224 | tf_op jit(solution)/shard_map/ppermute | solution.py:482
  39.0 0.4 collective-permute-start.7
  39.4 3.3 %project.7 = bf16[1024,1024]{1,0:T(8,128)(2,1)} custom-call(bf16[1024,4096]{1,0:T(8,128)(2,1)S(1)} %get-tuple-element.80.tok, bf16[1024,128]{1,0:T(8,128)(2,1)S(1)} %get-tuple-element.103.weighted_ref, bf16[4096,1024]{1,0:T(8,128)(2,1)S(1)} %get-tuple-element.81.frozen.refs_5_.refs_2_, ...), custom_call_target="tpu_custom_call", output_to_operand_aliasing={{}: (4, {})} | custom-call | flops 2214592512 | bytes 11010048 | tf_op jit(solution)/shard_map/project/pallas_call | solution.py:272
  42.7 0.6 collective-permute-done.7
  43.5 2.7 %collective-permute-start.8 = (f32[2,200,128]{2,1,0:T(8,128)S(1)}, f32[2,200,128]{2,1,0:T(8,128)S(1)}, u32[]{:S(2)}, u32[]{:S(2)}) collective-permute-start(f32[2,200,128]{2,1,0:T(8,128)S(1)} %maximum_maximum_fusion), channel_id=1, source_target_pairs={{0,16},{1,17},{2,18},{3,19},{4,20},{5,21},{6,22},{7,23},{8,24},{9,... | collective-permute-start | bytes 614408 | tf_op jit(solution)/shard_map/ppermute | solution.py:482
  46.1 8.1 %collective-permute-done.8.recv = f32[2,200,128]{2,1,0:T(8,128)S(1)} collective-permute-done((f32[2,200,128]{2,1,0:T(8,128)S(1)}, f32[2,200,128]{2,1,0:T(8,128)S(1)}, u32[]{:S(2)}, u32[]{:S(2)}) %collective-permute-start.8) | collective-permute-done | bytes 204832 | tf_op jit(solution)/shard_map/ppermute | solution.py:482
  54.3 0.1 owner_rows.1
  54.5 2.7 %input_grads.3 = (bf16[1024,4096]{1,0:T(8,128)(2,1)}, bf16[1024,256]{1,0:T(8,128)(2,1)S(1)}) custom-call(bf16[1024,1024]{1,0:T(8,128)(2,1)S(1)} %get-tuple-element.106.refs_0_, bf16[1024,128]{1,0:T(8,128)(2,1)S(1)} %get-tuple-element.114.refs_1_, f32[8,1024]{1,0:T(8,128)S(1)} %get-tuple-element.115.refs_2_, f32[8,1024]{1,0:T(8,128)S(1)} %get-tuple-element.116.refs_3_, ...), custom_call_target="tpu_custom_call" | custom-call | flops 1342177280 | bytes 4194304 | tf_op jit(solution)/shard_map/input_grads/pallas_call | solution.py:374
  57.1 3.4 %collective-permute-done.9 = f32[2,168,128]{2,1,0:T(8,128)S(1)} collective-permute-done((f32[2,168,128]{2,1,0:T(8,128)S(1)}, f32[2,168,128]{2,1,0:T(8,128)S(1)}, u32[]{:S(2)}, u32[]{:S(2)}) %collective-permute-start.9) | collective-permute-done | bytes 172064 | tf_op jit(solution)/shard_map/ppermute | solution.py:482
  60.7 3.9 %input_grads.4.refs_4_ = bf16[1024,4096]{1,0:T(8,128)(2,1)} custom-call(bf16[1024,1024]{1,0:T(8,128)(2,1)S(1)} %get-tuple-element.106.refs_0_, bf16[1024,256]{1,0:T(8,128)(2,1)S(1)} %get-tuple-element.130.refs_1_, bf16[4096,1024]{1,0:T(8,128)(2,1)S(1)} %get-tuple-element.81.frozen.refs_5_.refs_2_, ...), custom_call_target="tpu_custom_call", output_to_operand_aliasing={{}: (4, {})} | custom-call | flops 2684354560 | bytes 6291456 | tf_op jit(solution)/shard_map/input_grads/pallas_call | solution.py:374
  64.6 3.3 %collective-permute-done.10 = f32[4,168,128]{2,1,0:T(8,128)S(1)} collective-permute-done((f32[4,168,128]{2,1,0:T(8,128)S(1)}, f32[4,168,128]{2,1,0:T(8,128)S(1)}, u32[]{:S(2)}, u32[]{:S(2)}) %collective-permute-start.10) | collective-permute-done | bytes 344096 | tf_op jit(solution)/shard_map/ppermute | solution.py:482
  67.9 1.2 %collective-permute-start.11 = (f32[8,168,128]{2,1,0:T(8,128)S(1)}, f32[8,168,128]{2,1,0:T(8,128)S(1)}, u32[]{:S(2)}, u32[]{:S(2)}) collective-permute-start(f32[8,168,128]{2,1,0:T(8,128)S(1)} %pad_maximum_fusion.refs_0_), channel_id=1, source_target_pairs={{0,2},{1,5},{2,0},{3,7},{4,6},{5,1},{6,4},{7,3},{8,10},{9,13},{10,... | collective-permute-start | bytes 2064392 | tf_op jit(solution)/shard_map/ppermute | solution.py:482
  69.1 8.0 %input_grads.5 = bf16[1024,4096]{1,0:T(8,128)(2,1)} custom-call(bf16[1024,1024]{1,0:T(8,128)(2,1)S(1)} %get-tuple-element.106.refs_0_, bf16[1024,256]{1,0:T(8,128)(2,1)S(1)} %get-tuple-element.130.refs_1_, bf16[4096,1024]{1,0:T(8,128)(2,1)S(1)} %get-tuple-element.81.frozen.refs_5_.refs_2_, ...), custom_call_target="tpu_custom_call", output_to_operand_aliasing={{}: (4, {})} | custom-call | flops 6710886400 | bytes 12582912 | tf_op jit(solution)/shard_map/input_grads/pallas_call | solution.py:374
  77.1 1.8 %collective-permute-done.11.refs_1_ = f32[8,168,128]{2,1,0:T(8,128)S(1)} collective-permute-done((f32[8,168,128]{2,1,0:T(8,128)S(1)}, f32[8,168,128]{2,1,0:T(8,128)S(1)}, u32[]{:S(2)}, u32[]{:S(2)}) %collective-permute-start.11) | collective-permute-done | bytes 688160 | tf_op jit(solution)/shard_map/ppermute | solution.py:482
  78.9 0.5 collective-permute-start.12
  79.6 0.5 collective-permute-start.15
  80.1 2.0 %collective-permute-done.15.refs_6_ = f32[8,128]{1,0:T(8,128)S(1)} collective-permute-done((f32[8,128]{1,0:T(8,128)S(1)}, f32[8,128]{1,0:T(8,128)S(1)}, u32[]{:S(2)}, u32[]{:S(2)}) %collective-permute-start.15) | collective-permute-done | bytes 4128 | tf_op jit(solution)/shard_map/ppermute | solution.py:482
  82.1 3.4 %clip_write.1 = (f32[4096,128]{1,0:T(8,128)}, f32[128,1024]{1,0:T(8,128)}, f32[8,4096]{1,0:T(8,128)}, f32[8]{0:T(128)}, f32[1]{0:T(128)}) custom-call(s32[2]{0:T(128)S(1)} %pad_add_fusion.where_ref, f32[8,168,128]{2,1,0:T(8,128)S(1)} %pad_maximum_fusion.refs_0_, f32[8,168,128]{2,1,0:T(8,128)S(1)} %collective-permute-done.11.refs_1_, ...), custom_call_target="tpu_custom_call" | custom-call | tf_op jit(solution)/shard_map/clip_write/pallas_call | solution.py:456
  (25 shorter events, 0.7 us)
Async XLA Ops:
  13.3 3.9 %collective-permute-start = (f32[16,128,128]{2,1,0:T(8,128)S(1)}, f32[16,128,128]{2,1,0:T(8,128)S(1)}, u32[]{:S(2)}, u32[]{:S(2)}) collective-permute-start(f32[16,128,128]{2,1,0:T(8,128)S(1)} %get-tuple-element.78), channel_id=1, source_target_pairs={{0,1},{1,0},{2,3},{3,2},{4,5},{5,4},{6,7},{7,6},{8,9},{9,8},{10,11... | collective-permute-start | bytes 3145736 | tf_op jit(solution)/shard_map/ppermute | solution.py:482
  13.9 3.4 %collective-permute-start.1 = (f32[16,72,128]{2,1,0:T(8,128)S(1)}, f32[16,72,128]{2,1,0:T(8,128)S(1)}, u32[]{:S(2)}, u32[]{:S(2)}) collective-permute-start(f32[16,72,128]{2,1,0:T(8,128)S(1)} %get-tuple-element.79), channel_id=1, source_target_pairs={{0,1},{1,0},{2,3},{3,2},{4,5},{5,4},{6,7},{7,6},{8,9},{9,8},{10,11... | collective-permute-start | bytes 1769480 | tf_op jit(solution)/shard_map/ppermute | solution.py:482
  17.5 11.7 %collective-permute-start.2 = (f32[8,128,128]{2,1,0:T(8,128)S(1)}, f32[8,128,128]{2,1,0:T(8,128)S(1)}, u32[]{:S(2)}, u32[]{:S(2)}) collective-permute-start(f32[8,128,128]{2,1,0:T(8,128)S(1)} %get-tuple-element.88), channel_id=1, source_target_pairs={{0,2},{1,5},{2,0},{3,7},{4,6},{5,1},{6,4},{7,3},{8,10},{9,13},{10,... | collective-permute-start | bytes 1572872 | tf_op jit(solution)/shard_map/ppermute | solution.py:482
  20.4 8.7 %collective-permute-start.3 = (f32[8,72,128]{2,1,0:T(8,128)S(1)}, f32[8,72,128]{2,1,0:T(8,128)S(1)}, u32[]{:S(2)}, u32[]{:S(2)}) collective-permute-start(f32[8,72,128]{2,1,0:T(8,128)S(1)} %get-tuple-element.89), channel_id=1, source_target_pairs={{0,8},{1,9},{2,10},{3,11},{4,12},{5,13},{6,14},{7,15},{8,0},{9,1},... | collective-permute-start | bytes 884744 | tf_op jit(solution)/shard_map/ppermute | solution.py:482
  29.3 7.9 %collective-permute-start.4 = (f32[4,128,128]{2,1,0:T(8,128)S(1)}, f32[4,128,128]{2,1,0:T(8,128)S(1)}, u32[]{:S(2)}, u32[]{:S(2)}) collective-permute-start(f32[4,128,128]{2,1,0:T(8,128)S(1)} %get-tuple-element.95), channel_id=1, source_target_pairs={{0,4},{1,3},{2,6},{3,1},{4,0},{5,7},{6,2},{7,5},{8,12},{9,11},{10,... | collective-permute-start | bytes 786440 | tf_op jit(solution)/shard_map/ppermute | solution.py:482
  29.8 5.9 %collective-permute-start.5 = (f32[4,72,128]{2,1,0:T(8,128)S(1)}, f32[4,72,128]{2,1,0:T(8,128)S(1)}, u32[]{:S(2)}, u32[]{:S(2)}) collective-permute-start(f32[4,72,128]{2,1,0:T(8,128)S(1)} %get-tuple-element.96), channel_id=1, source_target_pairs={{0,2},{1,5},{2,0},{3,7},{4,6},{5,1},{6,4},{7,3},{8,10},{9,13},{10,... | collective-permute-start | bytes 442376 | tf_op jit(solution)/shard_map/ppermute | solution.py:482
  37.2 6.2 %collective-permute-start.6 = (f32[2,128,128]{2,1,0:T(8,128)S(1)}, f32[2,128,128]{2,1,0:T(8,128)S(1)}, u32[]{:S(2)}, u32[]{:S(2)}) collective-permute-start(f32[2,128,128]{2,1,0:T(8,128)S(1)} %slice_add_fusion.9), channel_id=1, source_target_pairs={{0,8},{1,9},{2,10},{3,11},{4,12},{5,13},{6,14},{7,15},{8,0},{9,1},... | collective-permute-start | bytes 393224 | tf_op jit(solution)/shard_map/ppermute | solution.py:482
  39.0 4.4 %collective-permute-start.7 = (f32[2,72,128]{2,1,0:T(8,128)S(1)}, f32[2,72,128]{2,1,0:T(8,128)S(1)}, u32[]{:S(2)}, u32[]{:S(2)}) collective-permute-start(f32[2,72,128]{2,1,0:T(8,128)S(1)} %slice_add_fusion.11), channel_id=1, source_target_pairs={{0,4},{1,3},{2,6},{3,1},{4,0},{5,7},{6,2},{7,5},{8,12},{9,11},{10,... | collective-permute-start | bytes 221192 | tf_op jit(solution)/shard_map/ppermute | solution.py:482
  43.5 10.8 %collective-permute-start.8 = (f32[2,200,128]{2,1,0:T(8,128)S(1)}, f32[2,200,128]{2,1,0:T(8,128)S(1)}, u32[]{:S(2)}, u32[]{:S(2)}) collective-permute-start(f32[2,200,128]{2,1,0:T(8,128)S(1)} %maximum_maximum_fusion), channel_id=1, source_target_pairs={{0,16},{1,17},{2,18},{3,19},{4,20},{5,21},{6,22},{7,23},{8,24},{9,... | collective-permute-start | bytes 614408 | tf_op jit(solution)/shard_map/ppermute | solution.py:482
  54.4 6.1 %collective-permute-start.9 = (f32[2,168,128]{2,1,0:T(8,128)S(1)}, f32[2,168,128]{2,1,0:T(8,128)S(1)}, u32[]{:S(2)}, u32[]{:S(2)}) collective-permute-start(f32[2,168,128]{2,1,0:T(8,128)S(1)} %get-tuple-element.120), channel_id=1, source_target_pairs={{0,8},{1,9},{2,10},{3,11},{4,12},{5,13},{6,14},{7,15},{8,0},{9,1},... | collective-permute-start | bytes 516104 | tf_op jit(solution)/shard_map/ppermute | solution.py:482
  60.6 7.3 %collective-permute-start.10 = (f32[4,168,128]{2,1,0:T(8,128)S(1)}, f32[4,168,128]{2,1,0:T(8,128)S(1)}, u32[]{:S(2)}, u32[]{:S(2)}) collective-permute-start(f32[4,168,128]{2,1,0:T(8,128)S(1)} %pad_maximum_fusion.1), channel_id=1, source_target_pairs={{0,4},{1,3},{2,6},{3,1},{4,0},{5,7},{6,2},{7,5},{8,12},{9,11},{10,... | collective-permute-start | bytes 1032200 | tf_op jit(solution)/shard_map/ppermute | solution.py:482
  67.9 11.0 %collective-permute-start.11 = (f32[8,168,128]{2,1,0:T(8,128)S(1)}, f32[8,168,128]{2,1,0:T(8,128)S(1)}, u32[]{:S(2)}, u32[]{:S(2)}) collective-permute-start(f32[8,168,128]{2,1,0:T(8,128)S(1)} %pad_maximum_fusion.refs_0_), channel_id=1, source_target_pairs={{0,2},{1,5},{2,0},{3,7},{4,6},{5,1},{6,4},{7,3},{8,10},{9,13},{10,... | collective-permute-start | bytes 2064392 | tf_op jit(solution)/shard_map/ppermute | solution.py:482
  78.9 3.1 %collective-permute-start.14 = (f32[8,168,128]{2,1,0:T(8,128)S(1)}, f32[8,168,128]{2,1,0:T(8,128)S(1)}, u32[]{:S(2)}, u32[]{:S(2)}) collective-permute-start(f32[8,168,128]{2,1,0:T(8,128)S(1)} %collective-permute-done.11.refs_1_), channel_id=1, source_target_pairs={{0,1},{1,0},{2,3},{3,2},{4,5},{5,4},{6,7},{7,6},{8,9},{9,8},{10,11... | collective-permute-start | bytes 2064392 | tf_op jit(solution)/shard_map/ppermute | solution.py:482
  78.9 3.1 %collective-permute-start.12 = (f32[4,168,128]{2,1,0:T(8,128)S(1)}, f32[4,168,128]{2,1,0:T(8,128)S(1)}, u32[]{:S(2)}, u32[]{:S(2)}) collective-permute-start(f32[4,168,128]{2,1,0:T(8,128)S(1)} %pad_maximum_fusion.1), channel_id=1, source_target_pairs={{0,1},{1,0},{2,3},{3,2},{4,5},{5,4},{6,7},{7,6},{8,9},{9,8},{10,11... | collective-permute-start | bytes 1032200 | tf_op jit(solution)/shard_map/ppermute | solution.py:482
  79.5 2.6 %collective-permute-start.13 = (f32[4,168,128]{2,1,0:T(8,128)S(1)}, f32[4,168,128]{2,1,0:T(8,128)S(1)}, u32[]{:S(2)}, u32[]{:S(2)}) collective-permute-start(f32[4,168,128]{2,1,0:T(8,128)S(1)} %slice.115), channel_id=1, source_target_pairs={{0,1},{1,0},{2,3},{3,2},{4,5},{5,4},{6,7},{7,6},{8,9},{9,8},{10,11... | collective-permute-start | bytes 1032200 | tf_op jit(solution)/shard_map/ppermute | solution.py:482
  79.6 2.5 %collective-permute-start.15 = (f32[8,128]{1,0:T(8,128)S(1)}, f32[8,128]{1,0:T(8,128)S(1)}, u32[]{:S(2)}, u32[]{:S(2)}) collective-permute-start(f32[8,128]{1,0:T(8,128)S(1)} %get-tuple-element.117.refs_4_.refs_5_), channel_id=1, source_target_pairs={{0,1},{1,0},{2,3},{3,2},{4,5},{5,4},{6,7},{7,6},{8,9},{9,8},{10,11... | collective-permute-start | bytes 12296 | tf_op jit(solution)/shard_map/ppermute | solution.py:482

commit v5 on v4

--- a/solution.py
+++ b/solution.py
@@ -53,7 +53,7 @@
 def local_kernel(
     orders_a, orders_b, where_ref, ids_hbm, gate_hbm, down_hbm, up_hbm, tok_hbm, ups_hbm, frozen_hbm,
     keep_a, send_a, keep_b, send_b, weighted_ref, lowgrad_ref, plain_ref, share_ref, wide_ref, ups,
-    tok, up, frozen, ids, gate, down, both, back, left_t, weighted_t, grad_up, stats, sem, tok_sem, ups_sem,
+    tok, up, frozen, ids, gate, down, both, left_t, weighted_t, grad_up, stats, sem, tok_sem, ups_sem,
 ):
     rows, width = tok.shape
     experts, ranks = gate.shape[0], down.shape[1]
@@ -81,6 +81,7 @@
     up_copy.start()
     for t in range(TILES):
         tok_copy(t).start()
+        ups_copy(t).start()
     frozen_copy = fetch(frozen_hbm, frozen, sem.at[4])
     mine, side = where_ref[0], where_ref[1]
     row_i = lax.broadcasted_iota(jnp.int32, (experts, ranks), 0)
@@ -90,69 +91,72 @@
     wide_ref[:, ranks:] = nn(gate[...].astype(F32).T.astype(BF16), twice).astype(BF16)
     down_copy.wait()
     wide_ref[:, :ranks] = down[...]
-    for t in range(TILES):
-        part = pl.ds(t * tile, tile)
-        tok_copy(t).wait()
-        if t == 1:
-            for later in range(TILES):
-                ups_copy(later).start()
-        if t == TILES - 1:
-            frozen_copy.start()
-        both[part, :] = nn(tok[part, :], wide_ref[...])
     ids_copy.wait()
     count = jnp.sum((ids[...] != 0).astype(jnp.int32))
     up_copy.wait()
-    for t in range(TILES):
-        part = pl.ds(t * tile, tile)
-        ups_copy(t).wait()
-        live = lax.broadcasted_iota(jnp.int32, (tile, 1), 0) + t * tile < count
-        ups[part, :] = ups[part, :] * live.astype(F32).astype(BF16)
-    back[...] = nt(ups[...], up[...])
-    logits = both[:, ranks:].T[:experts, :]
-    shifted = logits - jnp.max(logits, axis=0, keepdims=True)
-    powers = jnp.exp(shifted)
-    total = jnp.sum(powers, axis=0, keepdims=True)
-    prob = powers / total
-    logp = shifted - jnp.log(total)
-    ent = -jnp.sum(prob * logp, axis=0, keepdims=True)
-    alive = (lax.broadcasted_iota(jnp.int32, (1, rows), 1) < count).astype(F32)
-    share = alive * prob
-    share_ref[...] = share
-    big, rest = split(prob)
-    mid, small = split(rest)
-    parts = jnp.concatenate([big, mid, small], axis=0).T.astype(BF16)
     row_p = lax.broadcasted_iota(jnp.int32, (3 * experts, ranks), 0)
     col_p = lax.broadcasted_iota(jnp.int32, (3 * experts, ranks), 1)
     spread_by = (row_p % experts == col_p // rank).astype(BF16)
     row_g = lax.broadcasted_iota(jnp.int32, (experts, 2 * ranks), 0)
     col_g = lax.broadcasted_iota(jnp.int32, (experts, 2 * ranks), 1)
     group = ((col_g % ranks) // rank == row_g).astype(BF16)
-    tasks = []
-    for t in range(TILES):
+    kinds = experts // 2 + 1
+
+    def finish(t):
         part = pl.ds(t * tile, tile)
-        spread = nn(parts[t * tile : (t + 1) * tile], spread_by)
+        live = lax.broadcasted_iota(jnp.int32, (tile, 1), 0) + t * tile < count
+        masked = ups[part, :] * live.astype(F32).astype(BF16)
+        ups[part, :] = masked
+        back = nt(masked, up[...])
+        logits = both[part, ranks:].T[:experts, :]
+        shifted = logits - jnp.max(logits, axis=0, keepdims=True)
+        powers = jnp.exp(shifted)
+        total = jnp.sum(powers, axis=0, keepdims=True)
+        prob = powers / total
+        logp = shifted - jnp.log(total)
+        ent = -jnp.sum(prob * logp, axis=0, keepdims=True)
+        alive = (lax.broadcasted_iota(jnp.int32, (1, tile), 1) + t * tile < count).astype(F32)
+        share = alive * prob
+        share_ref[:, part] = share
+        big, rest = split(prob)
+        mid, small = split(rest)
+        parts = jnp.concatenate([big, mid, small], axis=0).T.astype(BF16)
+        spread = nn(parts, spread_by)
         low = both[part, :ranks].astype(BF16).astype(F32)
         weighted = (low * spread).astype(BF16)
         weighted_ref[part, :] = weighted
         weighted_t[:, part] = weighted.astype(F32).T.astype(BF16)
-        low_grad = (2.0 * spread * back[part, :]).astype(BF16)
+        low_grad = (2.0 * spread * back).astype(BF16)
         lowgrad_ref[part, :] = low_grad
         left_t[:ranks, part] = low_grad.astype(F32).T.astype(BF16)
-        big, small = split(low * back[part, :])
-        tasks.append(nt(group, jnp.concatenate([big, small], axis=1).astype(BF16)))
+        big, small = split(low * back)
+        task = 2.0 * nt(group, jnp.concatenate([big, small], axis=1).astype(BF16))
+        inner = jnp.sum(prob * task, axis=0, keepdims=True)
+        plain = prob * (task - inner) + 50.0 * share * (logp + ent)
+        plain_ref[:, part] = plain
+        for kind in range(kinds):
+            value = plain if kind == 0 else share * pltpu.roll(prob, experts - kind, 0)
+            big, small = split(value)
+            at = pl.ds(ranks + 2 * kind * experts, 2 * experts)
+            left_t[at, part] = jnp.concatenate([big, small], axis=0).astype(BF16)
+        return jnp.sum(share, axis=1, keepdims=True), jnp.sum(alive * ent, axis=1, keepdims=True)
+
+    load = jnp.zeros((experts, 1), F32)
+    entropy = jnp.zeros((1, 1), F32)
+    for t in range(TILES + 1):
+        if t < TILES:
+            tok_copy(t).wait()
+        if t > 0:
+            ups_copy(t - 1).wait()
+        if t == TILES - 1:
+            frozen_copy.start()
+        if t < TILES:
+            part = pl.ds(t * tile, tile)
+            both[part, :] = nn(tok[part, :], wide_ref[...])
+        if t > 0:
+            more = finish(t - 1)
+            load, entropy = load + more[0], entropy + more[1]
     grad_up[...] = 2.0 * nn(weighted_t[...], ups[...])
-    task = 2.0 * jnp.concatenate(tasks, axis=1)
-    inner = jnp.sum(prob * task, axis=0, keepdims=True)
-    plain = prob * (task - inner) + 50.0 * share * (logp + ent)
-    plain_ref[...] = plain
-    kinds = experts // 2 + 1
-    for kind in range(kinds):
-        value = plain if kind == 0 else share * pltpu.roll(prob, experts - kind, 0)
-        big, small = split(value)
-        at = pl.ds(ranks + 2 * kind * experts, 2 * experts)
-        left_t[at, :] = jnp.concatenate([big, small], axis=0).astype(BF16)
-    load = jnp.sum(share, axis=1, keepdims=True)
-    entropy = jnp.sum(alive * ent, axis=1, keepdims=True)
     half = experts // 2
     lane = lax.broadcasted_iota(jnp.int32, (half, LANES), 1)
     pair_load = jnp.where(lane < LANES // 4, load[:half], load[half:])
@@ -229,7 +233,6 @@
             VMEM((experts, width), BF16),
             VMEM((width, ranks), BF16),
             VMEM((rows, 2 * ranks), F32),
-            VMEM((rows, ranks), F32),
             VMEM((2 * ranks, rows), BF16),
             VMEM((ranks, rows), BF16),
             VMEM((ranks, outs), F32),

time: 85.8 us -> 85.2 us (level)
  transfers between devices with their start and end apart: 16 -> 16, of which waited for: 9 -> 9; matrix products, arithmetic and copies ran while one was open for 0% -> 0% of each run, Pallas kernels for 32% -> 33%
where the time goes in v5:
time: 85.2 us; the launch traced here: 85 us
  Pallas kernels  43.3 us (51%)
  waiting for transfers between devices  25.6 us (30%)
  starting transfers between devices  14.6 us (17%)
  between operations  0.99 us (1%)
    ppermute x16, waiting for transfers between devices, swap(): lax.ppermute(array, 'dp', [(i, i ^ masks[i & 1]) for i in range(size)])  25.6 us
    ppermute x16, starting transfers between devices, swap(): lax.ppermute(array, 'dp', [(i, i ^ masks[i & 1]) for i in range(size)])  14.6 us
    pallas_call x3, Pallas kernels, input_grads(): pl.pallas_call(functools.partial(input_kernel, experts, begin, first), ou...  14.5 us
    pallas_call x4, Pallas kernels, project(): pl.pallas_call(functools.partial(project_kernel, begin), out_shape=HBM((r...  13.3 us
    pallas_call x1, Pallas kernels, local_grads(): pl.pallas_call(functools.partial(local_kernel, orders_a, orders_b), out_s...  12 us
    pallas_call x1, Pallas kernels, clip_write(): pl.pallas_call(functools.partial(clip_kernel, orders, experts, limit), ou...  3.41 us
  transfers between devices with their start and end apart: 16, of which 9 were waited for; matrix products, arithmetic and copies ran while one was open for 0% of the time, Pallas kernels for 33%

profile of v5, /device:TPU:0, one launch (start us, length us, event | category | flops | bytes accessed | tf_op | source)
XLA Modules:
  0.0 85.0 jit_solution(12294187026859365577)
XLA Ops:
  0.7 12.0 %local_grads.1 = (f32[16,128,128]{2,1,0:T(8,128)S(1)}, f32[16,128,128]{2,1,0:T(8,128)S(1)}, f32[16,72,128]{2,1,0:T(8,128)S(1)}, f32[16,72,128]{2,1,0:T(8,128)S(1...) custom-call(s32[2]{0:T(128)S(1)} %pad_add_fusion.where_ref, ...), custom_call_target="tpu_custom_call" | custom-call | flops 4294967296 | bytes 10485760 | tf_op jit(solution)/shard_map/local_grads/pallas_call | solution.py:212
  12.7 0.6 collective-permute-start
  13.3 0.1 collective-permute-start.1
  13.3 3.3 %project.4.rest_0_ = bf16[1024,1024]{1,0:T(8,128)(2,1)} custom-call(bf16[1024,4096]{1,0:T(8,128)(2,1)S(1)} %get-tuple-element.80.tok, bf16[1024,128]{1,0:T(8,128)(2,1)S(1)} %get-tuple-element.103.weighted_ref, bf16[4096,1024]{1,0:T(8,128)(2,1)S(1)} %get-tuple-element.81.frozen.refs_5_.refs_2_, bf16[128,1024]{1,0:T(8,128)(2,1)S(1)} %get-tuple-element.82.up_ref), custom_call_target="tpu_custom_call" | custom-call | flops 2214592512 | bytes 11010048 | tf_op jit(solution)/shard_map/project/pallas_call | solution.py:275
  16.7 0.1 slice_add_fusion
  16.8 3.0 %collective-permute-start.2 = (f32[8,128,128]{2,1,0:T(8,128)S(1)}, f32[8,128,128]{2,1,0:T(8,128)S(1)}, u32[]{:S(2)}, u32[]{:S(2)}) collective-permute-start(f32[8,128,128]{2,1,0:T(8,128)S(1)} %get-tuple-element.88), channel_id=1, source_target_pairs={{0,2},{1,5},{2,0},{3,7},{4,6},{5,1},{6,4},{7,3},{8,10},{9,13},{10,... | collective-permute-start | bytes 1572872 | tf_op jit(solution)/shard_map/ppermute | solution.py:485
  19.8 1.6 %collective-permute-start.3 = (f32[8,72,128]{2,1,0:T(8,128)S(1)}, f32[8,72,128]{2,1,0:T(8,128)S(1)}, u32[]{:S(2)}, u32[]{:S(2)}) collective-permute-start(f32[8,72,128]{2,1,0:T(8,128)S(1)} %get-tuple-element.89), channel_id=1, source_target_pairs={{0,8},{1,9},{2,10},{3,11},{4,12},{5,13},{6,14},{7,15},{8,0},{9,1},... | collective-permute-start | bytes 884744 | tf_op jit(solution)/shard_map/ppermute | solution.py:485
  21.4 3.3 %project.5.rest_0_ = bf16[1024,1024]{1,0:T(8,128)(2,1)} custom-call(bf16[1024,4096]{1,0:T(8,128)(2,1)S(1)} %get-tuple-element.80.tok, bf16[1024,128]{1,0:T(8,128)(2,1)S(1)} %get-tuple-element.103.weighted_ref, bf16[4096,1024]{1,0:T(8,128)(2,1)S(1)} %get-tuple-element.81.frozen.refs_5_.refs_2_, ...), custom_call_target="tpu_custom_call", output_to_operand_aliasing={{}: (4, {})} | custom-call | flops 2214592512 | bytes 11010048 | tf_op jit(solution)/shard_map/project/pallas_call | solution.py:275
  24.7 3.9 %collective-permute-done.3 = f32[8,72,128]{2,1,0:T(8,128)S(1)} collective-permute-done((f32[8,72,128]{2,1,0:T(8,128)S(1)}, f32[8,72,128]{2,1,0:T(8,128)S(1)}, u32[]{:S(2)}, u32[]{:S(2)}) %collective-permute-start.3) | collective-permute-done | bytes 294944 | tf_op jit(solution)/shard_map/ppermute | solution.py:485
  28.7 0.5 collective-permute-start.4
  29.2 1.5 %collective-permute-start.5 = (f32[4,72,128]{2,1,0:T(8,128)S(1)}, f32[4,72,128]{2,1,0:T(8,128)S(1)}, u32[]{:S(2)}, u32[]{:S(2)}) collective-permute-start(f32[4,72,128]{2,1,0:T(8,128)S(1)} %get-tuple-element.96), channel_id=1, source_target_pairs={{0,2},{1,5},{2,0},{3,7},{4,6},{5,1},{6,4},{7,3},{8,10},{9,13},{10,... | collective-permute-start | bytes 442376 | tf_op jit(solution)/shard_map/ppermute | solution.py:485
  30.7 3.5 %project.6.rest_0_ = bf16[1024,1024]{1,0:T(8,128)(2,1)} custom-call(bf16[1024,4096]{1,0:T(8,128)(2,1)S(1)} %get-tuple-element.80.tok, bf16[1024,128]{1,0:T(8,128)(2,1)S(1)} %get-tuple-element.103.weighted_ref, bf16[4096,1024]{1,0:T(8,128)(2,1)S(1)} %get-tuple-element.81.frozen.refs_5_.refs_2_, ...), custom_call_target="tpu_custom_call", output_to_operand_aliasing={{}: (4, {})} | custom-call | flops 2214592512 | bytes 11010048 | tf_op jit(solution)/shard_map/project/pallas_call | solution.py:275
  34.2 0.9 %collective-permute-done.5 = f32[4,72,128]{2,1,0:T(8,128)S(1)} collective-permute-done((f32[4,72,128]{2,1,0:T(8,128)S(1)}, f32[4,72,128]{2,1,0:T(8,128)S(1)}, u32[]{:S(2)}, u32[]{:S(2)}) %collective-permute-start.5) | collective-permute-done | bytes 147488 | tf_op jit(solution)/shard_map/ppermute | solution.py:485
  35.1 1.5 %collective-permute-done.4 = f32[4,128,128]{2,1,0:T(8,128)S(1)} collective-permute-done((f32[4,128,128]{2,1,0:T(8,128)S(1)}, f32[4,128,128]{2,1,0:T(8,128)S(1)}, u32[]{:S(2)}, u32[]{:S(2)}) %collective-permute-start.4) | collective-permute-done | bytes 262176 | tf_op jit(solution)/shard_map/ppermute | solution.py:485
  36.6 1.8 %collective-permute-start.6 = (f32[2,128,128]{2,1,0:T(8,128)S(1)}, f32[2,128,128]{2,1,0:T(8,128)S(1)}, u32[]{:S(2)}, u32[]{:S(2)}) collective-permute-start(f32[2,128,128]{2,1,0:T(8,128)S(1)} %slice_add_fusion.9), channel_id=1, source_target_pairs={{0,8},{1,9},{2,10},{3,11},{4,12},{5,13},{6,14},{7,15},{8,0},{9,1},... | collective-permute-start | bytes 393224 | tf_op jit(solution)/shard_map/ppermute | solution.py:485
  38.4 0.5 collective-permute-start.7
  38.8 3.3 %project.7 = bf16[1024,1024]{1,0:T(8,128)(2,1)} custom-call(bf16[1024,4096]{1,0:T(8,128)(2,1)S(1)} %get-tuple-element.80.tok, bf16[1024,128]{1,0:T(8,128)(2,1)S(1)} %get-tuple-element.103.weighted_ref, bf16[4096,1024]{1,0:T(8,128)(2,1)S(1)} %get-tuple-element.81.frozen.refs_5_.refs_2_, ...), custom_call_target="tpu_custom_call", output_to_operand_aliasing={{}: (4, {})} | custom-call | flops 2214592512 | bytes 11010048 | tf_op jit(solution)/shard_map/project/pallas_call | solution.py:275
  42.1 0.6 collective-permute-done.7
  42.8 2.7 %collective-permute-start.8 = (f32[2,200,128]{2,1,0:T(8,128)S(1)}, f32[2,200,128]{2,1,0:T(8,128)S(1)}, u32[]{:S(2)}, u32[]{:S(2)}) collective-permute-start(f32[2,200,128]{2,1,0:T(8,128)S(1)} %maximum_maximum_fusion), channel_id=1, source_target_pairs={{0,16},{1,17},{2,18},{3,19},{4,20},{5,21},{6,22},{7,23},{8,24},{9,... | collective-permute-start | bytes 614408 | tf_op jit(solution)/shard_map/ppermute | solution.py:485
  45.5 8.1 %collective-permute-done.8.recv = f32[2,200,128]{2,1,0:T(8,128)S(1)} collective-permute-done((f32[2,200,128]{2,1,0:T(8,128)S(1)}, f32[2,200,128]{2,1,0:T(8,128)S(1)}, u32[]{:S(2)}, u32[]{:S(2)}) %collective-permute-start.8) | collective-permute-done | bytes 204832 | tf_op jit(solution)/shard_map/ppermute | solution.py:485
  53.6 0.1 owner_rows.1
  53.8 2.7 %input_grads.3 = (bf16[1024,4096]{1,0:T(8,128)(2,1)}, bf16[1024,256]{1,0:T(8,128)(2,1)S(1)}) custom-call(bf16[1024,1024]{1,0:T(8,128)(2,1)S(1)} %get-tuple-element.106.refs_0_, bf16[1024,128]{1,0:T(8,128)(2,1)S(1)} %get-tuple-element.114.refs_1_, f32[8,1024]{1,0:T(8,128)S(1)} %get-tuple-element.115.refs_2_, f32[8,1024]{1,0:T(8,128)S(1)} %get-tuple-element.116.refs_3_, ...), custom_call_target="tpu_custom_call" | custom-call | flops 1342177280 | bytes 4194304 | tf_op jit(solution)/shard_map/input_grads/pallas_call | solution.py:377
  56.5 3.4 %collective-permute-done.9 = f32[2,168,128]{2,1,0:T(8,128)S(1)} collective-permute-done((f32[2,168,128]{2,1,0:T(8,128)S(1)}, f32[2,168,128]{2,1,0:T(8,128)S(1)}, u32[]{:S(2)}, u32[]{:S(2)}) %collective-permute-start.9) | collective-permute-done | bytes 172064 | tf_op jit(solution)/shard_map/ppermute | solution.py:485
  60.0 3.9 %input_grads.4.refs_4_ = bf16[1024,4096]{1,0:T(8,128)(2,1)} custom-call(bf16[1024,1024]{1,0:T(8,128)(2,1)S(1)} %get-tuple-element.106.refs_0_, bf16[1024,256]{1,0:T(8,128)(2,1)S(1)} %get-tuple-element.130.refs_1_, bf16[4096,1024]{1,0:T(8,128)(2,1)S(1)} %get-tuple-element.81.frozen.refs_5_.refs_2_, ...), custom_call_target="tpu_custom_call", output_to_operand_aliasing={{}: (4, {})} | custom-call | flops 2684354560 | bytes 6291456 | tf_op jit(solution)/shard_map/input_grads/pallas_call | solution.py:377
  63.9 3.3 %collective-permute-done.10 = f32[4,168,128]{2,1,0:T(8,128)S(1)} collective-permute-done((f32[4,168,128]{2,1,0:T(8,128)S(1)}, f32[4,168,128]{2,1,0:T(8,128)S(1)}, u32[]{:S(2)}, u32[]{:S(2)}) %collective-permute-start.10) | collective-permute-done | bytes 344096 | tf_op jit(solution)/shard_map/ppermute | solution.py:485
  67.3 1.2 %collective-permute-start.11 = (f32[8,168,128]{2,1,0:T(8,128)S(1)}, f32[8,168,128]{2,1,0:T(8,128)S(1)}, u32[]{:S(2)}, u32[]{:S(2)}) collective-permute-start(f32[8,168,128]{2,1,0:T(8,128)S(1)} %pad_maximum_fusion.refs_0_), channel_id=1, source_target_pairs={{0,2},{1,5},{2,0},{3,7},{4,6},{5,1},{6,4},{7,3},{8,10},{9,13},{10,... | collective-permute-start | bytes 2064392 | tf_op jit(solution)/shard_map/ppermute | solution.py:485
  68.5 8.0 %input_grads.5 = bf16[1024,4096]{1,0:T(8,128)(2,1)} custom-call(bf16[1024,1024]{1,0:T(8,128)(2,1)S(1)} %get-tuple-element.106.refs_0_, bf16[1024,256]{1,0:T(8,128)(2,1)S(1)} %get-tuple-element.130.refs_1_, bf16[4096,1024]{1,0:T(8,128)(2,1)S(1)} %get-tuple-element.81.frozen.refs_5_.refs_2_, ...), custom_call_target="tpu_custom_call", output_to_operand_aliasing={{}: (4, {})} | custom-call | flops 6710886400 | bytes 12582912 | tf_op jit(solution)/shard_map/input_grads/pallas_call | solution.py:377
  76.5 1.8 %collective-permute-done.11.refs_1_ = f32[8,168,128]{2,1,0:T(8,128)S(1)} collective-permute-done((f32[8,168,128]{2,1,0:T(8,128)S(1)}, f32[8,168,128]{2,1,0:T(8,128)S(1)}, u32[]{:S(2)}, u32[]{:S(2)}) %collective-permute-start.11) | collective-permute-done | bytes 688160 | tf_op jit(solution)/shard_map/ppermute | solution.py:485
  78.3 0.5 collective-permute-start.12
  78.9 0.5 collective-permute-start.15
  79.4 2.0 %collective-permute-done.15.refs_6_ = f32[8,128]{1,0:T(8,128)S(1)} collective-permute-done((f32[8,128]{1,0:T(8,128)S(1)}, f32[8,128]{1,0:T(8,128)S(1)}, u32[]{:S(2)}, u32[]{:S(2)}) %collective-permute-start.15) | collective-permute-done | bytes 4128 | tf_op jit(solution)/shard_map/ppermute | solution.py:485
  81.5 3.4 %clip_write.1 = (f32[4096,128]{1,0:T(8,128)}, f32[128,1024]{1,0:T(8,128)}, f32[8,4096]{1,0:T(8,128)}, f32[8]{0:T(128)}, f32[1]{0:T(128)}) custom-call(s32[2]{0:T(128)S(1)} %pad_add_fusion.where_ref, f32[8,168,128]{2,1,0:T(8,128)S(1)} %pad_maximum_fusion.refs_0_, f32[8,168,128]{2,1,0:T(8,128)S(1)} %collective-permute-done.11.refs_1_, ...), custom_call_target="tpu_custom_call" | custom-call | tf_op jit(solution)/shard_map/clip_write/pallas_call | solution.py:459
  (25 shorter events, 0.7 us)
Async XLA Ops:
  12.7 3.9 %collective-permute-start = (f32[16,128,128]{2,1,0:T(8,128)S(1)}, f32[16,128,128]{2,1,0:T(8,128)S(1)}, u32[]{:S(2)}, u32[]{:S(2)}) collective-permute-start(f32[16,128,128]{2,1,0:T(8,128)S(1)} %get-tuple-element.78), channel_id=1, source_target_pairs={{0,1},{1,0},{2,3},{3,2},{4,5},{5,4},{6,7},{7,6},{8,9},{9,8},{10,11... | collective-permute-start | bytes 3145736 | tf_op jit(solution)/shard_map/ppermute | solution.py:485
  13.3 3.4 %collective-permute-start.1 = (f32[16,72,128]{2,1,0:T(8,128)S(1)}, f32[16,72,128]{2,1,0:T(8,128)S(1)}, u32[]{:S(2)}, u32[]{:S(2)}) collective-permute-start(f32[16,72,128]{2,1,0:T(8,128)S(1)} %get-tuple-element.79), channel_id=1, source_target_pairs={{0,1},{1,0},{2,3},{3,2},{4,5},{5,4},{6,7},{7,6},{8,9},{9,8},{10,11... | collective-permute-start | bytes 1769480 | tf_op jit(solution)/shard_map/ppermute | solution.py:485
  16.8 11.7 %collective-permute-start.2 = (f32[8,128,128]{2,1,0:T(8,128)S(1)}, f32[8,128,128]{2,1,0:T(8,128)S(1)}, u32[]{:S(2)}, u32[]{:S(2)}) collective-permute-start(f32[8,128,128]{2,1,0:T(8,128)S(1)} %get-tuple-element.88), channel_id=1, source_target_pairs={{0,2},{1,5},{2,0},{3,7},{4,6},{5,1},{6,4},{7,3},{8,10},{9,13},{10,... | collective-permute-start | bytes 1572872 | tf_op jit(solution)/shard_map/ppermute | solution.py:485
  19.8 8.7 %collective-permute-start.3 = (f32[8,72,128]{2,1,0:T(8,128)S(1)}, f32[8,72,128]{2,1,0:T(8,128)S(1)}, u32[]{:S(2)}, u32[]{:S(2)}) collective-permute-start(f32[8,72,128]{2,1,0:T(8,128)S(1)} %get-tuple-element.89), channel_id=1, source_target_pairs={{0,8},{1,9},{2,10},{3,11},{4,12},{5,13},{6,14},{7,15},{8,0},{9,1},... | collective-permute-start | bytes 884744 | tf_op jit(solution)/shard_map/ppermute | solution.py:485
  28.7 7.8 %collective-permute-start.4 = (f32[4,128,128]{2,1,0:T(8,128)S(1)}, f32[4,128,128]{2,1,0:T(8,128)S(1)}, u32[]{:S(2)}, u32[]{:S(2)}) collective-permute-start(f32[4,128,128]{2,1,0:T(8,128)S(1)} %get-tuple-element.95), channel_id=1, source_target_pairs={{0,4},{1,3},{2,6},{3,1},{4,0},{5,7},{6,2},{7,5},{8,12},{9,11},{10,... | collective-permute-start | bytes 786440 | tf_op jit(solution)/shard_map/ppermute | solution.py:485
  29.2 5.9 %collective-permute-start.5 = (f32[4,72,128]{2,1,0:T(8,128)S(1)}, f32[4,72,128]{2,1,0:T(8,128)S(1)}, u32[]{:S(2)}, u32[]{:S(2)}) collective-permute-start(f32[4,72,128]{2,1,0:T(8,128)S(1)} %get-tuple-element.96), channel_id=1, source_target_pairs={{0,2},{1,5},{2,0},{3,7},{4,6},{5,1},{6,4},{7,3},{8,10},{9,13},{10,... | collective-permute-start | bytes 442376 | tf_op jit(solution)/shard_map/ppermute | solution.py:485
  36.6 6.2 %collective-permute-start.6 = (f32[2,128,128]{2,1,0:T(8,128)S(1)}, f32[2,128,128]{2,1,0:T(8,128)S(1)}, u32[]{:S(2)}, u32[]{:S(2)}) collective-permute-start(f32[2,128,128]{2,1,0:T(8,128)S(1)} %slice_add_fusion.9), channel_id=1, source_target_pairs={{0,8},{1,9},{2,10},{3,11},{4,12},{5,13},{6,14},{7,15},{8,0},{9,1},... | collective-permute-start | bytes 393224 | tf_op jit(solution)/shard_map/ppermute | solution.py:485
  38.4 4.4 %collective-permute-start.7 = (f32[2,72,128]{2,1,0:T(8,128)S(1)}, f32[2,72,128]{2,1,0:T(8,128)S(1)}, u32[]{:S(2)}, u32[]{:S(2)}) collective-permute-start(f32[2,72,128]{2,1,0:T(8,128)S(1)} %slice_add_fusion.11), channel_id=1, source_target_pairs={{0,4},{1,3},{2,6},{3,1},{4,0},{5,7},{6,2},{7,5},{8,12},{9,11},{10,... | collective-permute-start | bytes 221192 | tf_op jit(solution)/shard_map/ppermute | solution.py:485
  42.8 10.8 %collective-permute-start.8 = (f32[2,200,128]{2,1,0:T(8,128)S(1)}, f32[2,200,128]{2,1,0:T(8,128)S(1)}, u32[]{:S(2)}, u32[]{:S(2)}) collective-permute-start(f32[2,200,128]{2,1,0:T(8,128)S(1)} %maximum_maximum_fusion), channel_id=1, source_target_pairs={{0,16},{1,17},{2,18},{3,19},{4,20},{5,21},{6,22},{7,23},{8,24},{9,... | collective-permute-start | bytes 614408 | tf_op jit(solution)/shard_map/ppermute | solution.py:485
  53.8 6.1 %collective-permute-start.9 = (f32[2,168,128]{2,1,0:T(8,128)S(1)}, f32[2,168,128]{2,1,0:T(8,128)S(1)}, u32[]{:S(2)}, u32[]{:S(2)}) collective-permute-start(f32[2,168,128]{2,1,0:T(8,128)S(1)} %get-tuple-element.120), channel_id=1, source_target_pairs={{0,8},{1,9},{2,10},{3,11},{4,12},{5,13},{6,14},{7,15},{8,0},{9,1},... | collective-permute-start | bytes 516104 | tf_op jit(solution)/shard_map/ppermute | solution.py:485
  60.0 7.3 %collective-permute-start.10 = (f32[4,168,128]{2,1,0:T(8,128)S(1)}, f32[4,168,128]{2,1,0:T(8,128)S(1)}, u32[]{:S(2)}, u32[]{:S(2)}) collective-permute-start(f32[4,168,128]{2,1,0:T(8,128)S(1)} %pad_maximum_fusion.1), channel_id=1, source_target_pairs={{0,4},{1,3},{2,6},{3,1},{4,0},{5,7},{6,2},{7,5},{8,12},{9,11},{10,... | collective-permute-start | bytes 1032200 | tf_op jit(solution)/shard_map/ppermute | solution.py:485
  67.3 11.0 %collective-permute-start.11 = (f32[8,168,128]{2,1,0:T(8,128)S(1)}, f32[8,168,128]{2,1,0:T(8,128)S(1)}, u32[]{:S(2)}, u32[]{:S(2)}) collective-permute-start(f32[8,168,128]{2,1,0:T(8,128)S(1)} %pad_maximum_fusion.refs_0_), channel_id=1, source_target_pairs={{0,2},{1,5},{2,0},{3,7},{4,6},{5,1},{6,4},{7,3},{8,10},{9,13},{10,... | collective-permute-start | bytes 2064392 | tf_op jit(solution)/shard_map/ppermute | solution.py:485
  78.3 3.1 %collective-permute-start.14 = (f32[8,168,128]{2,1,0:T(8,128)S(1)}, f32[8,168,128]{2,1,0:T(8,128)S(1)}, u32[]{:S(2)}, u32[]{:S(2)}) collective-permute-start(f32[8,168,128]{2,1,0:T(8,128)S(1)} %collective-permute-done.11.refs_1_), channel_id=1, source_target_pairs={{0,1},{1,0},{2,3},{3,2},{4,5},{5,4},{6,7},{7,6},{8,9},{9,8},{10,11... | collective-permute-start | bytes 2064392 | tf_op jit(solution)/shard_map/ppermute | solution.py:485
  78.3 3.1 %collective-permute-start.12 = (f32[4,168,128]{2,1,0:T(8,128)S(1)}, f32[4,168,128]{2,1,0:T(8,128)S(1)}, u32[]{:S(2)}, u32[]{:S(2)}) collective-permute-start(f32[4,168,128]{2,1,0:T(8,128)S(1)} %pad_maximum_fusion.1), channel_id=1, source_target_pairs={{0,1},{1,0},{2,3},{3,2},{4,5},{5,4},{6,7},{7,6},{8,9},{9,8},{10,11... | collective-permute-start | bytes 1032200 | tf_op jit(solution)/shard_map/ppermute | solution.py:485
  78.9 2.6 %collective-permute-start.13 = (f32[4,168,128]{2,1,0:T(8,128)S(1)}, f32[4,168,128]{2,1,0:T(8,128)S(1)}, u32[]{:S(2)}, u32[]{:S(2)}) collective-permute-start(f32[4,168,128]{2,1,0:T(8,128)S(1)} %slice.115), channel_id=1, source_target_pairs={{0,1},{1,0},{2,3},{3,2},{4,5},{5,4},{6,7},{7,6},{8,9},{9,8},{10,11... | collective-permute-start | bytes 1032200 | tf_op jit(solution)/shard_map/ppermute | solution.py:485
  78.9 2.5 %collective-permute-start.15 = (f32[8,128]{1,0:T(8,128)S(1)}, f32[8,128]{1,0:T(8,128)S(1)}, u32[]{:S(2)}, u32[]{:S(2)}) collective-permute-start(f32[8,128]{1,0:T(8,128)S(1)} %get-tuple-element.117.refs_4_.refs_5_), channel_id=1, source_target_pairs={{0,1},{1,0},{2,3},{3,2},{4,5},{5,4},{6,7},{7,6},{8,9},{9,8},{10,11... | collective-permute-start | bytes 12296 | tf_op jit(solution)/shard_map/ppermute | solution.py:485
